TPU v7x, 32 devices: a whole 2x2x4 slice. The times are simulated.
32 devices in a mesh: pair: 2 (over core), row: 16 (over z, y, x).
Axes of the slice: x: 2, y: 2, z: 4, core: 2. Of those that a mesh axis runs over, the one named last changes fastest.
Arguments:
- snapshot: float32 [4096, 1024], P('row', 'pair'), may hold values from -6 to 6
- weights: float32 [8, 128], replicated, may hold values from 0 to 1
- block_home: int32 [8], P('pair'), may hold values from 0 to 7, each once
- plan: int32 [2, 2, 4], P(None, 'pair'), may hold values from 0 to 3, each once within a row
Outputs:
- rotated: float32 [4096, 1024], P('row', 'pair')
- column_norms: float32 [1024], P('pair')
All inputs are finite; a program needn't handle non-finite values. Where the computation divides by a largest or mean magnitude, that divisor is 1e-20 or more.
Results may differ from a plain program's by a relative error of at most 0.0001.
Values sent between devices are 32-bit elements; how exact they have to be, the bound alone decides.
No kernel may reach another device: no remote copies, remote signals or barrier semaphores. Data moves between devices by JAX's collectives and lax.ppermute only.
A program may use at most 128 MiB of HBM per device.

v0:
```python
import jax
import jax.numpy as jnp
from jax import lax
from jax.sharding import PartitionSpec as P

epsilon = 1e-06
step_size = 4.0
newton_turns = 5
highest = lax.Precision.HIGHEST


def shifted(block, axis, distance):
    devices = range(lax.axis_size(axis))
    route = [((i - distance) % len(devices), i) for i in devices]
    return lax.ppermute(block, axis, route)


def rotation(gram_matrix, spread):
    diagonal_part = jnp.diagonal(gram_matrix, axis1=1, axis2=2)
    inverse = lax.rsqrt(diagonal_part + epsilon)
    corr = gram_matrix * inverse[:, :, None] * inverse[:, None, :]
    skew_part = step_size * corr * (spread[:, :, None] - spread[:, None, :])
    row_bound = 1.0 + jnp.max(jnp.sum(jnp.abs(skew_part), axis=2), axis=1)
    unit_matrix = jnp.eye(gram_matrix.shape[1], dtype=jnp.float32)
    current = unit_matrix[None] + skew_part / row_bound[:, None, None]
    for index in range(newton_turns):
        inner_gram = jnp.einsum("pcd,pce->pde", current, current, precision=highest)
        current = jnp.einsum(
            "pcd,pde->pce", current, 1.5 * unit_matrix[None] - 0.5 * inner_gram, precision=highest
        )
    return current


def full_gram(paired):
    local_gram = jnp.einsum("rpc,rpd->pcd", paired, paired, precision=highest)
    return lax.psum(local_gram, "row")


def assemble(carried, cross_gram):
    first_diag = carried[0::2]
    second = carried[1::2]
    upper_rows = jnp.concatenate([first_diag, cross_gram], axis=2)
    lower_rows = jnp.concatenate([jnp.swapaxes(cross_gram, 1, 2), second], axis=2)
    return jnp.concatenate([upper_rows, lower_rows], axis=1)


def body(snapshot, weights, block_home, plan):
    row_count = snapshot.shape[0]
    block_width = weights.shape[1]
    slot_count = block_home.shape[0]
    rounds = plan.shape[0]
    blocks_here = snapshot.reshape(row_count, slot_count, block_width)
    spread = jnp.take(weights, block_home, axis=0)
    carried = jnp.zeros((slot_count, block_width, block_width), jnp.float32)
    for round_index in range(rounds):
        ordering = plan[round_index, 0]
        blocks_here = jnp.take(blocks_here, ordering, axis=1)
        spread = jnp.take(spread, ordering, axis=0)
        paired = blocks_here.reshape(row_count, 2, 2 * block_width)
        if round_index == 0:
            gram_matrix = full_gram(paired)
        else:
            carried = jnp.take(carried, ordering, axis=0)
            local_cross = jnp.einsum(
                "rpc,rpd->pcd", blocks_here[:, 0::2], blocks_here[:, 1::2], precision=highest
            )
            cross_gram = lax.psum(local_cross, "row")
            gram_matrix = assemble(carried, cross_gram)
        turn_matrix = rotation(gram_matrix, spread.reshape(2, 2 * block_width))
        result = jnp.einsum("rpc,pcd->rpd", paired, turn_matrix, precision=highest)
        blocks_here = result.reshape(row_count, slot_count, block_width)
        gram_times = jnp.einsum("pcd,pde->pce", gram_matrix, turn_matrix, precision=highest)
        rotated_gram = jnp.einsum("pcd,pce->pde", turn_matrix, gram_times, precision=highest)
        carried = jnp.stack(
            [
                rotated_gram[:, :block_width, :block_width],
                rotated_gram[:, block_width:, block_width:],
            ],
            axis=1,
        ).reshape(slot_count, block_width, block_width)
        ahead_block, ahead_scale, ahead_own = shifted(
            (blocks_here[:, 0], spread[0], carried[0]), "pair", 1
        )
        behind_block, behind_scale, behind_own = shifted(
            (blocks_here[:, 3], spread[3], carried[3]), "pair", -1
        )
        carried = jnp.stack([ahead_own, carried[1], carried[2], behind_own], axis=0)
        blocks_here = jnp.stack(
            [ahead_block, blocks_here[:, 1], blocks_here[:, 2], behind_block], axis=1
        )
        spread = jnp.stack([ahead_scale, spread[1], spread[2], behind_scale], axis=0)
    final_matrix = blocks_here.reshape(row_count, slot_count * block_width)
    squares = jnp.diagonal(carried, axis1=1, axis2=2).reshape(slot_count * block_width)
    return (final_matrix, jnp.sqrt(squares))


def solution(mesh):
    in_specs = (P("row", "pair"), P(), P("pair"), P(None, "pair", None))
    out_specs = (P("row", "pair"), P("pair"))
    return jax.shard_map(body, mesh=mesh, in_specs=in_specs, out_specs=out_specs, check_vma=False)
```

profile of v0, /device:TPU:0, one launch (start us, length us, event | category | flops | bytes accessed | tf_op | source)
XLA Modules:
  0.0 318.9 jit_solution(17270181886986516772)
XLA Ops:
  8.6 0.7 compare_and_fusion.2
  11.1 1.2 copy.124
  13.5 1.5 fusion.21
  15.0 0.7 fusion.15
  16.5 110.4 %all-reduce.3.cloned.1.call-done = f32[2,256,256]{2,1,0:T(8,128)} async-done(((f32[2,256,256]{2,1,0:T(8,128)}), f32[2,256,256]{2,1,0:T(8,128)}) %all-reduce.3.cloned.1.call-update) | async-done | bytes 524304 | tf_op jit(solution)/shard_map/psum | solution.py:36
  126.9 17.3 %copy.128 = f32[2,256,256]{0,2,1:T(8,128)} copy(f32[2,256,256]{2,1,0:T(8,128)} %all-reduce.3.cloned.1.call-done) | data formatting | bytes 1048576 | tf_op jit(solution)/shard_map/psum | solution.py:36
  144.2 2.3 gather_fusion
  147.1 1.4 fusion.9
  148.5 0.8 fusion.16
  149.3 1.1 fusion.8
  151.1 1.1 fusion.7
  152.8 1.1 fusion.6
  154.6 1.1 fusion.5
  156.3 1.1 fusion.28
  158.1 1.3 fusion.27
  162.8 1.3 fusion.10
  164.4 104.3 %all-reduce.5.cloned.1.call-done = f32[2,128,128]{2,1,0:T(8,128)} async-done(((f32[2,128,128]{2,1,0:T(8,128)}), f32[2,128,128]{2,1,0:T(8,128)}) %all-reduce.5.cloned.1.call-update) | async-done | bytes 131088 | tf_op jit(solution)/shard_map/psum | solution.py:67
  268.7 1.1 copy.144
  269.8 0.9 maximum_maximum_fusion
  270.7 16.6 %copy.145 = f32[2,256,256]{0,2,1:T(8,128)} copy(f32[2,256,256]{2,1,0:T(8,128)S(1)} %maximum_maximum_fusion) | data formatting | bytes 1048576 | tf_op jit(solution)/shard_map/concatenate | solution.py:44
  287.3 2.3 gather_fusion.3
  290.2 1.4 fusion.4
  291.6 0.8 fusion.17
  292.4 1.1 fusion.3
  294.2 1.1 fusion.2
  295.9 1.1 fusion.1
  297.7 1.1 fusion
  299.5 1.1 fusion.33
  301.2 1.1 fusion.34
  303.9 4.6 %copy.159 = f32[4,128,128]{0,2,1:T(8,128)} copy(f32[4,128,128]{2,1,0:T(8,128)S(1)} %pad_maximum_fusion.5) | data formatting | bytes 524288 | tf_op jit(solution)/shard_map/stack | solution.py:87
  308.5 1.8 gather_fusion.4
  311.1 1.0 copy.179
  (106 shorter events, 18.6 us)
Async XLA Ops:
  7.2 2.1 copy-start
  7.2 119.7 %all-reduce.3.cloned.1.call-start = ((), (), s32[]{:S(2)}) async-start(), calls=%async_computation | async-start | bytes 1048576 | tf_op jit(solution)/shard_map/psum | solution.py:36
  10.5 5.2 %collective-permute-start.5 = (f32[128]{0:T(128)S(1)}, f32[128]{0:T(128)S(1)}, u32[]{:S(2)}, u32[]{:S(2)}) collective-permute-start(f32[128]{0:T(128)S(1)} %get-tuple-element.23), channel_id=1, source_target_pairs={{16,0},{0,16},{17,1},{1,17},{18,2},{2,18},{19,3},{3,19},{20,4},{4,... | collective-permute-start | bytes 1544 | tf_op jit(solution)/shard_map/ppermute | solution.py:15
  11.0 4.8 %collective-permute-start.4 = (f32[128]{0:T(128)S(1)}, f32[128]{0:T(128)S(1)}, u32[]{:S(2)}, u32[]{:S(2)}) collective-permute-start(f32[128]{0:T(128)S(1)} %get-tuple-element.22), channel_id=1, source_target_pairs={{16,0},{0,16},{17,1},{1,17},{18,2},{2,18},{19,3},{3,19},{20,4},{4,... | collective-permute-start | bytes 1544 | tf_op jit(solution)/shard_map/ppermute | solution.py:15
  14.9 253.7 %all-reduce.5.cloned.1.call-start = ((), (), s32[]{:S(2)}) async-start(), calls=%async_computation.1 | async-start | bytes 262144 | tf_op jit(solution)/shard_map/psum | solution.py:67
  126.9 19.8 %copy-start.2 = (f32[2,256,256]{2,1,0:T(8,128)S(1)}, f32[2,256,256]{2,1,0:T(8,128)}, u32[]{:S(2)}) copy-start(f32[2,256,256]{2,1,0:T(8,128)} %all-reduce.3.cloned.1.call-done) | copy-start | bytes 1572868
  159.5 1.6 collective-permute-start.1
  159.6 1.5 collective-permute-start
  160.2 1.6 collective-permute-start.3
  160.6 1.5 collective-permute-start.2
  268.7 21.0 %copy-start.3 = (f32[2,128,128]{2,1,0:T(8,128)S(1)}, f32[2,128,128]{2,1,0:T(8,128)}, u32[]{:S(2)}) copy-start(f32[2,128,128]{2,1,0:T(8,128)} %all-reduce.5.cloned.1.call-done) | copy-start | bytes 393220
  269.8 42.3 %copy-start.1 = (f32[8,128]{1,0:T(8,128)S(1)}, f32[8,128]{1,0:T(8,128)}, u32[]{:S(2)}) copy-start(f32[8,128]{1,0:T(8,128)} %param.9) | copy-start | bytes 12292
  302.4 1.3 collective-permute-start.9
  302.5 1.4 collective-permute-start.8
  303.0 8.0 %collective-permute-start.7 = (f32[256,128]{0,1:T(8,128)S(1)}, f32[256,128]{0,1:T(8,128)S(1)}, u32[]{:S(2)}, u32[]{:S(2)}) collective-permute-start(f32[256,128]{0,1:T(8,128)S(1)} %get-tuple-element.11), channel_id=1, source_target_pairs={{16,0},{0,16},{17,1},{1,17},{18,2},{2,18},{19,3},{3,19},{20,4},{4,... | collective-permute-start | bytes 393224 | tf_op jit(solution)/shard_map/ppermute | solution.py:15
  303.2 7.8 %collective-permute-start.6 = (f32[256,128]{0,1:T(8,128)S(1)}, f32[256,128]{0,1:T(8,128)S(1)}, u32[]{:S(2)}, u32[]{:S(2)}) collective-permute-start(f32[256,128]{0,1:T(8,128)S(1)} %get-tuple-element.10), channel_id=1, source_target_pairs={{16,0},{0,16},{17,1},{1,17},{18,2},{2,18},{19,3},{3,19},{20,4},{4,... | collective-permute-start | bytes 393224 | tf_op jit(solution)/shard_map/ppermute | solution.py:15
Sparse Core Ops, SparseCore 0:
  15.1 111.7 all-reduce.2
  164.3 104.3 all-reduce.4
where the time goes:
time: 320 us; the launch traced here: 319 us
  waiting for transfers between devices  215 us (67%)
  local copies, waits for them, and re-layouts  53.7 us (17%)
  matrix products  26.9 us (8%)
  between operations  14.6 us (5%)
  other arithmetic  5.34 us (2%)
    psum x1, waiting for transfers between devices, full_gram(): return lax.psum(local_gram, 'row')  110 us
    psum x1, waiting for transfers between devices, body(): cross_gram = lax.psum(local_cross, 'row')  104 us
    psum x1, local copies, waits for them, and re-layouts, full_gram(): return lax.psum(local_gram, 'row')  17.3 us
    concatenate x1, local copies, waits for them, and re-layouts, assemble(): return jnp.concatenate([upper_rows, lower_rows], axis=1)  16.6 us
    dot_general x10, matrix products, rotation(): inner_gram = jnp.einsum('pcd,pce->pde', current, current, precision=highest)  11.4 us
    dot_general x10, matrix products, rotation(): jnp.einsum('pcd,pde->pce', current, 1.5 * unit_matrix[None] - 0.5 * inner...  6.9 us
  transfers between devices with their start and end apart: 12, of which 5 were waited for; matrix products, arithmetic and copies ran while one was open for 4% of the time, Pallas kernels for 0%

commit v1 on v0

v1 whole, which is shorter than its diff:
```python
import jax
import jax.numpy as jnp
from jax import lax
from jax.experimental import pallas as pl
from jax.experimental.pallas import tpu as pltpu
from jax.sharding import PartitionSpec as P

epsilon = 1e-06
step_size = 4.0
newton_turns = 5
tile = 8
f32 = jnp.float32
bf16 = jnp.bfloat16

VMEM = pl.BlockSpec(memory_space=pltpu.VMEM)
SMEM = pl.BlockSpec(memory_space=pltpu.SMEM)


def split(x):
    high = x.astype(bf16)
    return high, (x - high.astype(f32)).astype(bf16)


def dot(a, b, da, db):
    return lax.dot_general(a, b, (((da,), (db,)), ((), ())), preferred_element_type=f32)


def dot3(a, b, da, db):
    return dot(a[0], b[0], da, db) + (dot(a[0], b[1], da, db) + dot(a[1], b[0], da, db))


def iotas(n):
    return (
        lax.broadcasted_iota(jnp.int32, (n, n), 0),
        lax.broadcasted_iota(jnp.int32, (n, n), 1),
    )


def column(row):
    n = row.shape[1]
    return jnp.transpose(jnp.broadcast_to(row, (n, n)))


def start_rotation(gram, row_weight):
    n = gram.shape[0]
    i, j = iotas(n)
    same = i == j
    held = jnp.where(same, gram, 0.0)
    inv_row = lax.rsqrt(jnp.sum(held, axis=0, keepdims=True) + epsilon)
    inv_col = lax.rsqrt(jnp.sum(held, axis=1, keepdims=True) + epsilon)
    corr = gram * inv_col * inv_row
    skew = step_size * corr * (column(row_weight) - row_weight)
    bound = 1.0 + jnp.max(jnp.sum(jnp.abs(skew), axis=0, keepdims=True), axis=1, keepdims=True)
    return jnp.where(same, 1.0, 0.0) + skew * (1.0 / bound)


def rotations(grams, row_weights):
    n = grams[0].shape[0]
    i, j = iotas(n)
    diag15 = jnp.where(i == j, 1.5, 0.0)
    current = [start_rotation(g, w) for g, w in zip(grams, row_weights)]
    for _ in range(newton_turns):
        parts = [split(x) for x in current]
        inner = [dot3(p, p, 1, 1) for p in parts]
        turns = [split(diag15 - 0.5 * y) for y in inner]
        current = [dot3(p, t, 1, 0) for p, t in zip(parts, turns)]
    return current


def sizes(n, rows):
    return max(tile, rows // n)


def pack_kernel(plan, snap, out, *, width):
    n, chunk = out.shape[0], out.shape[1] - tile
    i, j = iotas(width)
    held = []
    diags = []
    for p in range(2):
        ab = [
            snap[:, pl.ds(pl.multiple_of(plan[0, 0, 2 * p + h] * width, width), width)]
            for h in range(2)
        ]
        parts = split(jnp.concatenate(ab, axis=1))
        gram = dot3(parts, parts, 0, 0)
        upper = gram[:width, :width]
        lower = gram[width:, width:]
        held.append(gram[:width, width:])
        held.append(jnp.where(i <= j, upper, lower))
        diags.append(jnp.sum(jnp.where(i == j, lower, 0.0), axis=0, keepdims=True))
    extra = jnp.concatenate(diags + [jnp.zeros((tile - 2, width), f32)], axis=0)
    for c in range(n):
        start = c * chunk
        out[c, :chunk, :] = held[start // width][start % width : start % width + chunk]
        out[c, chunk:, :] = extra if c == 0 else jnp.zeros((tile, width), f32)


def sum_kernel(parts, out):
    n = parts.shape[0]
    values = [parts[c] for c in range(n)]
    while len(values) > 1:
        values = [a + b for a, b in zip(values[0::2], values[1::2])] + (
            [values[-1]] if len(values) % 2 else []
        )
    for c in range(n):
        out[c] = values[0]


def unpack(gathered, p, width):
    chunk = gathered.shape[1] - tile
    rows = []
    per = width // chunk
    for q in range(2):
        first = (2 * p + q) * per
        rows.append(jnp.concatenate([gathered[first + c, :chunk, :] for c in range(per)], axis=0))
    cross, both = rows
    i, j = iotas(width)
    flipped = jnp.transpose(both)
    diag_b = gathered[0, chunk + p : chunk + p + 1, :]
    upper = jnp.where(i <= j, both, flipped)
    lower = jnp.where(i > j, both, jnp.where(i == j, diag_b, flipped))
    return whole(upper, cross, lower)


def whole(upper, cross, lower):
    return jnp.concatenate(
        [
            jnp.concatenate([upper, cross], axis=1),
            jnp.concatenate([jnp.transpose(cross), lower], axis=1),
        ],
        axis=0,
    )


def first_kernel(plan, home, weights, snap, gathered, send, keep, *, width):
    rows = snap.shape[0]
    grams, spreads, blocks = [], [], []
    for p in range(2):
        order = [plan[0, 0, 2 * p + h] for h in range(2)]
        grams.append(unpack(gathered, p, width))
        spreads.append(
            jnp.concatenate([weights[pl.ds(home[s], 1), :] for s in order], axis=1)
        )
        blocks.append(
            jnp.concatenate(
                [snap[:, pl.ds(pl.multiple_of(s * width, width), width)] for s in order], axis=1
            )
        )
    turns = rotations(grams, spreads)
    places = [[(send, 0), (keep, 0)], [(keep, 1), (send, 1)]]
    for p in range(2):
        q = split(turns[p])
        result = dot3(split(blocks[p]), q, 1, 0)
        moved = split(dot3(split(grams[p]), q, 1, 0))
        for h in range(2):
            ref, at = places[p][h]
            cut = slice(h * width, (h + 1) * width)
            own = dot3([x[:, cut] for x in q], [x[:, cut] for x in moved], 0, 0)
            ref[at, :rows, :] = result[:, cut]
            ref[at, rows : rows + width, :] = own
            ref[at, rows + width :, :] = jnp.broadcast_to(spreads[p][:, cut], (tile, width))


def gather_slots(keep, received, held):
    held[0] = received[0]
    held[1] = keep[0]
    held[2] = keep[1]
    held[3] = received[1]


def cross_kernel(plan, keep, received, out, held, *, rows, width):
    gather_slots(keep, received, held)
    n, chunk = out.shape[0], out.shape[1]
    crosses = []
    for p in range(2):
        a, b = [split(held[plan[1, 0, 2 * p + h], :rows, :]) for h in range(2)]
        crosses.append(dot3(a, b, 0, 0))
    for c in range(n):
        start = c * chunk
        if start < 2 * width:
            out[c] = crosses[start // width][start % width : start % width + chunk]
        else:
            out[c] = jnp.zeros((chunk, width), f32)


def second_kernel(plan, keep, received, gathered, send, kept, held, *, rows, width):
    gather_slots(keep, received, held)
    chunk = gathered.shape[1]
    per = width // chunk
    grams, spreads, blocks = [], [], []
    for p in range(2):
        order = [plan[1, 0, 2 * p + h] for h in range(2)]
        cross = jnp.concatenate([gathered[p * per + c] for c in range(per)], axis=0)
        own = [held[s, rows : rows + width, :] for s in order]
        grams.append(whole(own[0], cross, own[1]))
        spreads.append(
            jnp.concatenate([held[s, rows + width : rows + width + 1, :] for s in order], axis=1)
        )
        blocks.append(jnp.concatenate([held[s, :rows, :] for s in order], axis=1))
    turns = rotations(grams, spreads)
    places = [[(send, 0), (kept, 0)], [(kept, 1), (send, 1)]]
    for p in range(2):
        q = split(turns[p])
        result = dot3(split(blocks[p]), q, 1, 0)
        moved = dot3(split(grams[p]), q, 1, 0)
        squares = jnp.sum(turns[p] * moved, axis=0, keepdims=True)
        norms = jnp.sqrt(squares)
        for h in range(2):
            ref, at = places[p][h]
            cut = slice(h * width, (h + 1) * width)
            ref[at, :rows, :] = result[:, cut]
            ref[at, rows:, :] = jnp.broadcast_to(norms[:, cut], (tile, width))


def last_kernel(kept, received, final, norms):
    rows = final.shape[0]
    width = kept.shape[2]
    order = [(received, 0), (kept, 0), (kept, 1), (received, 1)]
    for s, (ref, at) in enumerate(order):
        final[:, s * width : (s + 1) * width] = ref[at, :rows, :]
        norms[s : s + 1, :] = ref[at, rows : rows + 1, :]


def call(kernel, outs, specs, scratch=(), **static):
    def run(*refs):
        kernel(*refs, **static)

    run.__name__ = kernel.__name__
    return pl.pallas_call(
        run,
        out_shape=outs,
        in_specs=specs,
        out_specs=jax.tree.map(lambda _: VMEM, outs),
        scratch_shapes=scratch,
        name=kernel.__name__,
    )


def shape(*dims):
    return jax.ShapeDtypeStruct(dims, f32)


def exchange(send):
    count = lax.axis_size("pair")
    ahead = [((i - 1) % count, i) for i in range(count)]
    behind = [((i + 1) % count, i) for i in range(count)]
    if sorted(ahead) == sorted(behind):
        return lax.ppermute(send, "pair", ahead)
    return jnp.stack(
        [lax.ppermute(send[0], "pair", ahead), lax.ppermute(send[1], "pair", behind)]
    )


def total(parts):
    mine = lax.all_to_all(parts, "row", 0, 0, tiled=True)
    summed = call(sum_kernel, shape(*parts.shape), [VMEM])(mine)
    return lax.all_to_all(summed, "row", 0, 0, tiled=True)


def body(snapshot, weights, block_home, plan):
    rows = snapshot.shape[0]
    width = weights.shape[1]
    n = lax.axis_size("row")
    packed = call(
        pack_kernel, shape(n, sizes(n, 4 * width) + tile, width), [SMEM, VMEM], width=width
    )(plan, snapshot)
    gathered = total(packed)
    tall = rows + width + tile
    send, keep = call(
        first_kernel,
        [shape(2, tall, width), shape(2, tall, width)],
        [SMEM, SMEM, VMEM, VMEM, VMEM],
        width=width,
    )(plan, block_home, weights, snapshot, gathered)
    received = exchange(send)
    scratch = [pltpu.VMEM((4, tall, width), f32)]
    cross = call(
        cross_kernel,
        shape(n, sizes(n, 2 * width), width),
        [SMEM, VMEM, VMEM],
        scratch,
        rows=rows,
        width=width,
    )(plan, keep, received)
    gathered = total(cross)
    send, kept = call(
        second_kernel,
        [shape(2, rows + tile, width), shape(2, rows + tile, width)],
        [SMEM, VMEM, VMEM, VMEM],
        scratch,
        rows=rows,
        width=width,
    )(plan, keep, received, gathered)
    final, norms = call(
        last_kernel, [shape(rows, 4 * width), shape(4, width)], [VMEM, VMEM]
    )(kept, exchange(send))
    return final, norms.reshape(4 * width)


def solution(mesh):
    in_specs = (P("row", "pair"), P(), P("pair"), P(None, "pair", None))
    out_specs = (P("row", "pair"), P("pair"))
    return jax.shard_map(body, mesh=mesh, in_specs=in_specs, out_specs=out_specs, check_vma=False)
```

time: 320 us -> 87.3 us (0.27)
  waiting for transfers between devices: 215 us -> 3.7 us
  blocking collectives: 0 us -> 58.3 us
  local copies, waits for them, and re-layouts: 53.7 us -> 1.45 us
  matrix products: 26.9 us -> 0 us
  Pallas kernels: 0 us -> 22.6 us
  between operations: 14.6 us -> 0.64 us
  other arithmetic: 5.34 us -> 0 us
    psum x2 -> x0, waiting for transfers between devices: 215 us -> none  [the longest x1 110 us: full_gram(): return lax.psum(local_gram, 'row')]
    all_to_all x0 -> x4, blocking collectives: none -> 58.3 us  [the longest x2 31.9 us: total(): mine = lax.all_to_all(parts, 'row', 0, 0, tiled=True)]
    dot_general x28 -> x0, matrix products: 26.9 us -> none  [the longest x10 11.4 us: rotation(): inner_gram = jnp.einsum('pcd,pce->pde', current, current, precision=highest)]
    pallas_call x0 -> x7, Pallas kernels: none -> 22.6 us  [the longest x1 6.83 us: body(): call(first_kernel, [shape(2, tall, width), shape(2, tall, width)], [SMEM,...]
    psum x1 -> x0, local copies, waits for them, and re-layouts: 17.3 us -> none  [full_gram(): return lax.psum(local_gram, 'row')]
    concatenate x1 -> x0, local copies, waits for them, and re-layouts: 16.6 us -> none  [assemble(): return jnp.concatenate([upper_rows, lower_rows], axis=1)]
    gather x9 -> x0, local copies, waits for them, and re-layouts: 9.84 us -> none  [the longest x2 4.66 us: rotation(): diagonal_part = jnp.diagonal(gram_matrix, axis1=1, axis2=2)]
    another operation x5 -> x0, local copies, waits for them, and re-layouts: 4.72 us -> none  [the longest x1 4.64 us: body(): carried = jnp.stack([ahead_own, carried[1], carried[2], behind_own], axis=0)]
  transfers between devices with their start and end apart: 12 -> 2, of which waited for: 5 -> 2; matrix products, arithmetic and copies ran while one was open for 4% -> 0% of each run, Pallas kernels for 0% -> 0%
where the time goes in v1:
time: 87.3 us; the launch traced here: 86.7 us
  blocking collectives  58.3 us (67%)
  Pallas kernels  22.6 us (26%)
  waiting for transfers between devices  3.7 us (4%)
  local copies, waits for them, and re-layouts  1.45 us (2%)
    all_to_all x2, blocking collectives, total(): mine = lax.all_to_all(parts, 'row', 0, 0, tiled=True)  31.9 us
    all_to_all x2, blocking collectives, total(): return lax.all_to_all(summed, 'row', 0, 0, tiled=True)  26.3 us
    pallas_call x1, Pallas kernels, body(): call(first_kernel, [shape(2, tall, width), shape(2, tall, width)], [SMEM,...  6.83 us
    pallas_call x1, Pallas kernels, body(): call(second_kernel, [shape(2, rows + tile, width), shape(2, rows + tile,...  6.22 us
    ppermute x2, waiting for transfers between devices, exchange(): return lax.ppermute(send, 'pair', ahead)  3.7 us
    pallas_call x2, Pallas kernels, total(): summed = call(sum_kernel, shape(*parts.shape), [VMEM])(mine)  3.28 us
    pallas_call x1, Pallas kernels, body(): call(pack_kernel, shape(n, sizes(n, 4 * width) + tile, width), [SMEM, VME...  2.24 us
    pallas_call x1, Pallas kernels, body(): call(cross_kernel, shape(n, sizes(n, 2 * width), width), [SMEM, VMEM, VME...  2.13 us
  transfers between devices with their start and end apart: 2, of which 2 were waited for; matrix products, arithmetic and copies ran while one was open for 0% of the time, Pallas kernels for 0%

profile of v1, /device:TPU:0, one launch (start us, length us, event | category | flops | bytes accessed | tf_op | source)
XLA Modules:
  0.0 86.7 jit_solution(14586972134531180965)
XLA Ops:
  0.6 2.2 %pack_kernel.1 = f32[16,40,128]{2,1,0:T(8,128)} custom-call(s32[2,1,4]{2,1,0:T(1,128)} %refs_0_.7, f32[256,512]{1,0:T(8,128)} %refs_3_.1), custom_call_target="tpu_custom_call" | custom-call | tf_op jit(solution)/shard_map/pack_kernel/pallas_call | solution.py:264
  2.9 19.8 %all_to_all.20.refs_0_ = f32[16,40,128]{2,1,0:T(8,128)} all-to-all(f32[16,40,128]{2,1,0:T(8,128)} %pack_kernel.1), channel_id=1, replica_groups=mesh['pair'=2,'row'=16] {'row'}, dimensions={0} | all-to-all | bytes 655360 | tf_op jit(solution)/shard_map/all_to_all | solution.py:255
  22.6 1.7 %sum_kernel.2 = f32[16,40,128]{2,1,0:T(8,128)} custom-call(f32[16,40,128]{2,1,0:T(8,128)} %all_to_all.20.refs_0_), custom_call_target="tpu_custom_call" | custom-call | tf_op jit(solution)/shard_map/sum_kernel/pallas_call | solution.py:256
  24.3 14.4 %all_to_all.21.refs_4_ = f32[16,40,128]{2,1,0:T(8,128)} all-to-all(f32[16,40,128]{2,1,0:T(8,128)} %sum_kernel.2), channel_id=1, replica_groups=mesh['pair'=2,'row'=16] {'row'}, dimensions={0} | all-to-all | bytes 655360 | tf_op jit(solution)/shard_map/all_to_all | solution.py:257
  38.7 6.8 %first_kernel.1 = (f32[2,392,128]{2,1,0:T(8,128)}, f32[2,392,128]{2,1,0:T(8,128)}) custom-call(s32[2,1,4]{2,1,0:T(1,128)} %refs_0_.7, s32[4]{0:T(128)} %refs_1_.3, f32[8,128]{1,0:T(8,128)} %refs_2_.1, f32[256,512]{1,0:T(8,128)} %refs_3_.1, f32[16,40,128]{2,1,0:T(8,128)} %all_to_all.21.refs_4_), custom_call_target="tpu_custom_call" | custom-call | tf_op jit(solution)/shard_map/first_kernel/pallas_call | solution.py:269
  45.6 0.0 collective-permute-start
  45.6 1.9 %collective-permute-done.refs_2_ = f32[2,392,128]{2,1,0:T(8,128)S(1)} collective-permute-done((f32[2,392,128]{2,1,0:T(8,128)}, f32[2,392,128]{2,1,0:T(8,128)S(1)}, u32[]{:S(2)}, u32[]{:S(2)}) %collective-permute-start) | collective-permute-done | bytes 401440 | tf_op jit(solution)/shard_map/ppermute | solution.py:248
  47.5 0.0 copy-start
  47.5 0.7 copy-done
  48.2 2.1 %cross_kernel.1 = f32[16,16,128]{2,1,0:T(8,128)} custom-call(s32[2,1,4]{2,1,0:T(1,128)} %refs_0_.7, f32[2,392,128]{2,1,0:T(8,128)} %get-tuple-element.8.refs_1_, f32[2,392,128]{2,1,0:T(8,128)} %copy-done), custom_call_target="tpu_custom_call" | custom-call | tf_op jit(solution)/shard_map/cross_kernel/pallas_call | solution.py:277
  50.4 12.2 %all_to_all.22.refs_0_ = f32[16,16,128]{2,1,0:T(8,128)} all-to-all(f32[16,16,128]{2,1,0:T(8,128)} %cross_kernel.1), channel_id=1, replica_groups=mesh['pair'=2,'row'=16] {'row'}, dimensions={0} | all-to-all | bytes 262144 | tf_op jit(solution)/shard_map/all_to_all | solution.py:255
  62.6 1.6 %sum_kernel.3 = f32[16,16,128]{2,1,0:T(8,128)} custom-call(f32[16,16,128]{2,1,0:T(8,128)} %all_to_all.22.refs_0_), custom_call_target="tpu_custom_call" | custom-call | tf_op jit(solution)/shard_map/sum_kernel/pallas_call | solution.py:256
  64.1 12.0 %all_to_all.23.refs_3_ = f32[16,16,128]{2,1,0:T(8,128)} all-to-all(f32[16,16,128]{2,1,0:T(8,128)} %sum_kernel.3), channel_id=1, replica_groups=mesh['pair'=2,'row'=16] {'row'}, dimensions={0} | all-to-all | bytes 262144 | tf_op jit(solution)/shard_map/all_to_all | solution.py:257
  76.1 6.2 %second_kernel.1 = (f32[2,264,128]{2,1,0:T(8,128)}, f32[2,264,128]{2,1,0:T(8,128)}) custom-call(s32[2,1,4]{2,1,0:T(1,128)} %refs_0_.7, f32[2,392,128]{2,1,0:T(8,128)} %get-tuple-element.8.refs_1_, f32[2,392,128]{2,1,0:T(8,128)} %copy-done, f32[16,16,128]{2,1,0:T(8,128)} %all_to_all.23.refs_3_), custom_call_target="tpu_custom_call" | custom-call | tf_op jit(solution)/shard_map/second_kernel/pallas_call | solution.py:286
  82.3 0.0 collective-permute-start.1
  82.3 1.8 %collective-permute-done.1.refs_1_ = f32[2,264,128]{2,1,0:T(8,128)S(1)} collective-permute-done((f32[2,264,128]{2,1,0:T(8,128)}, f32[2,264,128]{2,1,0:T(8,128)S(1)}, u32[]{:S(2)}, u32[]{:S(2)}) %collective-permute-start.1) | collective-permute-done | bytes 270368 | tf_op jit(solution)/shard_map/ppermute | solution.py:248
  84.1 0.0 copy-start.1
  84.1 0.7 copy-done.1
  84.8 1.9 %last_kernel.1 = (f32[256,512]{1,0:T(8,128)}, f32[4,128]{1,0:T(4,128)}) custom-call(f32[2,264,128]{2,1,0:T(8,128)} %get-tuple-element.10.refs_0_, f32[2,264,128]{2,1,0:T(8,128)} %copy-done.1), custom_call_target="tpu_custom_call" | custom-call | tf_op jit(solution)/shard_map/last_kernel/pallas_call | solution.py:294
Async XLA Ops:
  45.6 1.9 %collective-permute-start = (f32[2,392,128]{2,1,0:T(8,128)}, f32[2,392,128]{2,1,0:T(8,128)S(1)}, u32[]{:S(2)}, u32[]{:S(2)}) collective-permute-start(f32[2,392,128]{2,1,0:T(8,128)} %get-tuple-element.9), channel_id=1, source_target_pairs={{16,0},{0,16},{17,1},{1,17},{18,2},{2,18},{19,3},{3,19},{20,4},{4,... | collective-permute-start | bytes 1204232 | tf_op jit(solution)/shard_map/ppermute | solution.py:248
  47.5 0.7 copy-start
  82.3 1.8 %collective-permute-start.1 = (f32[2,264,128]{2,1,0:T(8,128)}, f32[2,264,128]{2,1,0:T(8,128)S(1)}, u32[]{:S(2)}, u32[]{:S(2)}) collective-permute-start(f32[2,264,128]{2,1,0:T(8,128)} %get-tuple-element.11), channel_id=1, source_target_pairs={{16,0},{0,16},{17,1},{1,17},{18,2},{2,18},{19,3},{3,19},{20,4},{4,... | collective-permute-start | bytes 811016 | tf_op jit(solution)/shard_map/ppermute | solution.py:248
  84.1 0.7 copy-start.1

commit v2 on v1

--- a/solution.py
+++ b/solution.py
@@ -9,6 +9,7 @@
 step_size = 4.0
 newton_turns = 5
 tile = 8
+grant = 16 * 1024 * 1024
 f32 = jnp.float32
 bf16 = jnp.bfloat16
 
@@ -221,6 +222,14 @@
         norms[s : s + 1, :] = ref[at, rows : rows + 1, :]
 
 
+def near(x):
+    return pltpu.with_memory_space_constraint(x, pltpu.VMEM)
+
+
+def far(x):
+    return pltpu.with_memory_space_constraint(x, pltpu.HBM)
+
+
 def call(kernel, outs, specs, scratch=(), **static):
     def run(*refs):
         kernel(*refs, **static)
@@ -232,12 +241,13 @@
         in_specs=specs,
         out_specs=jax.tree.map(lambda _: VMEM, outs),
         scratch_shapes=scratch,
+        compiler_params=pltpu.CompilerParams(vmem_limit_bytes=grant),
         name=kernel.__name__,
     )
 
 
 def shape(*dims):
-    return jax.ShapeDtypeStruct(dims, f32)
+    return pltpu.VMEM(dims, f32)
 
 
 def exchange(send):
@@ -245,7 +255,7 @@
     ahead = [((i - 1) % count, i) for i in range(count)]
     behind = [((i + 1) % count, i) for i in range(count)]
     if sorted(ahead) == sorted(behind):
-        return lax.ppermute(send, "pair", ahead)
+        return near(lax.ppermute(send, "pair", ahead))
     return jnp.stack(
         [lax.ppermute(send[0], "pair", ahead), lax.ppermute(send[1], "pair", behind)]
     )
@@ -253,8 +263,8 @@
 
 def total(parts):
     mine = lax.all_to_all(parts, "row", 0, 0, tiled=True)
-    summed = call(sum_kernel, shape(*parts.shape), [VMEM])(mine)
-    return lax.all_to_all(summed, "row", 0, 0, tiled=True)
+    summed = call(sum_kernel, shape(*parts.shape), [VMEM])(near(mine))
+    return near(lax.all_to_all(summed, "row", 0, 0, tiled=True))
 
 
 def body(snapshot, weights, block_home, plan):
@@ -263,7 +273,7 @@
     n = lax.axis_size("row")
     packed = call(
         pack_kernel, shape(n, sizes(n, 4 * width) + tile, width), [SMEM, VMEM], width=width
-    )(plan, snapshot)
+    )(far(plan), far(snapshot))
     gathered = total(packed)
     tall = rows + width + tile
     send, keep = call(
@@ -292,7 +302,9 @@
         width=width,
     )(plan, keep, received, gathered)
     final, norms = call(
-        last_kernel, [shape(rows, 4 * width), shape(4, width)], [VMEM, VMEM]
+        last_kernel,
+        [jax.ShapeDtypeStruct((rows, 4 * width), f32), jax.ShapeDtypeStruct((4, width), f32)],
+        [VMEM, VMEM],
     )(kept, exchange(send))
     return final, norms.reshape(4 * width)
 

time: 87.3 us -> 73.4 us (0.84)
  Pallas kernels: 22.6 us -> 13.5 us
  blocking collectives: 58.3 us -> 55.4 us
  local copies, waits for them, and re-layouts: 1.45 us -> 0.02 us
    pallas_call x3, Pallas kernels: 5.18 us -> 0.91 us  [the longest x1 0.86 us: body(): call(last_kernel, [jax.ShapeDtypeStruct((rows, 4 * width), f32), jax.Shap...]
    pallas_call x1, Pallas kernels: 6.83 us -> 5.38 us  [body(): call(first_kernel, [shape(2, tall, width), shape(2, tall, width)], [SMEM,...]
    all_to_all x2, blocking collectives: 26.3 us -> 24.9 us  [total(): return near(lax.all_to_all(summed, 'row', 0, 0, tiled=True))]
    unnamed x4 -> x8, local copies, waits for them, and re-layouts: 1.45 us -> 0.02 us
    pallas_call x1, Pallas kernels: 6.22 us -> 4.82 us  [body(): call(second_kernel, [shape(2, rows + tile, width), shape(2, rows + tile,...]
    all_to_all x2, blocking collectives: 31.9 us -> 30.6 us  [total(): mine = lax.all_to_all(parts, 'row', 0, 0, tiled=True)]
    pallas_call x1, Pallas kernels: 2.13 us -> 0.91 us  [body(): call(cross_kernel, shape(n, sizes(n, 2 * width), width), [SMEM, VMEM, VME...]
where the time goes in v2:
time: 73.4 us; the launch traced here: 73.1 us
  blocking collectives  55.4 us (75%)
  Pallas kernels  13.5 us (18%)
  waiting for transfers between devices  3.25 us (4%)
    all_to_all x2, blocking collectives, total(): mine = lax.all_to_all(parts, 'row', 0, 0, tiled=True)  30.6 us
    all_to_all x2, blocking collectives, total(): return near(lax.all_to_all(summed, 'row', 0, 0, tiled=True))  24.9 us
    pallas_call x1, Pallas kernels, body(): call(first_kernel, [shape(2, tall, width), shape(2, tall, width)], [SMEM,...  5.38 us
    pallas_call x1, Pallas kernels, body(): call(second_kernel, [shape(2, rows + tile, width), shape(2, rows + tile,...  4.82 us
    ppermute x2, waiting for transfers between devices, exchange(): return near(lax.ppermute(send, 'pair', ahead))  3.25 us
    pallas_call x1, Pallas kernels, body(): call(pack_kernel, shape(n, sizes(n, 4 * width) + tile, width), [SMEM, VME...  1.51 us
  transfers between devices with their start and end apart: 2, of which 2 were waited for; matrix products, arithmetic and copies ran while one was open for 0% of the time, Pallas kernels for 0%

profile of v2, /device:TPU:0, one launch (start us, length us, event | category | flops | bytes accessed | tf_op | source)
XLA Modules:
  0.0 73.1 jit_solution(8155962998684663122)
XLA Ops:
  0.6 1.5 %pack_kernel.1 = f32[16,40,128]{2,1,0:T(8,128)S(1)} custom-call(s32[2,1,4]{2,1,0:T(1,128)} %refs_0_.7, f32[256,512]{1,0:T(8,128)} %refs_3_.1), custom_call_target="tpu_custom_call" | custom-call | tf_op jit(solution)/shard_map/pack_kernel/pallas_call | solution.py:274
  2.1 19.5 %all_to_all.20.refs_0_ = f32[16,40,128]{2,1,0:T(8,128)S(1)} all-to-all(f32[16,40,128]{2,1,0:T(8,128)S(1)} %pack_kernel.1), channel_id=1, replica_groups=mesh['pair'=2,'row'=16] {'row'}, dimensions={0} | all-to-all | bytes 655360 | tf_op jit(solution)/shard_map/all_to_all | solution.py:265
  21.6 0.0 copy-start
  21.6 0.0 copy-start.1
  21.6 0.0 copy-start.2
  21.7 0.0 copy-start.3
  21.7 14.2 %all_to_all.21.refs_4_ = f32[16,40,128]{2,1,0:T(8,128)S(1)} all-to-all(f32[16,40,128]{2,1,0:T(8,128)S(1)} %sum_kernel.2), channel_id=1, replica_groups=mesh['pair'=2,'row'=16] {'row'}, dimensions={0} | all-to-all | bytes 655360 | tf_op jit(solution)/shard_map/all_to_all | solution.py:267
  35.9 0.0 copy-done
  35.9 0.0 copy-done.1
  35.9 0.0 copy-done.2
  35.9 0.0 copy-done.3
  35.9 5.4 %first_kernel.1 = (f32[2,392,128]{2,1,0:T(8,128)S(1)}, f32[2,392,128]{2,1,0:T(8,128)S(1)}) custom-call(s32[2,1,4]{2,1,0:T(1,128)S(1)} %copy-done.1, s32[4]{0:T(128)S(1)} %copy-done.3, f32[8,128]{1,0:T(8,128)S(1)} %copy-done.2, f32[256,512]{1,0:T(8,128)S(1)} %copy-done, f32[16,40,128]{2,1,0:T(8,128)S(1)} %all_to_all.21.refs_4_), custom_call_target="tpu_custom_call" | custom-call | tf_op jit(solution)/shard_map/first_kernel/pallas_call | solution.py:279
  41.3 0.1 collective-permute-start
  41.4 1.7 %collective-permute-done.refs_2_ = f32[2,392,128]{2,1,0:T(8,128)S(1)} collective-permute-done((f32[2,392,128]{2,1,0:T(8,128)S(1)}, f32[2,392,128]{2,1,0:T(8,128)S(1)}, u32[]{:S(2)}, u32[]{:S(2)}) %collective-permute-start) | collective-permute-done | bytes 401440 | tf_op jit(solution)/shard_map/ppermute | solution.py:258
  43.1 0.9 %cross_kernel.1 = f32[16,16,128]{2,1,0:T(8,128)S(1)} custom-call(s32[2,1,4]{2,1,0:T(1,128)S(1)} %copy-done.1, f32[2,392,128]{2,1,0:T(8,128)S(1)} %get-tuple-element.8.refs_1_, f32[2,392,128]{2,1,0:T(8,128)S(1)} %collective-permute-done.refs_2_), custom_call_target="tpu_custom_call" | custom-call | tf_op jit(solution)/shard_map/cross_kernel/pallas_call | solution.py:287
  44.0 11.1 %all_to_all.22.refs_0_ = f32[16,16,128]{2,1,0:T(8,128)S(1)} all-to-all(f32[16,16,128]{2,1,0:T(8,128)S(1)} %cross_kernel.1), channel_id=1, replica_groups=mesh['pair'=2,'row'=16] {'row'}, dimensions={0} | all-to-all | bytes 262144 | tf_op jit(solution)/shard_map/all_to_all | solution.py:265
  55.1 10.7 %all_to_all.23.refs_3_ = f32[16,16,128]{2,1,0:T(8,128)S(1)} all-to-all(f32[16,16,128]{2,1,0:T(8,128)S(1)} %sum_kernel.3), channel_id=1, replica_groups=mesh['pair'=2,'row'=16] {'row'}, dimensions={0} | all-to-all | bytes 262144 | tf_op jit(solution)/shard_map/all_to_all | solution.py:267
  65.8 4.8 %second_kernel.1 = (f32[2,264,128]{2,1,0:T(8,128)S(1)}, f32[2,264,128]{2,1,0:T(8,128)S(1)}) custom-call(s32[2,1,4]{2,1,0:T(1,128)S(1)} %copy-done.1, f32[2,392,128]{2,1,0:T(8,128)S(1)} %get-tuple-element.8.refs_1_, f32[2,392,128]{2,1,0:T(8,128)S(1)} %collective-permute-done.refs_2_, f32[16,16,128]{2,1,0:T(8,128)S(1)} %all_to_all.23.refs_3_), custom_call_target="tpu_custom_call" | custom-call | tf_op jit(solution)/shard_map/second_kernel/pallas_call | solution.py:296
  70.6 0.1 collective-permute-start.1
  70.7 1.5 %collective-permute-done.1.refs_1_ = f32[2,264,128]{2,1,0:T(8,128)S(1)} collective-permute-done((f32[2,264,128]{2,1,0:T(8,128)S(1)}, f32[2,264,128]{2,1,0:T(8,128)S(1)}, u32[]{:S(2)}, u32[]{:S(2)}) %collective-permute-start.1) | collective-permute-done | bytes 270368 | tf_op jit(solution)/shard_map/ppermute | solution.py:258
  72.3 0.9 %last_kernel.1 = (f32[256,512]{1,0:T(8,128)}, f32[4,128]{1,0:T(4,128)}) custom-call(f32[2,264,128]{2,1,0:T(8,128)S(1)} %get-tuple-element.10.refs_0_, f32[2,264,128]{2,1,0:T(8,128)S(1)} %collective-permute-done.1.refs_1_), custom_call_target="tpu_custom_call" | custom-call | tf_op jit(solution)/shard_map/last_kernel/pallas_call | solution.py:304
  (2 shorter events, 0.0 us)
Async XLA Ops:
  21.6 14.3 %copy-start = (f32[256,512]{1,0:T(8,128)S(1)}, f32[256,512]{1,0:T(8,128)}, u32[]{:S(2)}) copy-start(f32[256,512]{1,0:T(8,128)} %refs_3_.1) | copy-start | bytes 1572868
  21.6 14.2 %copy-start.1 = (s32[2,1,4]{2,1,0:T(1,128)S(1)}, s32[2,1,4]{2,1,0:T(1,128)}, u32[]{:S(2)}) copy-start(s32[2,1,4]{2,1,0:T(1,128)} %refs_0_.7) | copy-start | bytes 100
  21.6 14.2 %copy-start.2 = (f32[8,128]{1,0:T(8,128)S(1)}, f32[8,128]{1,0:T(8,128)}, u32[]{:S(2)}) copy-start(f32[8,128]{1,0:T(8,128)} %refs_2_.1) | copy-start | bytes 12292
  21.7 14.2 %copy-start.3 = (s32[4]{0:T(128)S(1)}, s32[4]{0:T(128)}, u32[]{:S(2)}) copy-start(s32[4]{0:T(128)} %refs_1_.3) | copy-start | bytes 52
  41.3 1.8 %collective-permute-start = (f32[2,392,128]{2,1,0:T(8,128)S(1)}, f32[2,392,128]{2,1,0:T(8,128)S(1)}, u32[]{:S(2)}, u32[]{:S(2)}) collective-permute-start(f32[2,392,128]{2,1,0:T(8,128)S(1)} %get-tuple-element.9), channel_id=1, source_target_pairs={{16,0},{0,16},{17,1},{1,17},{18,2},{2,18},{19,3},{3,19},{20,4},{4,... | collective-permute-start | bytes 1204232 | tf_op jit(solution)/shard_map/ppermute | solution.py:258
  70.6 1.6 %collective-permute-start.1 = (f32[2,264,128]{2,1,0:T(8,128)S(1)}, f32[2,264,128]{2,1,0:T(8,128)S(1)}, u32[]{:S(2)}, u32[]{:S(2)}) collective-permute-start(f32[2,264,128]{2,1,0:T(8,128)S(1)} %get-tuple-element.11), channel_id=1, source_target_pairs={{16,0},{0,16},{17,1},{1,17},{18,2},{2,18},{19,3},{3,19},{20,4},{4,... | collective-permute-start | bytes 811016 | tf_op jit(solution)/shard_map/ppermute | solution.py:258

commit v3 on v2

--- a/solution.py
+++ b/solution.py
@@ -8,6 +8,7 @@
 epsilon = 1e-06
 step_size = 4.0
 newton_turns = 5
+light_turn = 3
 tile = 8
 grant = 16 * 1024 * 1024
 f32 = jnp.float32
@@ -15,6 +16,7 @@
 
 VMEM = pl.BlockSpec(memory_space=pltpu.VMEM)
 SMEM = pl.BlockSpec(memory_space=pltpu.SMEM)
+ANY = pl.BlockSpec(memory_space=pl.ANY)
 
 
 def split(x):
@@ -58,13 +60,19 @@
 def rotations(grams, row_weights):
     n = grams[0].shape[0]
     i, j = iotas(n)
-    diag15 = jnp.where(i == j, 1.5, 0.0)
+    same = i == j
+    diag15 = jnp.where(same, 1.5, 0.0)
+    diag05 = jnp.where(same, 0.5, 0.0)
     current = [start_rotation(g, w) for g, w in zip(grams, row_weights)]
-    for _ in range(newton_turns):
+    for turn in range(newton_turns):
         parts = [split(x) for x in current]
         inner = [dot3(p, p, 1, 1) for p in parts]
-        turns = [split(diag15 - 0.5 * y) for y in inner]
-        current = [dot3(p, t, 1, 0) for p, t in zip(parts, turns)]
+        if turn < light_turn:
+            turns = [split(diag15 - 0.5 * y) for y in inner]
+            current = [dot3(p, t, 1, 0) for p, t in zip(parts, turns)]
+        else:
+            fixes = [(diag05 - 0.5 * y).astype(bf16) for y in inner]
+            current = [x + dot(p[0], e, 1, 0) for x, p, e in zip(current, parts, fixes)]
     return current
 
 
@@ -133,48 +141,66 @@
     )
 
 
-def first_kernel(plan, home, weights, snap, gathered, send, keep, *, width):
+def pair_of(snap, plan, p, width):
+    return jnp.concatenate(
+        [
+            snap[:, pl.ds(pl.multiple_of(plan[0, 0, 2 * p + h] * width, width), width)]
+            for h in range(2)
+        ],
+        axis=1,
+    )
+
+
+def half(x, h):
+    width = x.shape[1] // 2
+    return x[:, h * width : (h + 1) * width]
+
+
+def first_kernel(plan, home, weights, snap, gathered, send, turned, spread, *, width):
     rows = snap.shape[0]
-    grams, spreads, blocks = [], [], []
-    for p in range(2):
-        order = [plan[0, 0, 2 * p + h] for h in range(2)]
+    grams, spreads = [], []
+    for p in range(2):
         grams.append(unpack(gathered, p, width))
         spreads.append(
-            jnp.concatenate([weights[pl.ds(home[s], 1), :] for s in order], axis=1)
-        )
-        blocks.append(
             jnp.concatenate(
-                [snap[:, pl.ds(pl.multiple_of(s * width, width), width)] for s in order], axis=1
+                [weights[pl.ds(home[plan[0, 0, 2 * p + h]], 1), :] for h in range(2)], axis=1
             )
         )
     turns = rotations(grams, spreads)
-    places = [[(send, 0), (keep, 0)], [(keep, 1), (send, 1)]]
-    for p in range(2):
-        q = split(turns[p])
-        result = dot3(split(blocks[p]), q, 1, 0)
-        moved = split(dot3(split(grams[p]), q, 1, 0))
+    for p in range(2):
+        q = half(turns[p], p)
+        send[p, :rows, :] = dot3(split(pair_of(snap, plan, p, width)), split(q), 1, 0)
+        send[p, rows:, :] = jnp.broadcast_to(half(spreads[p], p), (tile, width))
+        spread[p] = jnp.broadcast_to(half(spreads[p], 1 - p), (tile, width))
+        turned[p] = turns[p]
+
+
+def stay_kernel(plan, snap, turned, keep, *, width):
+    for p in range(2):
+        q = half(turned[p], 1 - p)
+        keep[p] = dot3(split(pair_of(snap, plan, p, width)), split(q), 1, 0)
+
+
+def carry_kernel(gathered, turned, send, keep, *, width):
+    for p in range(2):
+        q = split(turned[p])
+        moved = split(dot3(split(unpack(gathered, p, width)), q, 1, 0))
         for h in range(2):
-            ref, at = places[p][h]
-            cut = slice(h * width, (h + 1) * width)
-            own = dot3([x[:, cut] for x in q], [x[:, cut] for x in moved], 0, 0)
-            ref[at, :rows, :] = result[:, cut]
-            ref[at, rows : rows + width, :] = own
-            ref[at, rows + width :, :] = jnp.broadcast_to(spreads[p][:, cut], (tile, width))
-
-
-def gather_slots(keep, received, held):
-    held[0] = received[0]
-    held[1] = keep[0]
-    held[2] = keep[1]
-    held[3] = received[1]
-
-
-def cross_kernel(plan, keep, received, out, held, *, rows, width):
-    gather_slots(keep, received, held)
+            own = dot3([half(x, h) for x in q], [half(x, h) for x in moved], 0, 0)
+            (send if h == p else keep)[p] = own
+
+
+def slot_value(s, received, keep, cut):
+    values = [received[0, cut, :], keep[0, cut, :], keep[1, cut, :], received[1, cut, :]]
+    return jnp.where(s < 2, jnp.where(s == 0, *values[:2]), jnp.where(s == 2, *values[2:]))
+
+
+def cross_kernel(plan, keep, received, out, *, rows, width):
     n, chunk = out.shape[0], out.shape[1]
+    cut = slice(0, rows)
     crosses = []
     for p in range(2):
-        a, b = [split(held[plan[1, 0, 2 * p + h], :rows, :]) for h in range(2)]
+        a, b = [split(slot_value(plan[1, 0, 2 * p + h], received, keep, cut)) for h in range(2)]
         crosses.append(dot3(a, b, 0, 0))
     for c in range(n):
         start = c * chunk
@@ -184,42 +210,86 @@
             out[c] = jnp.zeros((chunk, width), f32)
 
 
-def second_kernel(plan, keep, received, gathered, send, kept, held, *, rows, width):
-    gather_slots(keep, received, held)
+def second_kernel(
+    plan, keep, received, spread, own_keep, own_received, gathered, send, turned, norms, *, rows
+):
+    width = keep.shape[2]
     chunk = gathered.shape[1]
     per = width // chunk
-    grams, spreads, blocks = [], [], []
+    every = slice(0, width)
+    grams, spreads = [], []
     for p in range(2):
         order = [plan[1, 0, 2 * p + h] for h in range(2)]
         cross = jnp.concatenate([gathered[p * per + c] for c in range(per)], axis=0)
-        own = [held[s, rows : rows + width, :] for s in order]
+        own = [slot_value(s, own_received, own_keep, every) for s in order]
         grams.append(whole(own[0], cross, own[1]))
+        wide = [received[0, rows:, :], spread[0], spread[1], received[1, rows:, :]]
         spreads.append(
-            jnp.concatenate([held[s, rows + width : rows + width + 1, :] for s in order], axis=1)
+            jnp.concatenate(
+                [
+                    jnp.where(
+                        s < 2, jnp.where(s == 0, *wide[:2]), jnp.where(s == 2, *wide[2:])
+                    )[:1]
+                    for s in order
+                ],
+                axis=1,
+            )
         )
-        blocks.append(jnp.concatenate([held[s, :rows, :] for s in order], axis=1))
     turns = rotations(grams, spreads)
-    places = [[(send, 0), (kept, 0)], [(kept, 1), (send, 1)]]
     for p in range(2):
         q = split(turns[p])
-        result = dot3(split(blocks[p]), q, 1, 0)
+        block = pair_after(plan, keep, received, p, rows)
+        send[p, :rows, :] = dot3(split(block), [half(x, p) for x in q], 1, 0)
         moved = dot3(split(grams[p]), q, 1, 0)
         squares = jnp.sum(turns[p] * moved, axis=0, keepdims=True)
-        norms = jnp.sqrt(squares)
-        for h in range(2):
-            ref, at = places[p][h]
-            cut = slice(h * width, (h + 1) * width)
-            ref[at, :rows, :] = result[:, cut]
-            ref[at, rows:, :] = jnp.broadcast_to(norms[:, cut], (tile, width))
-
-
-def last_kernel(kept, received, final, norms):
+        lengths = jnp.sqrt(squares)
+        send[p, rows:, :] = jnp.broadcast_to(half(lengths, p), (tile, width))
+        norms[p] = jnp.broadcast_to(half(lengths, 1 - p), (tile, width))
+        turned[p] = half(turns[p], 1 - p)
+
+
+def pair_after(plan, keep, received, p, rows):
+    return jnp.concatenate(
+        [
+            slot_value(plan[1, 0, 2 * p + h], received, keep, slice(0, rows))
+            for h in range(2)
+        ],
+        axis=1,
+    )
+
+
+def finish_kernel(plan, keep, received, turned, final, held, sems, *, rows):
+    width = keep.shape[2]
+    copies = []
+    for p in range(2):
+        block = pair_after(plan, keep, received, p, rows)
+        held[p] = dot3(split(block), split(turned[p]), 1, 0)
+        at = (1 + p) * width
+        copy = pltpu.make_async_copy(held.at[p], final.at[:, at : at + width], sems.at[p])
+        copy.start()
+        copies.append(copy)
+    for copy in copies:
+        copy.wait()
+
+
+def last_kernel(partly, norms_here, received, final, norms, sems):
+    del partly
     rows = final.shape[0]
-    width = kept.shape[2]
-    order = [(received, 0), (kept, 0), (kept, 1), (received, 1)]
-    for s, (ref, at) in enumerate(order):
-        final[:, s * width : (s + 1) * width] = ref[at, :rows, :]
-        norms[s : s + 1, :] = ref[at, rows : rows + 1, :]
+    width = received.shape[2]
+    copies = []
+    for p in range(2):
+        at = 3 * p * width
+        copy = pltpu.make_async_copy(
+            received.at[p, :rows, :], final.at[:, at : at + width], sems.at[p]
+        )
+        copy.start()
+        copies.append(copy)
+    norms[0:1, :] = received[0, rows : rows + 1, :]
+    norms[1:2, :] = norms_here[0, :1, :]
+    norms[2:3, :] = norms_here[1, :1, :]
+    norms[3:4, :] = received[1, rows : rows + 1, :]
+    for copy in copies:
+        copy.wait()
 
 
 def near(x):
@@ -230,17 +300,17 @@
     return pltpu.with_memory_space_constraint(x, pltpu.HBM)
 
 
-def call(kernel, outs, specs, scratch=(), **static):
+def call(kernel, outs, specs, scratch=(), out_specs=None, aliases=None, **static):
     def run(*refs):
         kernel(*refs, **static)
 
-    run.__name__ = kernel.__name__
     return pl.pallas_call(
         run,
         out_shape=outs,
         in_specs=specs,
-        out_specs=jax.tree.map(lambda _: VMEM, outs),
+        out_specs=jax.tree.map(lambda _: VMEM, outs) if out_specs is None else out_specs,
         scratch_shapes=scratch,
+        input_output_aliases=aliases or {},
         compiler_params=pltpu.CompilerParams(vmem_limit_bytes=grant),
         name=kernel.__name__,
     )
@@ -275,37 +345,55 @@
         pack_kernel, shape(n, sizes(n, 4 * width) + tile, width), [SMEM, VMEM], width=width
     )(far(plan), far(snapshot))
     gathered = total(packed)
-    tall = rows + width + tile
-    send, keep = call(
+    send, turned, spread = call(
         first_kernel,
-        [shape(2, tall, width), shape(2, tall, width)],
+        [shape(2, rows + tile, width), shape(2, 2 * width, 2 * width), shape(2, tile, width)],
         [SMEM, SMEM, VMEM, VMEM, VMEM],
         width=width,
     )(plan, block_home, weights, snapshot, gathered)
     received = exchange(send)
-    scratch = [pltpu.VMEM((4, tall, width), f32)]
+    keep = call(stay_kernel, shape(2, rows, width), [SMEM, VMEM, VMEM], width=width)(
+        plan, snapshot, turned
+    )
     cross = call(
         cross_kernel,
         shape(n, sizes(n, 2 * width), width),
         [SMEM, VMEM, VMEM],
-        scratch,
         rows=rows,
         width=width,
     )(plan, keep, received)
+    own_send, own_keep = call(
+        carry_kernel,
+        [shape(2, width, width), shape(2, width, width)],
+        [VMEM, VMEM],
+        width=width,
+    )(gathered, turned)
+    own_received = exchange(own_send)
     gathered = total(cross)
-    send, kept = call(
+    send, turned, norms = call(
         second_kernel,
-        [shape(2, rows + tile, width), shape(2, rows + tile, width)],
+        [shape(2, rows + tile, width), shape(2, 2 * width, width), shape(2, tile, width)],
+        [SMEM] + [VMEM] * 6,
+        rows=rows,
+    )(plan, keep, received, spread, own_keep, own_received, gathered)
+    arrived = exchange(send)
+    final_shape = jax.ShapeDtypeStruct((rows, 4 * width), f32)
+    partly = call(
+        finish_kernel,
+        final_shape,
         [SMEM, VMEM, VMEM, VMEM],
-        scratch,
+        [pltpu.VMEM((2, rows, width), f32), pltpu.SemaphoreType.DMA((2,))],
+        ANY,
         rows=rows,
-        width=width,
-    )(plan, keep, received, gathered)
+    )(plan, keep, received, turned)
     final, norms = call(
         last_kernel,
-        [jax.ShapeDtypeStruct((rows, 4 * width), f32), jax.ShapeDtypeStruct((4, width), f32)],
-        [VMEM, VMEM],
-    )(kept, exchange(send))
+        [final_shape, jax.ShapeDtypeStruct((4, width), f32)],
+        [ANY, VMEM, VMEM],
+        [pltpu.SemaphoreType.DMA((2,))],
+        [ANY, VMEM],
+        {0: 0},
+    )(partly, norms, arrived)
     return final, norms.reshape(4 * width)
 
 

time: 73.4 us -> 73.8 us (level)
  blocking collectives: 55.4 us -> 44.7 us
  waiting for transfers between devices: 3.25 us -> 7.05 us
  Pallas kernels: 13.5 us -> 17.1 us
  starting transfers between devices: 0.14 us -> 3.73 us
    all_to_all x2 -> x1, blocking collectives: 24.9 us -> 14.2 us  [total(): return near(lax.all_to_all(summed, 'row', 0, 0, tiled=True))]
    all_to_all x0 -> x1, waiting for transfers between devices: none -> 5.1 us  [total(): return near(lax.all_to_all(summed, 'row', 0, 0, tiled=True))]
    all_to_all x0 -> x1, starting transfers between devices: none -> 3.51 us  [total(): return near(lax.all_to_all(summed, 'row', 0, 0, tiled=True))]
    pallas_call x3 -> x6, Pallas kernels: 11.1 us -> 14.1 us  [the longest x1 4.59 us: body(): call(second_kernel, [shape(2, rows + tile, width), shape(2, 2 * width, wi...]
    ppermute x2 -> x3, waiting for transfers between devices: 3.25 us -> 1.95 us  [exchange(): return near(lax.ppermute(send, 'pair', ahead))]
  transfers between devices with their start and end apart: 2 -> 4, of which waited for: 2 -> 3; matrix products, arithmetic and copies ran while one was open for 0% -> 0% of each run, Pallas kernels for 0% -> 5%
where the time goes in v3:
time: 73.8 us; the launch traced here: 73.4 us
  blocking collectives  44.7 us (61%)
  Pallas kernels  17.1 us (23%)
  waiting for transfers between devices  7.05 us (10%)
  starting transfers between devices  3.73 us (5%)
  between operations  0.76 us (1%)
    all_to_all x2, blocking collectives, total(): mine = lax.all_to_all(parts, 'row', 0, 0, tiled=True)  30.6 us
    all_to_all x1, blocking collectives, total(): return near(lax.all_to_all(summed, 'row', 0, 0, tiled=True))  14.2 us
    all_to_all x1, waiting for transfers between devices, total(): return near(lax.all_to_all(summed, 'row', 0, 0, tiled=True))  5.1 us
    pallas_call x1, Pallas kernels, body(): call(second_kernel, [shape(2, rows + tile, width), shape(2, 2 * width, wi...  4.59 us
    pallas_call x1, Pallas kernels, body(): call(first_kernel, [shape(2, rows + tile, width), shape(2, 2 * width, 2 *...  4.41 us
    all_to_all x1, starting transfers between devices, total(): return near(lax.all_to_all(summed, 'row', 0, 0, tiled=True))  3.51 us
    ppermute x3, waiting for transfers between devices, exchange(): return near(lax.ppermute(send, 'pair', ahead))  1.95 us
    pallas_call x1, Pallas kernels, body(): call(finish_kernel, final_shape, [SMEM, VMEM, VMEM, VMEM], [pltpu.VMEM((2...  1.6 us
  transfers between devices with their start and end apart: 4, of which 3 were waited for; matrix products, arithmetic and copies ran while one was open for 0% of the time, Pallas kernels for 5%

profile of v3, /device:TPU:0, one launch (start us, length us, event | category | flops | bytes accessed | tf_op | source)
XLA Modules:
  0.0 73.4 jit_solution(1314016046135085001)
XLA Ops:
  0.6 1.5 %pack_kernel.1 = f32[16,40,128]{2,1,0:T(8,128)S(1)} custom-call(s32[2,1,4]{2,1,0:T(1,128)} %refs_0_.11, f32[256,512]{1,0:T(8,128)} %refs_1_.5), custom_call_target="tpu_custom_call" | custom-call | tf_op jit(solution)/shard_map/pack_kernel/pallas_call | solution.py:344
  2.1 19.5 %all_to_all.20.refs_0_ = f32[16,40,128]{2,1,0:T(8,128)S(1)} all-to-all(f32[16,40,128]{2,1,0:T(8,128)S(1)} %pack_kernel.1), channel_id=1, replica_groups=mesh['pair'=2,'row'=16] {'row'}, dimensions={0} | all-to-all | bytes 655360 | tf_op jit(solution)/shard_map/all_to_all | solution.py:335
  21.6 0.0 copy-start
  21.6 0.0 copy-start.1
  21.6 0.0 copy-start.2
  21.7 0.0 copy-start.3
  21.7 14.2 %all_to_all.21.refs_4_.refs_0_ = f32[16,40,128]{2,1,0:T(8,128)S(1)} all-to-all(f32[16,40,128]{2,1,0:T(8,128)S(1)} %sum_kernel.2), channel_id=1, replica_groups=mesh['pair'=2,'row'=16] {'row'}, dimensions={0} | all-to-all | bytes 655360 | tf_op jit(solution)/shard_map/all_to_all | solution.py:337
  35.9 0.0 copy-done
  35.9 0.0 copy-done.1
  35.9 0.0 copy-done.2
  35.9 0.0 copy-done.3
  35.9 4.4 %first_kernel.1 = (f32[2,264,128]{2,1,0:T(8,128)S(1)}, f32[2,256,256]{2,1,0:T(8,128)S(1)}, f32[2,8,128]{2,1,0:T(8,128)S(1)}) custom-call(s32[2,1,4]{2,1,0:T(1,128)S(1)} %copy-done.1, s32[4]{0:T(128)S(1)} %copy-done.3, f32[8,128]{1,0:T(8,128)S(1)} %copy-done.2, f32[256,512]{1,0:T(8,128)S(1)} %copy-done, f32[16,40,128]{2,1,0:T(8,128)S(1)} %all_to_all.21.refs_4_.refs_0_), custom_call_target="tpu_custom_call" | custom-call | tf_op jit(solution)/shard_map/first_kernel/pallas_call | solution.py:348
  40.3 0.1 collective-permute-start
  40.4 0.9 %stay_kernel.1.refs_1_ = f32[2,256,128]{2,1,0:T(8,128)S(1)} custom-call(s32[2,1,4]{2,1,0:T(1,128)S(1)} %copy-done.1, f32[256,512]{1,0:T(8,128)S(1)} %copy-done, f32[2,256,256]{2,1,0:T(8,128)S(1)} %get-tuple-element.12.refs_2_.refs_1_), custom_call_target="tpu_custom_call" | custom-call | tf_op jit(solution)/shard_map/stay_kernel/pallas_call | solution.py:355
  41.3 0.6 collective-permute-done.refs_2_
  41.9 0.9 %cross_kernel.1 = f32[16,16,128]{2,1,0:T(8,128)S(1)} custom-call(s32[2,1,4]{2,1,0:T(1,128)S(1)} %copy-done.1, f32[2,256,128]{2,1,0:T(8,128)S(1)} %stay_kernel.1.refs_1_, f32[2,264,128]{2,1,0:T(8,128)S(1)} %collective-permute-done.refs_2_), custom_call_target="tpu_custom_call" | custom-call | tf_op jit(solution)/shard_map/cross_kernel/pallas_call | solution.py:358
  42.8 11.1 %all_to_all.22.refs_0_ = f32[16,16,128]{2,1,0:T(8,128)S(1)} all-to-all(f32[16,16,128]{2,1,0:T(8,128)S(1)} %cross_kernel.1), channel_id=1, replica_groups=mesh['pair'=2,'row'=16] {'row'}, dimensions={0} | all-to-all | bytes 262144 | tf_op jit(solution)/shard_map/all_to_all | solution.py:335
  53.9 0.7 sum_kernel.3
  54.6 3.5 %all-to-all-start.3 = ((f32[16,16,128]{2,1,0:T(8,128)}), f32[16,16,128]{2,1,0:T(8,128)S(1)}, u32[]{:S(2)}, u32[]{:S(2)}) async-start(f32[16,16,128]{2,1,0:T(8,128)} %sum_kernel.3), calls=%async_computation.3 | async-start | bytes 262144 | tf_op jit(solution)/shard_map/all_to_all | solution.py:337
  58.1 1.2 %carry_kernel.1 = (f32[2,128,128]{2,1,0:T(8,128)S(1)}, f32[2,128,128]{2,1,0:T(8,128)S(1)}) custom-call(f32[16,40,128]{2,1,0:T(8,128)S(1)} %all_to_all.21.refs_4_.refs_0_, f32[2,256,256]{2,1,0:T(8,128)S(1)} %get-tuple-element.12.refs_2_.refs_1_), custom_call_target="tpu_custom_call" | custom-call | tf_op jit(solution)/shard_map/carry_kernel/pallas_call | solution.py:365
  59.3 0.1 collective-permute-start.1
  59.4 1.3 %collective-permute-done.1.refs_5_ = f32[2,128,128]{2,1,0:T(8,128)S(1)} collective-permute-done((f32[2,128,128]{2,1,0:T(8,128)S(1)}, f32[2,128,128]{2,1,0:T(8,128)S(1)}, u32[]{:S(2)}, u32[]{:S(2)}) %collective-permute-start.1) | collective-permute-done | bytes 131104 | tf_op jit(solution)/shard_map/ppermute | solution.py:328
  60.7 5.1 %all-to-all-done.3.refs_6_ = f32[16,16,128]{2,1,0:T(8,128)S(1)} async-done(((f32[16,16,128]{2,1,0:T(8,128)}), f32[16,16,128]{2,1,0:T(8,128)S(1)}, u32[]{:S(2)}, u32[]{:S(2)}) %all-to-all-start.3) | async-done | bytes 131104 | tf_op jit(solution)/shard_map/all_to_all | solution.py:337
  65.8 4.6 %second_kernel.1 = (f32[2,264,128]{2,1,0:T(8,128)S(1)}, f32[2,256,128]{2,1,0:T(8,128)S(1)}, f32[2,8,128]{2,1,0:T(8,128)S(1)}) custom-call(s32[2,1,4]{2,1,0:T(1,128)S(1)} %copy-done.1, f32[2,256,128]{2,1,0:T(8,128)S(1)} %stay_kernel.1.refs_1_, f32[2,264,128]{2,1,0:T(8,128)S(1)} %collective-permute-done.refs_2_, f32[2,8,128]{2,1,0:T(8,128)S(1)} %get-tuple-element.14.refs_3_, ...), custom_call_target="tpu_custom_call" | custom-call | tf_op jit(solution)/shard_map/second_kernel/pallas_call | solution.py:373
  70.4 0.1 collective-permute-start.2
  70.5 1.6 %finish_kernel.1.refs_0_ = f32[256,512]{1,0:T(8,128)} custom-call(s32[2,1,4]{2,1,0:T(1,128)S(1)} %copy-done.1, f32[2,256,128]{2,1,0:T(8,128)S(1)} %stay_kernel.1.refs_1_, f32[2,264,128]{2,1,0:T(8,128)S(1)} %collective-permute-done.refs_2_, f32[2,256,128]{2,1,0:T(8,128)S(1)} %get-tuple-element.17.refs_3_), custom_call_target="tpu_custom_call" | custom-call | tf_op jit(solution)/shard_map/finish_kernel/pallas_call | solution.py:381
  72.1 0.0 collective-permute-done.2.refs_2_
  72.1 1.3 %last_kernel.1 = (f32[256,512]{1,0:T(8,128)}, f32[4,128]{1,0:T(4,128)}) custom-call(f32[256,512]{1,0:T(8,128)} %finish_kernel.1.refs_0_, f32[2,8,128]{2,1,0:T(8,128)S(1)} %get-tuple-element.18.refs_1_, f32[2,264,128]{2,1,0:T(8,128)S(1)} %collective-permute-done.2.refs_2_), custom_call_target="tpu_custom_call", output_to_operand_aliasing={{0}: (0, {})} | custom-call | tf_op jit(solution)/shard_map/last_kernel/pallas_call | solution.py:389
  (1 shorter events, 0.0 us)
Async XLA Ops:
  21.6 14.3 %copy-start = (f32[256,512]{1,0:T(8,128)S(1)}, f32[256,512]{1,0:T(8,128)}, u32[]{:S(2)}) copy-start(f32[256,512]{1,0:T(8,128)} %refs_1_.5) | copy-start | bytes 1572868
  21.6 14.2 %copy-start.1 = (s32[2,1,4]{2,1,0:T(1,128)S(1)}, s32[2,1,4]{2,1,0:T(1,128)}, u32[]{:S(2)}) copy-start(s32[2,1,4]{2,1,0:T(1,128)} %refs_0_.11) | copy-start | bytes 100
  21.6 14.2 %copy-start.2 = (f32[8,128]{1,0:T(8,128)S(1)}, f32[8,128]{1,0:T(8,128)}, u32[]{:S(2)}) copy-start(f32[8,128]{1,0:T(8,128)} %refs_2_.1) | copy-start | bytes 12292
  21.7 14.2 %copy-start.3 = (s32[4]{0:T(128)S(1)}, s32[4]{0:T(128)}, u32[]{:S(2)}) copy-start(s32[4]{0:T(128)} %refs_1_.4) | copy-start | bytes 52
  40.3 1.6 %collective-permute-start = (f32[2,264,128]{2,1,0:T(8,128)S(1)}, f32[2,264,128]{2,1,0:T(8,128)S(1)}, u32[]{:S(2)}, u32[]{:S(2)}) collective-permute-start(f32[2,264,128]{2,1,0:T(8,128)S(1)} %get-tuple-element.13), channel_id=1, source_target_pairs={{16,0},{0,16},{17,1},{1,17},{18,2},{2,18},{19,3},{3,19},{20,4},{4,... | collective-permute-start | bytes 811016 | tf_op jit(solution)/shard_map/ppermute | solution.py:328
  54.6 11.3 %all-to-all-start.3 = ((f32[16,16,128]{2,1,0:T(8,128)}), f32[16,16,128]{2,1,0:T(8,128)S(1)}, u32[]{:S(2)}, u32[]{:S(2)}) async-start(f32[16,16,128]{2,1,0:T(8,128)} %sum_kernel.3), calls=%async_computation.3 | async-start | bytes 262144 | tf_op jit(solution)/shard_map/all_to_all | solution.py:337
  59.3 1.4 %collective-permute-start.1 = (f32[2,128,128]{2,1,0:T(8,128)S(1)}, f32[2,128,128]{2,1,0:T(8,128)S(1)}, u32[]{:S(2)}, u32[]{:S(2)}) collective-permute-start(f32[2,128,128]{2,1,0:T(8,128)S(1)} %get-tuple-element.16), channel_id=1, source_target_pairs={{16,0},{0,16},{17,1},{1,17},{18,2},{2,18},{19,3},{3,19},{20,4},{4,... | collective-permute-start | bytes 393224 | tf_op jit(solution)/shard_map/ppermute | solution.py:328
  70.4 1.7 %collective-permute-start.2 = (f32[2,264,128]{2,1,0:T(8,128)S(1)}, f32[2,264,128]{2,1,0:T(8,128)S(1)}, u32[]{:S(2)}, u32[]{:S(2)}) collective-permute-start(f32[2,264,128]{2,1,0:T(8,128)S(1)} %get-tuple-element.19), channel_id=1, source_target_pairs={{16,0},{0,16},{17,1},{1,17},{18,2},{2,18},{19,3},{3,19},{20,4},{4,... | collective-permute-start | bytes 811016 | tf_op jit(solution)/shard_map/ppermute | solution.py:328

commit v4 on v2

v4 whole, which is shorter than its diff:
```python
import jax
import jax.numpy as jnp
from jax import lax
from jax.experimental import pallas as pl
from jax.experimental.pallas import tpu as pltpu
from jax.sharding import PartitionSpec as P

epsilon = 1e-06
step_size = 4.0
newton_turns = 5
light_turn = 3
tile = 8
grant = 16 * 1024 * 1024
f32 = jnp.float32
bf16 = jnp.bfloat16

VMEM = pl.BlockSpec(memory_space=pltpu.VMEM)
SMEM = pl.BlockSpec(memory_space=pltpu.SMEM)


def split(x):
    high = x.astype(bf16)
    return high, (x - high.astype(f32)).astype(bf16)


def dot(a, b, da, db):
    return lax.dot_general(a, b, (((da,), (db,)), ((), ())), preferred_element_type=f32)


def dot3(a, b, da, db):
    return dot(a[0], b[0], da, db) + (dot(a[0], b[1], da, db) + dot(a[1], b[0], da, db))


def iotas(n):
    return (
        lax.broadcasted_iota(jnp.int32, (n, n), 0),
        lax.broadcasted_iota(jnp.int32, (n, n), 1),
    )


def column(row):
    n = row.shape[1]
    return jnp.transpose(jnp.broadcast_to(row, (n, n)))


def start_rotation(gram, row_weight):
    n = gram.shape[0]
    i, j = iotas(n)
    same = i == j
    held = jnp.where(same, gram, 0.0)
    inv_row = lax.rsqrt(jnp.sum(held, axis=0, keepdims=True) + epsilon)
    inv_col = lax.rsqrt(jnp.sum(held, axis=1, keepdims=True) + epsilon)
    corr = gram * inv_col * inv_row
    skew = step_size * corr * (column(row_weight) - row_weight)
    bound = 1.0 + jnp.max(jnp.sum(jnp.abs(skew), axis=0, keepdims=True), axis=1, keepdims=True)
    return jnp.where(same, 1.0, 0.0) + skew * (1.0 / bound)


def rotations(grams, row_weights):
    n = grams[0].shape[0]
    i, j = iotas(n)
    same = i == j
    diag15 = jnp.where(same, 1.5, 0.0)
    diag05 = jnp.where(same, 0.5, 0.0)
    current = [start_rotation(g, w) for g, w in zip(grams, row_weights)]
    for turn in range(newton_turns):
        parts = [split(x) for x in current]
        inner = [dot3(p, p, 1, 1) for p in parts]
        if turn < light_turn:
            turns = [split(diag15 - 0.5 * y) for y in inner]
            current = [dot3(p, t, 1, 0) for p, t in zip(parts, turns)]
        else:
            fixes = [(diag05 - 0.5 * y).astype(bf16) for y in inner]
            current = [x + dot(p[0], e, 1, 0) for x, p, e in zip(current, parts, fixes)]
    return current


def sizes(n, rows):
    return max(tile, rows // n)


def pack_kernel(plan, snap, out, *, width):
    n, chunk = out.shape[0], out.shape[1] - tile
    i, j = iotas(width)
    held = []
    diags = []
    for p in range(2):
        ab = [
            snap[:, pl.ds(pl.multiple_of(plan[0, 0, 2 * p + h] * width, width), width)]
            for h in range(2)
        ]
        parts = split(jnp.concatenate(ab, axis=1))
        gram = dot3(parts, parts, 0, 0)
        upper = gram[:width, :width]
        lower = gram[width:, width:]
        held.append(gram[:width, width:])
        held.append(jnp.where(i <= j, upper, lower))
        diags.append(jnp.sum(jnp.where(i == j, lower, 0.0), axis=0, keepdims=True))
    extra = jnp.concatenate(diags + [jnp.zeros((tile - 2, width), f32)], axis=0)
    for c in range(n):
        start = c * chunk
        out[c, :chunk, :] = held[start // width][start % width : start % width + chunk]
        out[c, chunk:, :] = extra if c == 0 else jnp.zeros((tile, width), f32)


def added(values):
    while len(values) > 1:
        values = [a + b for a, b in zip(values[0::2], values[1::2])] + (
            [values[-1]] if len(values) % 2 else []
        )
    return values[0]


def sum_kernel(parts, out):
    n = parts.shape[0]
    value = added([parts[c] for c in range(n)])
    for c in range(n):
        out[c] = value


def half_sum_kernel(parts, out):
    out[...] = added([parts[c] for c in range(parts.shape[0])])


def join_kernel(here, there, out):
    value = here[...] + there[...]
    for c in range(out.shape[0]):
        out[c] = value


def unpack(gathered, p, width):
    chunk = gathered.shape[1] - tile
    rows = []
    per = width // chunk
    for q in range(2):
        first = (2 * p + q) * per
        rows.append(jnp.concatenate([gathered[first + c, :chunk, :] for c in range(per)], axis=0))
    cross, both = rows
    i, j = iotas(width)
    flipped = jnp.transpose(both)
    diag_b = gathered[0, chunk + p : chunk + p + 1, :]
    upper = jnp.where(i <= j, both, flipped)
    lower = jnp.where(i > j, both, jnp.where(i == j, diag_b, flipped))
    return whole(upper, cross, lower)


def whole(upper, cross, lower):
    return jnp.concatenate(
        [
            jnp.concatenate([upper, cross], axis=1),
            jnp.concatenate([jnp.transpose(cross), lower], axis=1),
        ],
        axis=0,
    )


def pair_of(snap, plan, p, width):
    return jnp.concatenate(
        [
            snap[:, pl.ds(pl.multiple_of(plan[0, 0, 2 * p + h] * width, width), width)]
            for h in range(2)
        ],
        axis=1,
    )


def half(x, h):
    width = x.shape[1] // 2
    return x[:, h * width : (h + 1) * width]


def own_gram(gram, q):
    return dot3(q, split(dot3(split(gram), q, 1, 0)), 0, 0)


def first_kernel(plan, home, weights, snap, gathered, send, turned, spread, *, width):
    rows = snap.shape[0]
    grams, spreads = [], []
    for p in range(2):
        grams.append(unpack(gathered, p, width))
        spreads.append(
            jnp.concatenate(
                [weights[pl.ds(home[plan[0, 0, 2 * p + h]], 1), :] for h in range(2)], axis=1
            )
        )
    turns = rotations(grams, spreads)
    for p in range(2):
        q = split(half(turns[p], p))
        send[p, :rows, :] = dot3(split(pair_of(snap, plan, p, width)), q, 1, 0)
        send[p, rows : rows + width, :] = own_gram(grams[p], q)
        send[p, rows + width :, :] = jnp.broadcast_to(half(spreads[p], p), (tile, width))
        spread[p] = jnp.broadcast_to(half(spreads[p], 1 - p), (tile, width))
        turned[p] = half(turns[p], 1 - p)


def stay_kernel(plan, snap, gathered, turned, spread, keep, *, width):
    rows = snap.shape[0]
    for p in range(2):
        q = split(turned[p])
        keep[p, :rows, :] = dot3(split(pair_of(snap, plan, p, width)), q, 1, 0)
        keep[p, rows : rows + width, :] = own_gram(unpack(gathered, p, width), q)
        keep[p, rows + width :, :] = spread[p]


def slot_value(s, received, keep, cut):
    values = [received[0, cut, :], keep[0, cut, :], keep[1, cut, :], received[1, cut, :]]
    return jnp.where(s < 2, jnp.where(s == 0, *values[:2]), jnp.where(s == 2, *values[2:]))


def cross_kernel(plan, keep, received, out, high, low, *, rows, width):
    n, chunk = out.shape[0], out.shape[1]
    crosses = []
    for p in range(2):
        blocks = []
        for h in range(2):
            at = slice(h * width, (h + 1) * width)
            block = split(slot_value(plan[1, 0, 2 * p + h], received, keep, slice(0, rows)))
            high[p, :, at] = block[0]
            low[p, :, at] = block[1]
            blocks.append(block)
        crosses.append(dot3(*blocks, 0, 0))
    for c in range(n):
        start = c * chunk
        if start < 2 * width:
            out[c] = crosses[start // width][start % width : start % width + chunk]
        else:
            out[c] = jnp.zeros((chunk, width), f32)


def second_kernel(plan, keep, received, high, low, gathered, send, turned, norms, *, rows, width):
    chunk = gathered.shape[1]
    per = width // chunk
    grams, spreads = [], []
    for p in range(2):
        order = [plan[1, 0, 2 * p + h] for h in range(2)]
        cross = jnp.concatenate([gathered[p * per + c] for c in range(per)], axis=0)
        own = [slot_value(s, received, keep, slice(rows, rows + width)) for s in order]
        grams.append(whole(own[0], cross, own[1]))
        wide = [
            slot_value(s, received, keep, slice(rows + width, rows + width + 1)) for s in order
        ]
        spreads.append(jnp.concatenate(wide, axis=1))
    turns = rotations(grams, spreads)
    for p in range(2):
        q = split(turns[p])
        send[p, :rows, :] = dot3((high[p], low[p]), [half(x, p) for x in q], 1, 0)
        moved = dot3(split(grams[p]), q, 1, 0)
        squares = jnp.sum(turns[p] * moved, axis=0, keepdims=True)
        lengths = jnp.sqrt(squares)
        send[p, rows:, :] = jnp.broadcast_to(half(lengths, p), (tile, width))
        norms[p] = jnp.broadcast_to(half(lengths, 1 - p), (tile, width))
        turned[p] = half(turns[p], 1 - p)


def finish_kernel(high, low, turned, kept):
    for p in range(2):
        kept[p] = dot3((high[p], low[p]), split(turned[p]), 1, 0)


def last_kernel(kept, norms_here, received, final, norms):
    rows, width = kept.shape[1], kept.shape[2]
    order = [received[0, :rows, :], kept[0], kept[1], received[1, :rows, :]]
    lengths = [received[0, rows:, :], norms_here[0], norms_here[1], received[1, rows:, :]]
    for s in range(4):
        final[:, s * width : (s + 1) * width] = order[s]
        norms[s : s + 1, :] = lengths[s][:1]


def near(x):
    return pltpu.with_memory_space_constraint(x, pltpu.VMEM)


def far(x):
    return pltpu.with_memory_space_constraint(x, pltpu.HBM)


def call(kernel, outs, specs, **static):
    def run(*refs):
        kernel(*refs, **static)

    return pl.pallas_call(
        run,
        out_shape=outs,
        in_specs=specs,
        out_specs=jax.tree.map(lambda _: VMEM, outs),
        compiler_params=pltpu.CompilerParams(vmem_limit_bytes=grant),
        name=kernel.__name__,
    )


def shape(*dims):
    return pltpu.VMEM(dims, f32)


def exchange(send):
    count = lax.axis_size("pair")
    ahead = [((i - 1) % count, i) for i in range(count)]
    behind = [((i + 1) % count, i) for i in range(count)]
    if sorted(ahead) == sorted(behind):
        return near(lax.ppermute(send, "pair", ahead))
    return jnp.stack(
        [lax.ppermute(send[0], "pair", ahead), lax.ppermute(send[1], "pair", behind)]
    )


def swap(parts, groups=None):
    return near(
        lax.all_to_all(parts, "row", 0, 0, tiled=True, axis_index_groups=groups)
    )


def total(parts):
    mine = swap(parts)
    return swap(call(sum_kernel, shape(*parts.shape), [VMEM])(mine))


def halved_total(parts):
    n = lax.axis_size("row")
    reach = n // 2
    groups = [list(range(reach)), list(range(reach, n))]
    mine = swap(parts, groups)
    here = call(half_sum_kernel, shape(*parts.shape[1:]), [VMEM])(mine)
    there = near(lax.ppermute(here, "row", [(i, (i + reach) % n) for i in range(n)]))
    both = call(join_kernel, shape(*parts.shape), [VMEM, VMEM])(here, there)
    return swap(both, groups)


def body(snapshot, weights, block_home, plan):
    rows = snapshot.shape[0]
    width = weights.shape[1]
    n = lax.axis_size("row")
    reach = n // 2
    packed = call(
        pack_kernel, shape(reach, sizes(reach, 4 * width) + tile, width), [SMEM, VMEM], width=width
    )(far(plan), far(snapshot))
    gathered = halved_total(packed)
    tall = rows + width + tile
    send, turned, spread = call(
        first_kernel,
        [shape(2, tall, width), shape(2, 2 * width, width), shape(2, tile, width)],
        [SMEM, SMEM, VMEM, VMEM, VMEM],
        width=width,
    )(plan, block_home, weights, snapshot, gathered)
    received = exchange(send)
    keep = call(
        stay_kernel, shape(2, tall, width), [SMEM, VMEM, VMEM, VMEM, VMEM], width=width
    )(plan, snapshot, gathered, turned, spread)
    wide = pltpu.VMEM((2, rows, 2 * width), bf16)
    cross, high, low = call(
        cross_kernel,
        [shape(n, sizes(n, 2 * width), width), wide, wide],
        [SMEM, VMEM, VMEM],
        rows=rows,
        width=width,
    )(plan, keep, received)
    gathered = total(cross)
    send, turned, norms = call(
        second_kernel,
        [shape(2, rows + tile, width), shape(2, 2 * width, width), shape(2, tile, width)],
        [SMEM] + [VMEM] * 5,
        rows=rows,
        width=width,
    )(plan, keep, received, high, low, gathered)
    arrived = exchange(send)
    kept = call(finish_kernel, shape(2, rows, width), [VMEM, VMEM, VMEM])(high, low, turned)
    final, norms = call(
        last_kernel,
        [jax.ShapeDtypeStruct((rows, 4 * width), f32), jax.ShapeDtypeStruct((4, width), f32)],
        [VMEM, VMEM, VMEM],
    )(kept, norms, arrived)
    return final, norms.reshape(4 * width)


def solution(mesh):
    in_specs = (P("row", "pair"), P(), P("pair"), P(None, "pair", None))
    out_specs = (P("row", "pair"), P("pair"))
    return jax.shard_map(body, mesh=mesh, in_specs=in_specs, out_specs=out_specs, check_vma=False)
```

time: 73.4 us -> 67.7 us (0.922)
  blocking collectives: 55.4 us -> 45 us
  starting transfers between devices: 0.14 us -> 2.8 us
  Pallas kernels: 13.5 us -> 14.9 us
  waiting for transfers between devices: 3.25 us -> 4.02 us
    all_to_all x4, blocking collectives: 55.4 us -> 45 us  [swap(): lax.all_to_all(parts, 'row', 0, 0, tiled=True, axis_index_groups=groups)]
    ppermute x0 -> x1, waiting for transfers between devices: none -> 2.66 us  [halved_total(): lax.ppermute(here, 'row', [(i, (i + reach) % n) for i in range(n)])]
    ppermute x0 -> x1, starting transfers between devices: none -> 2.65 us  [halved_total(): lax.ppermute(here, 'row', [(i, (i + reach) % n) for i in range(n)])]
    ppermute x2, waiting for transfers between devices: 3.25 us -> 1.35 us  [exchange(): return near(lax.ppermute(send, 'pair', ahead))]
    pallas_call x6 -> x9, Pallas kernels: 12.7 us -> 14 us  [the longest x1 5.05 us: body(): call(first_kernel, [shape(2, tall, width), shape(2, 2 * width, width), sh...]
  transfers between devices with their start and end apart: 2 -> 3, of which waited for: 2 -> 3; matrix products, arithmetic and copies ran while one was open for 0% -> 0% of each run, Pallas kernels for 0% -> 3%
where the time goes in v4:
time: 67.7 us; the launch traced here: 67.4 us
  blocking collectives  45 us (66%)
  Pallas kernels  14.9 us (22%)
  waiting for transfers between devices  4.02 us (6%)
  starting transfers between devices  2.8 us (4%)
  between operations  0.74 us (1%)
    all_to_all x4, blocking collectives, swap(): lax.all_to_all(parts, 'row', 0, 0, tiled=True, axis_index_groups=groups)  45 us
    pallas_call x1, Pallas kernels, body(): call(first_kernel, [shape(2, tall, width), shape(2, 2 * width, width), sh...  5.05 us
    pallas_call x1, Pallas kernels, body(): call(second_kernel, [shape(2, rows + tile, width), shape(2, 2 * width, wi...  4.58 us
    ppermute x1, waiting for transfers between devices, halved_total(): lax.ppermute(here, 'row', [(i, (i + reach) % n) for i in range(n)])  2.66 us
    ppermute x1, starting transfers between devices, halved_total(): lax.ppermute(here, 'row', [(i, (i + reach) % n) for i in range(n)])  2.65 us
    pallas_call x1, Pallas kernels, body(): call(stay_kernel, shape(2, tall, width), [SMEM, VMEM, VMEM, VMEM, VMEM],...  1.53 us
    pallas_call x1, Pallas kernels, body(): call(pack_kernel, shape(reach, sizes(reach, 4 * width) + tile, width), [S...  1.51 us
  transfers between devices with their start and end apart: 3, of which 3 were waited for; matrix products, arithmetic and copies ran while one was open for 0% of the time, Pallas kernels for 3%

profile of v4, /device:TPU:0, one launch (start us, length us, event | category | flops | bytes accessed | tf_op | source)
XLA Modules:
  0.0 67.4 jit_solution(4519314923226543483)
XLA Ops:
  0.6 1.5 %pack_kernel.1 = f32[8,72,128]{2,1,0:T(8,128)S(1)} custom-call(s32[2,1,4]{2,1,0:T(1,128)} %refs_0_.9, f32[256,512]{1,0:T(8,128)} %refs_1_.5), custom_call_target="tpu_custom_call" | custom-call | tf_op jit(solution)/shard_map/pack_kernel/pallas_call | solution.py:333
  2.1 13.3 %all_to_all.20.refs_0_ = f32[8,72,128]{2,1,0:T(8,128)S(1)} all-to-all(f32[8,72,128]{2,1,0:T(8,128)S(1)} %pack_kernel.1), channel_id=1, replica_groups={{0,1,2,3,4,5,6,7},{8,9,10,11,12,13,14,15},{16,17,18,19,20,21,22,23},{24..., dimensions={0} | all-to-all | bytes 589824 | tf_op jit(solution)/shard_map/all_to_all | solution.py:308
  15.4 0.0 copy-start
  15.4 2.7 %collective-permute-start = (f32[72,128]{1,0:T(8,128)S(1)}, f32[72,128]{1,0:T(8,128)S(1)}, u32[]{:S(2)}, u32[]{:S(2)}) collective-permute-start(f32[72,128]{1,0:T(8,128)S(1)} %half_sum_kernel.1.refs_0_), channel_id=1, source_target_pairs={{0,8},{1,9},{2,10},{3,11},{4,12},{5,13},{6,14},{7,15},{8,0},{9,1},... | collective-permute-start | bytes 110600 | tf_op jit(solution)/shard_map/ppermute | solution.py:323
  18.1 2.7 %collective-permute-done.refs_1_ = f32[72,128]{1,0:T(8,128)S(1)} collective-permute-done((f32[72,128]{1,0:T(8,128)S(1)}, f32[72,128]{1,0:T(8,128)S(1)}, u32[]{:S(2)}, u32[]{:S(2)}) %collective-permute-start) | collective-permute-done | bytes 36896 | tf_op jit(solution)/shard_map/ppermute | solution.py:323
  20.8 0.0 copy-start.1
  20.8 0.0 copy-start.2
  20.8 0.0 copy-start.3
  20.8 9.6 %all_to_all.21.refs_4_.refs_2_ = f32[8,72,128]{2,1,0:T(8,128)S(1)} all-to-all(f32[8,72,128]{2,1,0:T(8,128)S(1)} %join_kernel.1), channel_id=1, replica_groups={{0,1,2,3,4,5,6,7},{8,9,10,11,12,13,14,15},{16,17,18,19,20,21,22,23},{24..., dimensions={0} | all-to-all | bytes 589824 | tf_op jit(solution)/shard_map/all_to_all | solution.py:308
  30.4 0.0 copy-done
  30.4 0.0 copy-done.1
  30.4 0.0 copy-done.2
  30.5 0.0 copy-done.3
  30.5 5.0 %first_kernel.1 = (f32[2,392,128]{2,1,0:T(8,128)S(1)}, f32[2,256,128]{2,1,0:T(8,128)S(1)}, f32[2,8,128]{2,1,0:T(8,128)S(1)}) custom-call(s32[2,1,4]{2,1,0:T(1,128)S(1)} %copy-done.1, s32[4]{0:T(128)S(1)} %copy-done.3, f32[8,128]{1,0:T(8,128)S(1)} %copy-done.2, f32[256,512]{1,0:T(8,128)S(1)} %copy-done, f32[8,72,128]{2,1,0:T(8,128)S(1)} %all_to_all.21.refs_4_.refs_2_), custom_call_target="tpu_custom_call" | custom-call | tf_op jit(solution)/shard_map/first_kernel/pallas_call | solution.py:338
  35.5 0.1 collective-permute-start.1
  35.6 1.5 %stay_kernel.1.refs_1_ = f32[2,392,128]{2,1,0:T(8,128)S(1)} custom-call(s32[2,1,4]{2,1,0:T(1,128)S(1)} %copy-done.1, f32[256,512]{1,0:T(8,128)S(1)} %copy-done, f32[8,72,128]{2,1,0:T(8,128)S(1)} %all_to_all.21.refs_4_.refs_2_, f32[2,256,128]{2,1,0:T(8,128)S(1)} %get-tuple-element.13.refs_3_, f32[2,8,128]{2,1,0:T(8,128)S(1)} %get-tuple-element.14.refs_4_), custom_call_target="tpu_custom_call" | custom-call | tf_op jit(solution)/shard_map/stay_kernel/pallas_call | solution.py:345
  37.1 0.2 collective-permute-done.1.refs_2_
  37.3 0.9 %cross_kernel.1 = (f32[16,16,128]{2,1,0:T(8,128)S(1)}, bf16[2,256,256]{2,1,0:T(8,128)(2,1)S(1)}, bf16[2,256,256]{2,1,0:T(8,128)(2,1)S(1)}) custom-call(s32[2,1,4]{2,1,0:T(1,128)S(1)} %copy-done.1, f32[2,392,128]{2,1,0:T(8,128)S(1)} %stay_kernel.1.refs_1_, f32[2,392,128]{2,1,0:T(8,128)S(1)} %collective-permute-done.1.refs_2_), custom_call_target="tpu_custom_call" | custom-call | tf_op jit(solution)/shard_map/cross_kernel/pallas_call | solution.py:349
  38.2 11.3 %all_to_all.22.refs_0_ = f32[16,16,128]{2,1,0:T(8,128)S(1)} all-to-all(f32[16,16,128]{2,1,0:T(8,128)S(1)} %get-tuple-element.18), channel_id=1, replica_groups=mesh['pair'=2,'row'=16] {'row'}, dimensions={0} | all-to-all | bytes 262144 | tf_op jit(solution)/shard_map/all_to_all | solution.py:308
  49.6 10.8 %all_to_all.23.refs_5_ = f32[16,16,128]{2,1,0:T(8,128)S(1)} all-to-all(f32[16,16,128]{2,1,0:T(8,128)S(1)} %sum_kernel.1), channel_id=1, replica_groups=mesh['pair'=2,'row'=16] {'row'}, dimensions={0} | all-to-all | bytes 262144 | tf_op jit(solution)/shard_map/all_to_all | solution.py:308
  60.4 4.6 %second_kernel.1 = (f32[2,264,128]{2,1,0:T(8,128)S(1)}, f32[2,256,128]{2,1,0:T(8,128)S(1)}, f32[2,8,128]{2,1,0:T(8,128)S(1)}) custom-call(s32[2,1,4]{2,1,0:T(1,128)S(1)} %copy-done.1, f32[2,392,128]{2,1,0:T(8,128)S(1)} %stay_kernel.1.refs_1_, f32[2,392,128]{2,1,0:T(8,128)S(1)} %collective-permute-done.1.refs_2_, ...), custom_call_target="tpu_custom_call" | custom-call | tf_op jit(solution)/shard_map/second_kernel/pallas_call | solution.py:357
  64.9 0.1 collective-permute-start.2
  65.0 0.4 finish_kernel.1.refs_0_
  65.4 1.2 %collective-permute-done.2.refs_2_ = f32[2,264,128]{2,1,0:T(8,128)S(1)} collective-permute-done((f32[2,264,128]{2,1,0:T(8,128)S(1)}, f32[2,264,128]{2,1,0:T(8,128)S(1)}, u32[]{:S(2)}, u32[]{:S(2)}) %collective-permute-start.2) | collective-permute-done | bytes 270368 | tf_op jit(solution)/shard_map/ppermute | solution.py:300
  66.6 0.9 %last_kernel.1 = (f32[256,512]{1,0:T(8,128)}, f32[4,128]{1,0:T(4,128)}) custom-call(f32[2,256,128]{2,1,0:T(8,128)S(1)} %finish_kernel.1.refs_0_, f32[2,8,128]{2,1,0:T(8,128)S(1)} %get-tuple-element.20.refs_1_, f32[2,264,128]{2,1,0:T(8,128)S(1)} %collective-permute-done.2.refs_2_), custom_call_target="tpu_custom_call" | custom-call | tf_op jit(solution)/shard_map/last_kernel/pallas_call | solution.py:366
  (3 shorter events, 0.1 us)
Async XLA Ops:
  15.4 15.0 %copy-start = (f32[256,512]{1,0:T(8,128)S(1)}, f32[256,512]{1,0:T(8,128)}, u32[]{:S(2)}) copy-start(f32[256,512]{1,0:T(8,128)} %refs_1_.5) | copy-start | bytes 1572868
  15.4 5.3 %collective-permute-start = (f32[72,128]{1,0:T(8,128)S(1)}, f32[72,128]{1,0:T(8,128)S(1)}, u32[]{:S(2)}, u32[]{:S(2)}) collective-permute-start(f32[72,128]{1,0:T(8,128)S(1)} %half_sum_kernel.1.refs_0_), channel_id=1, source_target_pairs={{0,8},{1,9},{2,10},{3,11},{4,12},{5,13},{6,14},{7,15},{8,0},{9,1},... | collective-permute-start | bytes 110600 | tf_op jit(solution)/shard_map/ppermute | solution.py:323
  20.8 9.7 %copy-start.1 = (s32[2,1,4]{2,1,0:T(1,128)S(1)}, s32[2,1,4]{2,1,0:T(1,128)}, u32[]{:S(2)}) copy-start(s32[2,1,4]{2,1,0:T(1,128)} %refs_0_.9) | copy-start | bytes 100
  20.8 9.6 %copy-start.2 = (f32[8,128]{1,0:T(8,128)S(1)}, f32[8,128]{1,0:T(8,128)}, u32[]{:S(2)}) copy-start(f32[8,128]{1,0:T(8,128)} %refs_2_.1) | copy-start | bytes 12292
  20.8 9.6 %copy-start.3 = (s32[4]{0:T(128)S(1)}, s32[4]{0:T(128)}, u32[]{:S(2)}) copy-start(s32[4]{0:T(128)} %refs_1_.4) | copy-start | bytes 52
  35.5 1.8 %collective-permute-start.1 = (f32[2,392,128]{2,1,0:T(8,128)S(1)}, f32[2,392,128]{2,1,0:T(8,128)S(1)}, u32[]{:S(2)}, u32[]{:S(2)}) collective-permute-start(f32[2,392,128]{2,1,0:T(8,128)S(1)} %get-tuple-element.15), channel_id=1, source_target_pairs={{16,0},{0,16},{17,1},{1,17},{18,2},{2,18},{19,3},{3,19},{20,4},{4,... | collective-permute-start | bytes 1204232 | tf_op jit(solution)/shard_map/ppermute | solution.py:300
  64.9 1.6 %collective-permute-start.2 = (f32[2,264,128]{2,1,0:T(8,128)S(1)}, f32[2,264,128]{2,1,0:T(8,128)S(1)}, u32[]{:S(2)}, u32[]{:S(2)}) collective-permute-start(f32[2,264,128]{2,1,0:T(8,128)S(1)} %get-tuple-element.21), channel_id=1, source_target_pairs={{16,0},{0,16},{17,1},{1,17},{18,2},{2,18},{19,3},{3,19},{20,4},{4,... | collective-permute-start | bytes 811016 | tf_op jit(solution)/shard_map/ppermute | solution.py:300

commit v5 on v4

v5 whole, which is shorter than its diff:
```python
import jax
import jax.numpy as jnp
from jax import lax
from jax.experimental import pallas as pl
from jax.experimental.pallas import tpu as pltpu
from jax.sharding import PartitionSpec as P

epsilon = 1e-06
step_size = 4.0
newton_turns = 5
light_turn = 3
tile = 8
grant = 16 * 1024 * 1024
f32 = jnp.float32
bf16 = jnp.bfloat16

VMEM = pl.BlockSpec(memory_space=pltpu.VMEM)
SMEM = pl.BlockSpec(memory_space=pltpu.SMEM)


def split(x):
    high = x.astype(bf16)
    return high, (x - high.astype(f32)).astype(bf16)


def dot(a, b, da, db):
    return lax.dot_general(a, b, (((da,), (db,)), ((), ())), preferred_element_type=f32)


def dot3(a, b, da, db):
    return dot(a[0], b[0], da, db) + (dot(a[0], b[1], da, db) + dot(a[1], b[0], da, db))


def iotas(n):
    return (
        lax.broadcasted_iota(jnp.int32, (n, n), 0),
        lax.broadcasted_iota(jnp.int32, (n, n), 1),
    )


def column(row):
    n = row.shape[1]
    return jnp.transpose(jnp.broadcast_to(row, (n, n)))


def start_rotation(gram, row_weight):
    n = gram.shape[0]
    i, j = iotas(n)
    same = i == j
    held = jnp.where(same, gram, 0.0)
    inv_row = lax.rsqrt(jnp.sum(held, axis=0, keepdims=True) + epsilon)
    inv_col = lax.rsqrt(jnp.sum(held, axis=1, keepdims=True) + epsilon)
    corr = gram * inv_col * inv_row
    skew = step_size * corr * (column(row_weight) - row_weight)
    bound = 1.0 + jnp.max(jnp.sum(jnp.abs(skew), axis=0, keepdims=True), axis=1, keepdims=True)
    return jnp.where(same, 1.0, 0.0) + skew * (1.0 / bound)


def rotations(grams, row_weights, fillers=()):
    n = grams[0].shape[0]
    i, j = iotas(n)
    same = i == j
    diag15 = jnp.where(same, 1.5, 0.0)
    diag05 = jnp.where(same, 0.5, 0.0)
    current = [start_rotation(g, w) for g, w in zip(grams, row_weights)]
    for turn in range(newton_turns):
        parts = [split(x) for x in current]
        inner = [dot3(p, p, 1, 1) for p in parts]
        if turn < len(fillers):
            fillers[turn]()
        if turn < light_turn:
            turns = [split(diag15 - 0.5 * y) for y in inner]
            current = [dot3(p, t, 1, 0) for p, t in zip(parts, turns)]
        else:
            fixes = [(diag05 - 0.5 * y).astype(bf16) for y in inner]
            current = [x + dot(p[0], e, 1, 0) for x, p, e in zip(current, parts, fixes)]
    return current


def sizes(n, rows):
    return max(tile, rows // n)


def chunk_rows(reach, width):
    return sizes(reach, 4 * width), sizes(reach, 8 * width), tile


def pair_of(snap, plan, p, width):
    return jnp.concatenate(
        [
            snap[:, pl.ds(pl.multiple_of(plan[0, 0, 2 * p + h] * width, width), width)]
            for h in range(2)
        ],
        axis=1,
    )


def pack_kernel(plan, snap, out, high, low, *, width):
    reach = out.shape[0]
    main, raw, _ = chunk_rows(reach, width)
    i, j = iotas(width)
    held = []
    diags = []
    for p in range(2):
        parts = split(pair_of(snap, plan, p, width))
        high[1 + p] = parts[0]
        low[1 + p] = parts[1]
        gram = dot3(parts, parts, 0, 0)
        upper = gram[:width, :width]
        lower = gram[width:, width:]
        held.append(gram[:width, width:])
        held.append(jnp.where(i <= j, upper, lower))
        diags.append(jnp.sum(jnp.where(i == j, lower, 0.0), axis=0, keepdims=True))
    extra = jnp.concatenate(diags + [jnp.zeros((tile - 2, width), f32)], axis=0)
    for c in range(reach):
        start = c * main
        out[c, :main, :] = held[start // width][start % width : start % width + main]
        out[c, main + raw :, :] = extra if c == 0 else jnp.zeros((tile, width), f32)


def raw_kernel(
    plan, plan_ahead, plan_behind, ahead, behind, packed, own_high, own_low, out, high, low, *, width
):
    del packed, own_high, own_low
    for s, snap, order, p in [(0, ahead, plan_ahead, 0), (3, behind, plan_behind, 1)]:
        parts = split(pair_of(snap, order, p, width))
        high[s] = parts[0]
        low[s] = parts[1]
    reach = out.shape[0]
    main, raw, _ = chunk_rows(reach, width)
    crosses = []
    for r in range(2):
        a, b = [plan[1, 0, 2 * r + h] for h in range(2)]
        crosses.append(dot3((high[b], low[b]), (high[a], low[a]), 0, 0))
    tall = 2 * width
    for c in range(reach):
        block, at = divmod(c * raw, tall)
        out[c, main : main + raw, :] = half(crosses[block // 2], block % 2)[at : at + raw]


def half(x, h):
    width = x.shape[1] // 2
    return x[:, h * width : (h + 1) * width]


def added(values):
    while len(values) > 1:
        values = [a + b for a, b in zip(values[0::2], values[1::2])] + (
            [values[-1]] if len(values) % 2 else []
        )
    return values[0]


def half_sum_kernel(parts, out):
    out[...] = added([parts[c] for c in range(parts.shape[0])])


def join_kernel(here, there, out):
    value = here[...] + there[...]
    for c in range(out.shape[0]):
        out[c] = value


def unpack(gathered, p, width):
    main, raw, _ = chunk_rows(gathered.shape[0], width)
    per = width // main
    cross, both = [
        jnp.concatenate(
            [gathered[(2 * p + q) * per + c, :main, :] for c in range(per)], axis=0
        )
        for q in range(2)
    ]
    i, j = iotas(width)
    flipped = jnp.transpose(both)
    diag_b = gathered[0, main + raw + p : main + raw + p + 1, :]
    upper = jnp.where(i <= j, both, flipped)
    lower = jnp.where(i > j, both, jnp.where(i == j, diag_b, flipped))
    return whole(upper, cross, jnp.transpose(cross), lower)


def unpack_raw(gathered, r, width):
    main, raw, _ = chunk_rows(gathered.shape[0], width)
    per = 2 * width // raw
    return jnp.concatenate(
        [
            jnp.concatenate(
                [
                    gathered[(2 * r + h) * per + c, main : main + raw, :]
                    for c in range(per)
                ],
                axis=0,
            )
            for h in range(2)
        ],
        axis=1,
    )


def whole(upper, cross, flipped, lower):
    return jnp.concatenate(
        [
            jnp.concatenate([upper, cross], axis=1),
            jnp.concatenate([flipped, lower], axis=1),
        ],
        axis=0,
    )


def own_gram(gram, q):
    return dot3(q, split(dot3(split(gram), q, 1, 0)), 0, 0)


def first_kernel(plan, home, weights, gathered, send, turned, spread, *, width):
    tall = 2 * width
    grams, spreads = [], []
    for p in range(2):
        grams.append(unpack(gathered, p, width))
        spreads.append(
            jnp.concatenate(
                [weights[pl.ds(home[plan[0, 0, 2 * p + h]], 1), :] for h in range(2)], axis=1
            )
        )
    turns = rotations(grams, spreads)
    for p in range(2):
        q = half(turns[p], p)
        send[p, :tall, :] = q
        send[p, tall : tall + width, :] = own_gram(grams[p], split(q))
        send[p, tall + width :, :] = jnp.broadcast_to(half(spreads[p], p), (tile, width))
        spread[p] = jnp.broadcast_to(half(spreads[p], 1 - p), (tile, width))
        turned[p] = half(turns[p], 1 - p)


def stay_kernel(gathered, turned, spread, keep, *, width):
    tall = 2 * width
    for p in range(2):
        q = turned[p]
        keep[p, :tall, :] = q
        keep[p, tall : tall + width, :] = own_gram(unpack(gathered, p, width), split(q))
        keep[p, tall + width :, :] = spread[p]


def slot_value(s, received, keep, cut):
    values = [received[0, cut, :], keep[0, cut, :], keep[1, cut, :], received[1, cut, :]]
    return jnp.where(s < 2, jnp.where(s == 0, *values[:2]), jnp.where(s == 2, *values[2:]))


def second_kernel(
    plan, keep, received, gathered, high, low, send, turned, norms, block_high, block_low, *, width
):
    tall = 2 * width
    rows = high.shape[1]
    grams, spreads, fillers = [], [], []

    def filler(r, h, s, q):
        def block():
            at = slice(h * width, (h + 1) * width)
            value = split(dot3((high[s], low[s]), q, 1, 0))
            block_high[r, :, at] = value[0]
            block_low[r, :, at] = value[1]

        return block

    for r in range(2):
        order = [plan[1, 0, 2 * r + h] for h in range(2)]
        first, second = [split(slot_value(s, received, keep, slice(0, tall))) for s in order]
        moved = dot3(split(unpack_raw(gathered, r, width)), first, 1, 0)
        flipped = dot3(second, split(moved), 0, 0)
        own = [slot_value(s, received, keep, slice(tall, tall + width)) for s in order]
        grams.append(whole(own[0], jnp.transpose(flipped), flipped, own[1]))
        wide = [
            slot_value(s, received, keep, slice(tall + width, tall + width + 1)) for s in order
        ]
        spreads.append(jnp.concatenate(wide, axis=1))
        fillers += [filler(r, h, s, q) for h, (s, q) in enumerate(zip(order, (first, second)))]
    turns = rotations(grams, spreads, fillers)
    for p in range(2):
        q = split(turns[p])
        send[p, :rows, :] = dot3(
            (block_high[p], block_low[p]), [half(x, p) for x in q], 1, 0
        )
        moved = dot3(split(grams[p]), q, 1, 0)
        squares = jnp.sum(turns[p] * moved, axis=0, keepdims=True)
        lengths = jnp.sqrt(squares)
        send[p, rows:, :] = jnp.broadcast_to(half(lengths, p), (tile, width))
        norms[p] = jnp.broadcast_to(half(lengths, 1 - p), (tile, width))
        turned[p] = half(turns[p], 1 - p)


def finish_kernel(high, low, turned, kept):
    for p in range(2):
        kept[p] = dot3((high[p], low[p]), split(turned[p]), 1, 0)


def last_kernel(kept, norms_here, received, final, norms):
    rows, width = kept.shape[1], kept.shape[2]
    order = [received[0, :rows, :], kept[0], kept[1], received[1, :rows, :]]
    lengths = [received[0, rows:, :], norms_here[0], norms_here[1], received[1, rows:, :]]
    for s in range(4):
        final[:, s * width : (s + 1) * width] = order[s]
        norms[s : s + 1, :] = lengths[s][:1]


def near(x):
    return pltpu.with_memory_space_constraint(x, pltpu.VMEM)


def far(x):
    return pltpu.with_memory_space_constraint(x, pltpu.HBM)


def call(kernel, outs, specs, aliases=None, **static):
    def run(*refs):
        kernel(*refs, **static)

    return pl.pallas_call(
        run,
        out_shape=outs,
        in_specs=specs,
        out_specs=jax.tree.map(lambda _: VMEM, outs),
        input_output_aliases=aliases or {},
        compiler_params=pltpu.CompilerParams(vmem_limit_bytes=grant),
        name=kernel.__name__,
    )


def shape(*dims):
    return pltpu.VMEM(dims, f32)


def routes():
    count = lax.axis_size("pair")
    ahead = [((i - 1) % count, i) for i in range(count)]
    behind = [((i + 1) % count, i) for i in range(count)]
    return ahead, behind, sorted(ahead) == sorted(behind)


def both_ways(x):
    ahead, behind, alike = routes()
    first = lax.ppermute(x, "pair", ahead)
    return first, first if alike else lax.ppermute(x, "pair", behind)


def exchange(send):
    ahead, behind, alike = routes()
    if alike:
        return near(lax.ppermute(send, "pair", ahead))
    return jnp.stack(
        [lax.ppermute(send[0], "pair", ahead), lax.ppermute(send[1], "pair", behind)]
    )


def swap(parts, groups=None):
    return near(
        lax.all_to_all(parts, "row", 0, 0, tiled=True, axis_index_groups=groups)
    )


def halved_total(parts):
    n = lax.axis_size("row")
    reach = n // 2
    groups = [list(range(reach)), list(range(reach, n))]
    mine = swap(parts, groups)
    here = call(half_sum_kernel, shape(*parts.shape[1:]), [VMEM])(mine)
    there = near(lax.ppermute(here, "row", [(i, (i + reach) % n) for i in range(n)]))
    both = call(join_kernel, shape(*parts.shape), [VMEM, VMEM])(here, there)
    return swap(both, groups)


def body(snapshot, weights, block_home, plan):
    rows = snapshot.shape[0]
    width = weights.shape[1]
    reach = lax.axis_size("row") // 2
    chunk = sum(chunk_rows(reach, width))
    snap_ahead, snap_behind = both_ways(snapshot)
    plan_ahead, plan_behind = both_ways(plan)
    wide = pltpu.VMEM((4, rows, 2 * width), bf16)
    packed, high, low = call(
        pack_kernel, [shape(reach, chunk, width), wide, wide], [SMEM, VMEM], width=width
    )(far(plan), far(snapshot))
    packed, high, low = call(
        raw_kernel,
        [shape(reach, chunk, width), wide, wide],
        [SMEM] * 3 + [VMEM] * 5,
        {5: 0, 6: 1, 7: 2},
        width=width,
    )(plan, plan_ahead, plan_behind, near(snap_ahead), near(snap_behind), packed, high, low)
    gathered = halved_total(packed)
    tall = 3 * width + tile
    send, turned, spread = call(
        first_kernel,
        [shape(2, tall, width), shape(2, 2 * width, width), shape(2, tile, width)],
        [SMEM, SMEM, VMEM, VMEM],
        width=width,
    )(plan, block_home, weights, gathered)
    received = exchange(send)
    keep = call(stay_kernel, shape(2, tall, width), [VMEM, VMEM, VMEM], width=width)(
        gathered, turned, spread
    )
    block = pltpu.VMEM((2, rows, 2 * width), bf16)
    send, turned, norms, block_high, block_low = call(
        second_kernel,
        [
            shape(2, rows + tile, width),
            shape(2, 2 * width, width),
            shape(2, tile, width),
            block,
            block,
        ],
        [SMEM] + [VMEM] * 5,
        width=width,
    )(plan, keep, received, gathered, high, low)
    arrived = exchange(send)
    kept = call(finish_kernel, shape(2, rows, width), [VMEM, VMEM, VMEM])(
        block_high, block_low, turned
    )
    final, norms = call(
        last_kernel,
        [jax.ShapeDtypeStruct((rows, 4 * width), f32), jax.ShapeDtypeStruct((4, width), f32)],
        [VMEM, VMEM, VMEM],
    )(kept, norms, arrived)
    return final, norms.reshape(4 * width)


def solution(mesh):
    in_specs = (P("row", "pair"), P(), P("pair"), P(None, "pair", None))
    out_specs = (P("row", "pair"), P("pair"))
    return jax.shard_map(body, mesh=mesh, in_specs=in_specs, out_specs=out_specs, check_vma=False)
```

time: 67.7 us -> 60.4 us (0.89)
  blocking collectives: 45 us -> 33.9 us
  waiting for transfers between devices: 4.02 us -> 6.1 us
  starting transfers between devices: 2.8 us -> 3.56 us
    all_to_all x4 -> x2, blocking collectives: 45 us -> 33.9 us  [swap(): lax.all_to_all(parts, 'row', 0, 0, tiled=True, axis_index_groups=groups)]
    ppermute x1, waiting for transfers between devices: 2.66 us -> 4.07 us  [halved_total(): lax.ppermute(here, 'row', [(i, (i + reach) % n) for i in range(n)])]
    pallas_call x1, Pallas kernels: 4.58 us -> 5.37 us  [body(): call(second_kernel, [shape(2, rows + tile, width), shape(2, 2 * width, wi...]
    pallas_call x4 -> x3, Pallas kernels: 3.96 us -> 3.54 us  [the longest x1 1.52 us: body(): call(pack_kernel, [shape(reach, chunk, width), wide, wide], [SMEM, VMEM],...]
  transfers between devices with their start and end apart: 3 -> 5, of which waited for: 3 -> 4; matrix products, arithmetic and copies ran while one was open for 0% -> 0% of each run, Pallas kernels for 3% -> 5%
where the time goes in v5:
time: 60.4 us; the launch traced here: 60.1 us
  blocking collectives  33.9 us (56%)
  Pallas kernels  15.2 us (25%)
  waiting for transfers between devices  6.1 us (10%)
  starting transfers between devices  3.56 us (6%)
  between operations  0.71 us (1%)
  local copies, waits for them, and re-layouts  0.69 us (1%)
    all_to_all x2, blocking collectives, swap(): lax.all_to_all(parts, 'row', 0, 0, tiled=True, axis_index_groups=groups)  33.9 us
    pallas_call x1, Pallas kernels, body(): call(second_kernel, [shape(2, rows + tile, width), shape(2, 2 * width, wi...  5.37 us
    pallas_call x1, Pallas kernels, body(): call(first_kernel, [shape(2, tall, width), shape(2, 2 * width, width), sh...  4.94 us
    ppermute x1, waiting for transfers between devices, halved_total(): lax.ppermute(here, 'row', [(i, (i + reach) % n) for i in range(n)])  4.07 us
    ppermute x1, starting transfers between devices, halved_total(): lax.ppermute(here, 'row', [(i, (i + reach) % n) for i in range(n)])  2.66 us
    ppermute x2, waiting for transfers between devices, exchange(): return near(lax.ppermute(send, 'pair', ahead))  1.88 us
    pallas_call x1, Pallas kernels, body(): call(pack_kernel, [shape(reach, chunk, width), wide, wide], [SMEM, VMEM],...  1.52 us
  transfers between devices with their start and end apart: 5, of which 4 were waited for; matrix products, arithmetic and copies ran while one was open for 0% of the time, Pallas kernels for 5%

profile of v5, /device:TPU:0, one launch (start us, length us, event | category | flops | bytes accessed | tf_op | source)
XLA Modules:
  0.0 60.1 jit_solution(8422090001111691576)
XLA Ops:
  0.6 0.6 collective-permute-start.1
  1.2 0.1 collective-permute-start
  1.3 1.5 %pack_kernel.1 = (f32[8,200,128]{2,1,0:T(8,128)S(1)}, bf16[4,256,256]{2,1,0:T(8,128)(2,1)S(1)}, bf16[4,256,256]{2,1,0:T(8,128)(2,1)S(1)}) custom-call(s32[2,1,4]{2,1,0:T(1,128)} %refs_0_.7, f32[256,512]{1,0:T(8,128)} %refs_1_.2), custom_call_target="tpu_custom_call" | custom-call | tf_op jit(solution)/shard_map/pack_kernel/pallas_call | solution.py:377
  2.8 0.1 collective-permute-done.refs_1_.refs_2_
  2.9 0.0 collective-permute-done.1.refs_3_.refs_4_
  2.9 0.0 copy-start
  2.9 0.7 %copy-done = s32[2,1,4]{2,1,0:T(1,128)S(1)} copy-done((s32[2,1,4]{2,1,0:T(1,128)S(1)}, s32[2,1,4]{2,1,0:T(1,128)}, u32[]{:S(2)}) %copy-start) | copy-done | bytes 56
  3.6 1.1 %raw_kernel.1 = (f32[8,200,128]{2,1,0:T(8,128)S(1)}, bf16[4,256,256]{2,1,0:T(8,128)(2,1)S(1)}, bf16[4,256,256]{2,1,0:T(8,128)(2,1)S(1)}) custom-call(s32[2,1,4]{2,1,0:T(1,128)S(1)} %copy-done, s32[2,1,4]{2,1,0:T(1,128)S(1)} %collective-permute-done.refs_1_.refs_2_, ...), custom_call_target="tpu_custom_call", output_to_operand_aliasing={{0}: (5, {}), {1}: (6, {}), {2}: (7, {})} | custom-call | tf_op jit(solution)/shard_map/raw_kernel/pallas_call | solution.py:380
  4.8 19.1 %all_to_all.10.refs_0_ = f32[8,200,128]{2,1,0:T(8,128)S(1)} all-to-all(f32[8,200,128]{2,1,0:T(8,128)S(1)} %get-tuple-element.21), channel_id=1, replica_groups={{0,1,2,3,4,5,6,7},{8,9,10,11,12,13,14,15},{16,17,18,19,20,21,22,23},{24..., dimensions={0} | all-to-all | bytes 1638400 | tf_op jit(solution)/shard_map/all_to_all | solution.py:354
  23.9 2.7 %collective-permute-start.2 = (f32[200,128]{1,0:T(8,128)S(1)}, f32[200,128]{1,0:T(8,128)S(1)}, u32[]{:S(2)}, u32[]{:S(2)}) collective-permute-start(f32[200,128]{1,0:T(8,128)S(1)} %half_sum_kernel.1.refs_0_), channel_id=1, source_target_pairs={{0,8},{1,9},{2,10},{3,11},{4,12},{5,13},{6,14},{7,15},{8,0},{9,1},... | collective-permute-start | bytes 307208 | tf_op jit(solution)/shard_map/ppermute | solution.py:364
  26.5 4.1 %collective-permute-done.2.refs_1_ = f32[200,128]{1,0:T(8,128)S(1)} collective-permute-done((f32[200,128]{1,0:T(8,128)S(1)}, f32[200,128]{1,0:T(8,128)S(1)}, u32[]{:S(2)}, u32[]{:S(2)}) %collective-permute-start.2) | collective-permute-done | bytes 102432 | tf_op jit(solution)/shard_map/ppermute | solution.py:364
  30.6 0.1 join_kernel.1
  30.7 0.0 copy-start.1
  30.7 0.0 copy-start.2
  30.7 14.8 %all_to_all.11.refs_3_.refs_0_ = f32[8,200,128]{2,1,0:T(8,128)S(1)} all-to-all(f32[8,200,128]{2,1,0:T(8,128)S(1)} %join_kernel.1), channel_id=1, replica_groups={{0,1,2,3,4,5,6,7},{8,9,10,11,12,13,14,15},{16,17,18,19,20,21,22,23},{24..., dimensions={0} | all-to-all | bytes 1638400 | tf_op jit(solution)/shard_map/all_to_all | solution.py:354
  45.5 0.0 copy-done.1
  45.5 0.0 copy-done.2
  45.5 4.9 %first_kernel.1 = (f32[2,392,128]{2,1,0:T(8,128)S(1)}, f32[2,256,128]{2,1,0:T(8,128)S(1)}, f32[2,8,128]{2,1,0:T(8,128)S(1)}) custom-call(s32[2,1,4]{2,1,0:T(1,128)S(1)} %copy-done, s32[4]{0:T(128)S(1)} %copy-done.2, f32[8,128]{1,0:T(8,128)S(1)} %copy-done.1, f32[8,200,128]{2,1,0:T(8,128)S(1)} %all_to_all.11.refs_3_.refs_0_), custom_call_target="tpu_custom_call" | custom-call | tf_op jit(solution)/shard_map/first_kernel/pallas_call | solution.py:389
  50.5 0.1 collective-permute-start.3
  50.6 0.9 %stay_kernel.1.refs_1_ = f32[2,392,128]{2,1,0:T(8,128)S(1)} custom-call(f32[8,200,128]{2,1,0:T(8,128)S(1)} %all_to_all.11.refs_3_.refs_0_, f32[2,256,128]{2,1,0:T(8,128)S(1)} %get-tuple-element.22.refs_1_, f32[2,8,128]{2,1,0:T(8,128)S(1)} %get-tuple-element.23.refs_2_), custom_call_target="tpu_custom_call" | custom-call | tf_op jit(solution)/shard_map/stay_kernel/pallas_call | solution.py:396
  51.5 0.8 %collective-permute-done.3.refs_2_ = f32[2,392,128]{2,1,0:T(8,128)S(1)} collective-permute-done((f32[2,392,128]{2,1,0:T(8,128)S(1)}, f32[2,392,128]{2,1,0:T(8,128)S(1)}, u32[]{:S(2)}, u32[]{:S(2)}) %collective-permute-start.3) | collective-permute-done | bytes 401440 | tf_op jit(solution)/shard_map/ppermute | solution.py:346
  52.3 5.4 %second_kernel.1 = (f32[2,264,128]{2,1,0:T(8,128)S(1)}, f32[2,256,128]{2,1,0:T(8,128)S(1)}, f32[2,8,128]{2,1,0:T(8,128)S(1)}, bf16[2,256,256]{2,1,0:T(8,128)(2,1)S(1)}, bf16[2,256,256]{2,1,0:T(8,128)(2,1)S(1)}) custom-call(s32[2,1,4]{2,1,0:T(1,128)S(1)} %copy-done, f32[2,392,128]{2,1,0:T(8,128)S(1)} %stay_kernel.1.refs_1_, ...), custom_call_target="tpu_custom_call" | custom-call | tf_op jit(solution)/shard_map/second_kernel/pallas_call | solution.py:400
  57.7 0.2 collective-permute-start.4
  57.9 0.4 finish_kernel.1.refs_0_
  58.2 1.1 %collective-permute-done.4.refs_2_ = f32[2,264,128]{2,1,0:T(8,128)S(1)} collective-permute-done((f32[2,264,128]{2,1,0:T(8,128)S(1)}, f32[2,264,128]{2,1,0:T(8,128)S(1)}, u32[]{:S(2)}, u32[]{:S(2)}) %collective-permute-start.4) | collective-permute-done | bytes 270368 | tf_op jit(solution)/shard_map/ppermute | solution.py:346
  59.3 0.9 %last_kernel.1 = (f32[256,512]{1,0:T(8,128)}, f32[4,128]{1,0:T(4,128)}) custom-call(f32[2,256,128]{2,1,0:T(8,128)S(1)} %finish_kernel.1.refs_0_, f32[2,8,128]{2,1,0:T(8,128)S(1)} %get-tuple-element.30.refs_1_, f32[2,264,128]{2,1,0:T(8,128)S(1)} %collective-permute-done.4.refs_2_), custom_call_target="tpu_custom_call" | custom-call | tf_op jit(solution)/shard_map/last_kernel/pallas_call | solution.py:416
  (1 shorter events, 0.0 us)
Async XLA Ops:
  0.6 2.3 %collective-permute-start.1 = (f32[256,512]{1,0:T(8,128)}, f32[256,512]{1,0:T(8,128)S(1)}, u32[]{:S(2)}, u32[]{:S(2)}) collective-permute-start(f32[256,512]{1,0:T(8,128)} %refs_1_.2), channel_id=1, source_target_pairs={{16,0},{0,16},{17,1},{1,17},{18,2},{2,18},{19,3},{3,19},{20,4},{4,... | collective-permute-start | bytes 1572872 | tf_op jit(solution)/shard_map/ppermute | solution.py:339
  1.2 1.7 %collective-permute-start = (s32[2,1,4]{2,1,0:T(1,128)}, s32[2,1,4]{2,1,0:T(1,128)S(1)}, u32[]{:S(2)}, u32[]{:S(2)}) collective-permute-start(s32[2,1,4]{2,1,0:T(1,128)} %refs_0_.7), channel_id=1, source_target_pairs={{16,0},{0,16},{17,1},{1,17},{18,2},{2,18},{19,3},{3,19},{20,4},{4,... | collective-permute-start | bytes 104 | tf_op jit(solution)/shard_map/ppermute | solution.py:339
  2.9 0.7 %copy-start = (s32[2,1,4]{2,1,0:T(1,128)S(1)}, s32[2,1,4]{2,1,0:T(1,128)}, u32[]{:S(2)}) copy-start(s32[2,1,4]{2,1,0:T(1,128)} %refs_0_.7) | copy-start | bytes 100
  23.9 6.7 %collective-permute-start.2 = (f32[200,128]{1,0:T(8,128)S(1)}, f32[200,128]{1,0:T(8,128)S(1)}, u32[]{:S(2)}, u32[]{:S(2)}) collective-permute-start(f32[200,128]{1,0:T(8,128)S(1)} %half_sum_kernel.1.refs_0_), channel_id=1, source_target_pairs={{0,8},{1,9},{2,10},{3,11},{4,12},{5,13},{6,14},{7,15},{8,0},{9,1},... | collective-permute-start | bytes 307208 | tf_op jit(solution)/shard_map/ppermute | solution.py:364
  30.7 14.9 %copy-start.1 = (f32[8,128]{1,0:T(8,128)S(1)}, f32[8,128]{1,0:T(8,128)}, u32[]{:S(2)}) copy-start(f32[8,128]{1,0:T(8,128)} %refs_2_.1) | copy-start | bytes 12292
  30.7 14.9 %copy-start.2 = (s32[4]{0:T(128)S(1)}, s32[4]{0:T(128)}, u32[]{:S(2)}) copy-start(s32[4]{0:T(128)} %refs_1_.3) | copy-start | bytes 52
  50.5 1.8 %collective-permute-start.3 = (f32[2,392,128]{2,1,0:T(8,128)S(1)}, f32[2,392,128]{2,1,0:T(8,128)S(1)}, u32[]{:S(2)}, u32[]{:S(2)}) collective-permute-start(f32[2,392,128]{2,1,0:T(8,128)S(1)} %get-tuple-element.24), channel_id=1, source_target_pairs={{16,0},{0,16},{17,1},{1,17},{18,2},{2,18},{19,3},{3,19},{20,4},{4,... | collective-permute-start | bytes 1204232 | tf_op jit(solution)/shard_map/ppermute | solution.py:346
  57.7 1.6 %collective-permute-start.4 = (f32[2,264,128]{2,1,0:T(8,128)S(1)}, f32[2,264,128]{2,1,0:T(8,128)S(1)}, u32[]{:S(2)}, u32[]{:S(2)}) collective-permute-start(f32[2,264,128]{2,1,0:T(8,128)S(1)} %get-tuple-element.31), channel_id=1, source_target_pairs={{16,0},{0,16},{17,1},{1,17},{18,2},{2,18},{19,3},{3,19},{20,4},{4,... | collective-permute-start | bytes 811016 | tf_op jit(solution)/shard_map/ppermute | solution.py:346

commit v6 on v5

--- a/solution.py
+++ b/solution.py
@@ -8,7 +8,6 @@
 epsilon = 1e-06
 step_size = 4.0
 newton_turns = 5
-light_turn = 3
 tile = 8
 grant = 16 * 1024 * 1024
 f32 = jnp.float32
@@ -63,18 +62,22 @@
     diag15 = jnp.where(same, 1.5, 0.0)
     diag05 = jnp.where(same, 0.5, 0.0)
     current = [start_rotation(g, w) for g, w in zip(grams, row_weights)]
-    for turn in range(newton_turns):
+    for turn in range(newton_turns - 1):
         parts = [split(x) for x in current]
         inner = [dot3(p, p, 1, 1) for p in parts]
         if turn < len(fillers):
             fillers[turn]()
-        if turn < light_turn:
+        if turn < newton_turns - 2:
             turns = [split(diag15 - 0.5 * y) for y in inner]
             current = [dot3(p, t, 1, 0) for p, t in zip(parts, turns)]
-        else:
-            fixes = [(diag05 - 0.5 * y).astype(bf16) for y in inner]
-            current = [x + dot(p[0], e, 1, 0) for x, p, e in zip(current, parts, fixes)]
-    return current
+    small = [diag05 - 0.5 * y for y in inner]
+    low = [e.astype(bf16) for e in small]
+    squared = [dot(e, e, 1, 0) for e in low]
+    rest = [(diag15 + (2.5 * e + u)).astype(bf16) for e, u in zip(small, squared)]
+    fixes = [
+        (e + dot(u.astype(bf16), r, 1, 0)).astype(bf16) for e, u, r in zip(small, squared, rest)
+    ]
+    return [x + dot(p[0], f, 1, 0) for x, p, f in zip(current, parts, fixes)]
 
 
 def sizes(n, rows):
@@ -95,8 +98,15 @@
     )
 
 
-def pack_kernel(plan, snap, out, high, low, *, width):
+def pack_kernel(plan, snap, out, high, low, plan_out, *, width):
     reach = out.shape[0]
+    t = lax.broadcasted_iota(jnp.int32, plan.shape, 0)
+    k = lax.broadcasted_iota(jnp.int32, plan.shape, 2)
+    copied = jnp.zeros(plan.shape, jnp.int32)
+    for a in range(plan.shape[0]):
+        for b in range(plan.shape[2]):
+            copied = jnp.where((t == a) & (k == b), plan[a, 0, b], copied)
+    plan_out[...] = copied
     main, raw, _ = chunk_rows(reach, width)
     i, j = iotas(width)
     held = []
@@ -374,8 +384,11 @@
     snap_ahead, snap_behind = both_ways(snapshot)
     plan_ahead, plan_behind = both_ways(plan)
     wide = pltpu.VMEM((4, rows, 2 * width), bf16)
-    packed, high, low = call(
-        pack_kernel, [shape(reach, chunk, width), wide, wide], [SMEM, VMEM], width=width
+    packed, high, low, plan = call(
+        pack_kernel,
+        [shape(reach, chunk, width), wide, wide, pltpu.VMEM(plan.shape, plan.dtype)],
+        [SMEM, VMEM],
+        width=width,
     )(far(plan), far(snapshot))
     packed, high, low = call(
         raw_kernel,

time: 60.4 us -> 59.4 us (0.983)
  local copies, waits for them, and re-layouts: 0.69 us -> 0.01 us
    unnamed x6 -> x4, local copies, waits for them, and re-layouts: 0.69 us -> 0.01 us
where the time goes in v6:
time: 59.4 us; the launch traced here: 59.2 us
  blocking collectives  33.9 us (57%)
  Pallas kernels  14.9 us (25%)
  waiting for transfers between devices  6.08 us (10%)
  starting transfers between devices  3.57 us (6%)
  between operations  0.71 us (1%)
    all_to_all x2, blocking collectives, swap(): lax.all_to_all(parts, 'row', 0, 0, tiled=True, axis_index_groups=groups)  33.9 us
    pallas_call x1, Pallas kernels, body(): call(second_kernel, [shape(2, rows + tile, width), shape(2, 2 * width, wi...  5.22 us
    pallas_call x1, Pallas kernels, body(): call(first_kernel, [shape(2, tall, width), shape(2, 2 * width, width), sh...  4.8 us
    ppermute x1, waiting for transfers between devices, halved_total(): lax.ppermute(here, 'row', [(i, (i + reach) % n) for i in range(n)])  4.06 us
    ppermute x1, starting transfers between devices, halved_total(): lax.ppermute(here, 'row', [(i, (i + reach) % n) for i in range(n)])  2.66 us
    ppermute x2, waiting for transfers between devices, exchange(): return near(lax.ppermute(send, 'pair', ahead))  1.87 us
    pallas_call x1, Pallas kernels, body(): call(pack_kernel, [shape(reach, chunk, width), wide, wide, pltpu.VMEM(pla...  1.52 us
  transfers between devices with their start and end apart: 5, of which 4 were waited for; matrix products, arithmetic and copies ran while one was open for 0% of the time, Pallas kernels for 5%

profile of v6, /device:TPU:0, one launch (start us, length us, event | category | flops | bytes accessed | tf_op | source)
XLA Modules:
  0.0 59.2 jit_solution(8366075841725028681)
XLA Ops:
  0.6 0.6 collective-permute-start.1
  1.2 0.1 collective-permute-start
  1.3 1.5 %pack_kernel.1 = (f32[8,200,128]{2,1,0:T(8,128)S(1)}, bf16[4,256,256]{2,1,0:T(8,128)(2,1)S(1)}, bf16[4,256,256]{2,1,0:T(8,128)(2,1)S(1)}, s32[2,1,4]{2,1,0:T(1,128)S(1)}) custom-call(s32[2,1,4]{2,1,0:T(1,128)} %refs_0_.1, f32[256,512]{1,0:T(8,128)} %refs_1_.2), custom_call_target="tpu_custom_call" | custom-call | tf_op jit(solution)/shard_map/pack_kernel/pallas_call | solution.py:387
  2.8 0.1 collective-permute-done.refs_1_.refs_2_
  2.9 0.0 collective-permute-done.1.refs_3_.refs_4_
  2.9 1.1 %raw_kernel.1 = (f32[8,200,128]{2,1,0:T(8,128)S(1)}, bf16[4,256,256]{2,1,0:T(8,128)(2,1)S(1)}, bf16[4,256,256]{2,1,0:T(8,128)(2,1)S(1)}) custom-call(s32[2,1,4]{2,1,0:T(1,128)S(1)} %get-tuple-element.19.refs_0_, s32[2,1,4]{2,1,0:T(1,128)S(1)} %collective-permute-done.refs_1_.refs_2_, ...), custom_call_target="tpu_custom_call", output_to_operand_aliasing={{0}: (5, {}), {1}: (6, {}), {2}: (7, {})} | custom-call | tf_op jit(solution)/shard_map/raw_kernel/pallas_call | solution.py:393
  4.1 19.1 %all_to_all.10.refs_0_ = f32[8,200,128]{2,1,0:T(8,128)S(1)} all-to-all(f32[8,200,128]{2,1,0:T(8,128)S(1)} %get-tuple-element.23), channel_id=1, replica_groups={{0,1,2,3,4,5,6,7},{8,9,10,11,12,13,14,15},{16,17,18,19,20,21,22,23},{24..., dimensions={0} | all-to-all | bytes 1638400 | tf_op jit(solution)/shard_map/all_to_all | solution.py:364
  23.2 2.7 %collective-permute-start.2 = (f32[200,128]{1,0:T(8,128)S(1)}, f32[200,128]{1,0:T(8,128)S(1)}, u32[]{:S(2)}, u32[]{:S(2)}) collective-permute-start(f32[200,128]{1,0:T(8,128)S(1)} %half_sum_kernel.1.refs_0_), channel_id=1, source_target_pairs={{0,8},{1,9},{2,10},{3,11},{4,12},{5,13},{6,14},{7,15},{8,0},{9,1},... | collective-permute-start | bytes 307208 | tf_op jit(solution)/shard_map/ppermute | solution.py:374
  25.9 4.1 %collective-permute-done.2.refs_1_ = f32[200,128]{1,0:T(8,128)S(1)} collective-permute-done((f32[200,128]{1,0:T(8,128)S(1)}, f32[200,128]{1,0:T(8,128)S(1)}, u32[]{:S(2)}, u32[]{:S(2)}) %collective-permute-start.2) | collective-permute-done | bytes 102432 | tf_op jit(solution)/shard_map/ppermute | solution.py:374
  29.9 0.1 join_kernel.1
  30.0 0.0 copy-start
  30.0 0.0 copy-start.1
  30.0 14.8 %all_to_all.11.refs_3_.refs_0_ = f32[8,200,128]{2,1,0:T(8,128)S(1)} all-to-all(f32[8,200,128]{2,1,0:T(8,128)S(1)} %join_kernel.1), channel_id=1, replica_groups={{0,1,2,3,4,5,6,7},{8,9,10,11,12,13,14,15},{16,17,18,19,20,21,22,23},{24..., dimensions={0} | all-to-all | bytes 1638400 | tf_op jit(solution)/shard_map/all_to_all | solution.py:364
  44.8 0.0 copy-done
  44.8 0.0 copy-done.1
  44.9 4.8 %first_kernel.1 = (f32[2,392,128]{2,1,0:T(8,128)S(1)}, f32[2,256,128]{2,1,0:T(8,128)S(1)}, f32[2,8,128]{2,1,0:T(8,128)S(1)}) custom-call(s32[2,1,4]{2,1,0:T(1,128)S(1)} %get-tuple-element.19.refs_0_, s32[4]{0:T(128)S(1)} %copy-done.1, f32[8,128]{1,0:T(8,128)S(1)} %copy-done, f32[8,200,128]{2,1,0:T(8,128)S(1)} %all_to_all.11.refs_3_.refs_0_), custom_call_target="tpu_custom_call" | custom-call | tf_op jit(solution)/shard_map/first_kernel/pallas_call | solution.py:402
  49.7 0.1 collective-permute-start.3
  49.7 0.9 %stay_kernel.1.refs_1_ = f32[2,392,128]{2,1,0:T(8,128)S(1)} custom-call(f32[8,200,128]{2,1,0:T(8,128)S(1)} %all_to_all.11.refs_3_.refs_0_, f32[2,256,128]{2,1,0:T(8,128)S(1)} %get-tuple-element.24.refs_1_, f32[2,8,128]{2,1,0:T(8,128)S(1)} %get-tuple-element.25.refs_2_), custom_call_target="tpu_custom_call" | custom-call | tf_op jit(solution)/shard_map/stay_kernel/pallas_call | solution.py:409
  50.6 0.8 %collective-permute-done.3.refs_2_ = f32[2,392,128]{2,1,0:T(8,128)S(1)} collective-permute-done((f32[2,392,128]{2,1,0:T(8,128)S(1)}, f32[2,392,128]{2,1,0:T(8,128)S(1)}, u32[]{:S(2)}, u32[]{:S(2)}) %collective-permute-start.3) | collective-permute-done | bytes 401440 | tf_op jit(solution)/shard_map/ppermute | solution.py:356
  51.5 5.2 %second_kernel.1 = (f32[2,264,128]{2,1,0:T(8,128)S(1)}, f32[2,256,128]{2,1,0:T(8,128)S(1)}, f32[2,8,128]{2,1,0:T(8,128)S(1)}, bf16[2,256,256]{2,1,0:T(8,128)(2,1)S(1)}, bf16[2,256,256]{2,1,0:T(8,128)(2,1)S(1)}) custom-call(s32[2,1,4]{2,1,0:T(1,128)S(1)} %get-tuple-element.19.refs_0_, f32[2,392,128]{2,1,0:T(8,128)S(1)} %stay_kernel.1.refs_1_, ...), custom_call_target="tpu_custom_call" | custom-call | tf_op jit(solution)/shard_map/second_kernel/pallas_call | solution.py:413
  56.7 0.2 collective-permute-start.4
  56.9 0.4 finish_kernel.1.refs_0_
  57.3 1.0 %collective-permute-done.4.refs_2_ = f32[2,264,128]{2,1,0:T(8,128)S(1)} collective-permute-done((f32[2,264,128]{2,1,0:T(8,128)S(1)}, f32[2,264,128]{2,1,0:T(8,128)S(1)}, u32[]{:S(2)}, u32[]{:S(2)}) %collective-permute-start.4) | collective-permute-done | bytes 270368 | tf_op jit(solution)/shard_map/ppermute | solution.py:356
  58.3 0.9 %last_kernel.1 = (f32[256,512]{1,0:T(8,128)}, f32[4,128]{1,0:T(4,128)}) custom-call(f32[2,256,128]{2,1,0:T(8,128)S(1)} %finish_kernel.1.refs_0_, f32[2,8,128]{2,1,0:T(8,128)S(1)} %get-tuple-element.32.refs_1_, f32[2,264,128]{2,1,0:T(8,128)S(1)} %collective-permute-done.4.refs_2_), custom_call_target="tpu_custom_call" | custom-call | tf_op jit(solution)/shard_map/last_kernel/pallas_call | solution.py:429
  (1 shorter events, 0.0 us)
Async XLA Ops:
  0.6 2.3 %collective-permute-start.1 = (f32[256,512]{1,0:T(8,128)}, f32[256,512]{1,0:T(8,128)S(1)}, u32[]{:S(2)}, u32[]{:S(2)}) collective-permute-start(f32[256,512]{1,0:T(8,128)} %refs_1_.2), channel_id=1, source_target_pairs={{16,0},{0,16},{17,1},{1,17},{18,2},{2,18},{19,3},{3,19},{20,4},{4,... | collective-permute-start | bytes 1572872 | tf_op jit(solution)/shard_map/ppermute | solution.py:349
  1.2 1.7 %collective-permute-start = (s32[2,1,4]{2,1,0:T(1,128)}, s32[2,1,4]{2,1,0:T(1,128)S(1)}, u32[]{:S(2)}, u32[]{:S(2)}) collective-permute-start(s32[2,1,4]{2,1,0:T(1,128)} %refs_0_.1), channel_id=1, source_target_pairs={{16,0},{0,16},{17,1},{1,17},{18,2},{2,18},{19,3},{3,19},{20,4},{4,... | collective-permute-start | bytes 104 | tf_op jit(solution)/shard_map/ppermute | solution.py:349
  23.2 6.7 %collective-permute-start.2 = (f32[200,128]{1,0:T(8,128)S(1)}, f32[200,128]{1,0:T(8,128)S(1)}, u32[]{:S(2)}, u32[]{:S(2)}) collective-permute-start(f32[200,128]{1,0:T(8,128)S(1)} %half_sum_kernel.1.refs_0_), channel_id=1, source_target_pairs={{0,8},{1,9},{2,10},{3,11},{4,12},{5,13},{6,14},{7,15},{8,0},{9,1},... | collective-permute-start | bytes 307208 | tf_op jit(solution)/shard_map/ppermute | solution.py:374
  30.0 14.9 %copy-start = (f32[8,128]{1,0:T(8,128)S(1)}, f32[8,128]{1,0:T(8,128)}, u32[]{:S(2)}) copy-start(f32[8,128]{1,0:T(8,128)} %refs_2_.1) | copy-start | bytes 12292
  30.0 14.9 %copy-start.1 = (s32[4]{0:T(128)S(1)}, s32[4]{0:T(128)}, u32[]{:S(2)}) copy-start(s32[4]{0:T(128)} %refs_1_.3) | copy-start | bytes 52
  49.7 1.8 %collective-permute-start.3 = (f32[2,392,128]{2,1,0:T(8,128)S(1)}, f32[2,392,128]{2,1,0:T(8,128)S(1)}, u32[]{:S(2)}, u32[]{:S(2)}) collective-permute-start(f32[2,392,128]{2,1,0:T(8,128)S(1)} %get-tuple-element.26), channel_id=1, source_target_pairs={{16,0},{0,16},{17,1},{1,17},{18,2},{2,18},{19,3},{3,19},{20,4},{4,... | collective-permute-start | bytes 1204232 | tf_op jit(solution)/shard_map/ppermute | solution.py:356
  56.7 1.6 %collective-permute-start.4 = (f32[2,264,128]{2,1,0:T(8,128)S(1)}, f32[2,264,128]{2,1,0:T(8,128)S(1)}, u32[]{:S(2)}, u32[]{:S(2)}) collective-permute-start(f32[2,264,128]{2,1,0:T(8,128)S(1)} %get-tuple-element.33), channel_id=1, source_target_pairs={{16,0},{0,16},{17,1},{1,17},{18,2},{2,18},{19,3},{3,19},{20,4},{4,... | collective-permute-start | bytes 811016 | tf_op jit(solution)/shard_map/ppermute | solution.py:356

commit v7 on v6

--- a/solution.py
+++ b/solution.py
@@ -28,6 +28,11 @@
 
 def dot3(a, b, da, db):
     return dot(a[0], b[0], da, db) + (dot(a[0], b[1], da, db) + dot(a[1], b[0], da, db))
+
+
+def outer(a):
+    cross = dot(a[1], a[0], 1, 1)
+    return dot(a[0], a[0], 1, 1) + (cross + jnp.transpose(cross))
 
 
 def iotas(n):
@@ -64,7 +69,7 @@
     current = [start_rotation(g, w) for g, w in zip(grams, row_weights)]
     for turn in range(newton_turns - 1):
         parts = [split(x) for x in current]
-        inner = [dot3(p, p, 1, 1) for p in parts]
+        inner = [outer(p) for p in parts]
         if turn < len(fillers):
             fillers[turn]()
         if turn < newton_turns - 2:
@@ -98,7 +103,7 @@
     )
 
 
-def pack_kernel(plan, snap, out, high, low, plan_out, *, width):
+def pack_kernel(plan, home, weights, snap, out, high, low, plan_out, spread, *, width):
     reach = out.shape[0]
     t = lax.broadcasted_iota(jnp.int32, plan.shape, 0)
     k = lax.broadcasted_iota(jnp.int32, plan.shape, 2)
@@ -107,6 +112,11 @@
         for b in range(plan.shape[2]):
             copied = jnp.where((t == a) & (k == b), plan[a, 0, b], copied)
     plan_out[...] = copied
+    for p in range(2):
+        row = jnp.concatenate(
+            [weights[pl.ds(home[plan[0, 0, 2 * p + h]], 1), :] for h in range(2)], axis=1
+        )
+        spread[p] = jnp.broadcast_to(row, (tile, 2 * width))
     main, raw, _ = chunk_rows(reach, width)
     i, j = iotas(width)
     held = []
@@ -132,6 +142,7 @@
     plan, plan_ahead, plan_behind, ahead, behind, packed, own_high, own_low, out, high, low, *, width
 ):
     del packed, own_high, own_low
+    plan, plan_ahead, plan_behind = plan[...], plan_ahead[...], plan_behind[...]
     for s, snap, order, p in [(0, ahead, plan_ahead, 0), (3, behind, plan_behind, 1)]:
         parts = split(pair_of(snap, order, p, width))
         high[s] = parts[0]
@@ -220,23 +231,18 @@
     return dot3(q, split(dot3(split(gram), q, 1, 0)), 0, 0)
 
 
-def first_kernel(plan, home, weights, gathered, send, turned, spread, *, width):
+def first_kernel(spread, gathered, send, turned, *, width):
     tall = 2 * width
     grams, spreads = [], []
     for p in range(2):
         grams.append(unpack(gathered, p, width))
-        spreads.append(
-            jnp.concatenate(
-                [weights[pl.ds(home[plan[0, 0, 2 * p + h]], 1), :] for h in range(2)], axis=1
-            )
-        )
+        spreads.append(spread[p, :1, :])
     turns = rotations(grams, spreads)
     for p in range(2):
         q = half(turns[p], p)
         send[p, :tall, :] = q
         send[p, tall : tall + width, :] = own_gram(grams[p], split(q))
         send[p, tall + width :, :] = jnp.broadcast_to(half(spreads[p], p), (tile, width))
-        spread[p] = jnp.broadcast_to(half(spreads[p], 1 - p), (tile, width))
         turned[p] = half(turns[p], 1 - p)
 
 
@@ -246,7 +252,7 @@
         q = turned[p]
         keep[p, :tall, :] = q
         keep[p, tall : tall + width, :] = own_gram(unpack(gathered, p, width), split(q))
-        keep[p, tall + width :, :] = spread[p]
+        keep[p, tall + width :, :] = half(spread[p], 1 - p)
 
 
 def slot_value(s, received, keep, cut):
@@ -259,6 +265,7 @@
 ):
     tall = 2 * width
     rows = high.shape[1]
+    plan = plan[...]
     grams, spreads, fillers = [], [], []
 
     def filler(r, h, s, q):
@@ -384,27 +391,33 @@
     snap_ahead, snap_behind = both_ways(snapshot)
     plan_ahead, plan_behind = both_ways(plan)
     wide = pltpu.VMEM((4, rows, 2 * width), bf16)
-    packed, high, low, plan = call(
+    packed, high, low, plan, spread = call(
         pack_kernel,
-        [shape(reach, chunk, width), wide, wide, pltpu.VMEM(plan.shape, plan.dtype)],
-        [SMEM, VMEM],
+        [
+            shape(reach, chunk, width),
+            wide,
+            wide,
+            pltpu.VMEM(plan.shape, plan.dtype),
+            shape(2, tile, 2 * width),
+        ],
+        [SMEM, SMEM, VMEM, VMEM],
         width=width,
-    )(far(plan), far(snapshot))
+    )(far(plan), far(block_home), far(weights), far(snapshot))
     packed, high, low = call(
         raw_kernel,
         [shape(reach, chunk, width), wide, wide],
-        [SMEM] * 3 + [VMEM] * 5,
+        [VMEM] * 8,
         {5: 0, 6: 1, 7: 2},
         width=width,
-    )(plan, plan_ahead, plan_behind, near(snap_ahead), near(snap_behind), packed, high, low)
+    )(plan, near(plan_ahead), near(plan_behind), near(snap_ahead), near(snap_behind), packed, high, low)
     gathered = halved_total(packed)
     tall = 3 * width + tile
-    send, turned, spread = call(
+    send, turned = call(
         first_kernel,
-        [shape(2, tall, width), shape(2, 2 * width, width), shape(2, tile, width)],
-        [SMEM, SMEM, VMEM, VMEM],
+        [shape(2, tall, width), shape(2, 2 * width, width)],
+        [VMEM, VMEM],
         width=width,
-    )(plan, block_home, weights, gathered)
+    )(spread, gathered)
     received = exchange(send)
     keep = call(stay_kernel, shape(2, tall, width), [VMEM, VMEM, VMEM], width=width)(
         gathered, turned, spread
@@ -419,7 +432,7 @@
             block,
             block,
         ],
-        [SMEM] + [VMEM] * 5,
+        [VMEM] * 6,
         width=width,
     )(plan, keep, received, gathered, high, low)
     arrived = exchange(send)

time: 59.4 us -> 57.6 us (0.970)
  Pallas kernels: 14.9 us -> 13.2 us
    pallas_call x2, Pallas kernels: 5.94 us -> 4.83 us  [the longest x1 4.2 us: body(): call(first_kernel, [shape(2, tall, width), shape(2, 2 * width, width)], [...]
    pallas_call x1, Pallas kernels: 5.22 us -> 4.6 us  [body(): call(second_kernel, [shape(2, rows + tile, width), shape(2, 2 * width, wi...]
where the time goes in v7:
time: 57.6 us; the launch traced here: 57.4 us
  blocking collectives  33.9 us (59%)
  Pallas kernels  13.2 us (23%)
  waiting for transfers between devices  6.06 us (11%)
  starting transfers between devices  3.56 us (6%)
  between operations  0.7 us (1%)
    all_to_all x2, blocking collectives, swap(): lax.all_to_all(parts, 'row', 0, 0, tiled=True, axis_index_groups=groups)  33.9 us
    pallas_call x1, Pallas kernels, body(): call(second_kernel, [shape(2, rows + tile, width), shape(2, 2 * width, wi...  4.6 us
    pallas_call x1, Pallas kernels, body(): call(first_kernel, [shape(2, tall, width), shape(2, 2 * width, width)], [...  4.2 us
    ppermute x1, waiting for transfers between devices, halved_total(): lax.ppermute(here, 'row', [(i, (i + reach) % n) for i in range(n)])  4.07 us
    ppermute x1, starting transfers between devices, halved_total(): lax.ppermute(here, 'row', [(i, (i + reach) % n) for i in range(n)])  2.65 us
    ppermute x2, waiting for transfers between devices, exchange(): return near(lax.ppermute(send, 'pair', ahead))  1.87 us
    pallas_call x1, Pallas kernels, body(): call(pack_kernel, [shape(reach, chunk, width), wide, wide, pltpu.VMEM(pla...  1.54 us
  transfers between devices with their start and end apart: 5, of which 4 were waited for; matrix products, arithmetic and copies ran while one was open for 0% of the time, Pallas kernels for 5%

profile of v7, /device:TPU:0, one launch (start us, length us, event | category | flops | bytes accessed | tf_op | source)
XLA Modules:
  0.0 57.4 jit_solution(5385093682368692003)
XLA Ops:
  0.6 0.6 collective-permute-start.1
  1.2 0.1 collective-permute-start
  1.3 1.5 %pack_kernel.1 = (f32[8,200,128]{2,1,0:T(8,128)S(1)}, bf16[4,256,256]{2,1,0:T(8,128)(2,1)S(1)}, bf16[4,256,256]{2,1,0:T(8,128)(2,1)S(1)}, s32[2,1,4]{2,1,0:T(1,128)S(1)}, f32[2,8,256]{2,1,0:T(8,128)S(1)}) custom-call(s32[2,1,4]{2,1,0:T(1,128)} %refs_0_.1, s32[4]{0:T(128)} %refs_1_.1, f32[8,128]{1,0:T(8,128)} %refs_2_.1, f32[256,512]{1,0:T(8,128)} %refs_3_.1), custom_call_target="tpu_custom_call" | custom-call | tf_op jit(solution)/shard_map/pack_kernel/pallas_call | solution.py:394
  2.8 0.1 collective-permute-done.refs_1_.refs_2_
  2.9 0.0 collective-permute-done.1.refs_3_.refs_4_
  2.9 0.6 %raw_kernel.1 = (f32[8,200,128]{2,1,0:T(8,128)S(1)}, bf16[4,256,256]{2,1,0:T(8,128)(2,1)S(1)}, bf16[4,256,256]{2,1,0:T(8,128)(2,1)S(1)}) custom-call(s32[2,1,4]{2,1,0:T(1,128)S(1)} %get-tuple-element.19.refs_0_, s32[2,1,4]{2,1,0:T(1,128)S(1)} %collective-permute-done.refs_1_.refs_2_, ...), custom_call_target="tpu_custom_call", output_to_operand_aliasing={{0}: (5, {}), {1}: (6, {}), {2}: (7, {})} | custom-call | tf_op jit(solution)/shard_map/raw_kernel/pallas_call | solution.py:406
  3.6 19.1 %all_to_all.10.refs_0_ = f32[8,200,128]{2,1,0:T(8,128)S(1)} all-to-all(f32[8,200,128]{2,1,0:T(8,128)S(1)} %get-tuple-element.23), channel_id=1, replica_groups={{0,1,2,3,4,5,6,7},{8,9,10,11,12,13,14,15},{16,17,18,19,20,21,22,23},{24..., dimensions={0} | all-to-all | bytes 1638400 | tf_op jit(solution)/shard_map/all_to_all | solution.py:371
  22.7 2.7 %collective-permute-start.2 = (f32[200,128]{1,0:T(8,128)S(1)}, f32[200,128]{1,0:T(8,128)S(1)}, u32[]{:S(2)}, u32[]{:S(2)}) collective-permute-start(f32[200,128]{1,0:T(8,128)S(1)} %half_sum_kernel.1.refs_0_), channel_id=1, source_target_pairs={{0,8},{1,9},{2,10},{3,11},{4,12},{5,13},{6,14},{7,15},{8,0},{9,1},... | collective-permute-start | bytes 307208 | tf_op jit(solution)/shard_map/ppermute | solution.py:381
  25.4 4.1 %collective-permute-done.2.refs_1_ = f32[200,128]{1,0:T(8,128)S(1)} collective-permute-done((f32[200,128]{1,0:T(8,128)S(1)}, f32[200,128]{1,0:T(8,128)S(1)}, u32[]{:S(2)}, u32[]{:S(2)}) %collective-permute-start.2) | collective-permute-done | bytes 102432 | tf_op jit(solution)/shard_map/ppermute | solution.py:381
  29.4 0.1 join_kernel.1
  29.5 14.8 %all_to_all.11.refs_1_.refs_0_.refs_3_ = f32[8,200,128]{2,1,0:T(8,128)S(1)} all-to-all(f32[8,200,128]{2,1,0:T(8,128)S(1)} %join_kernel.1), channel_id=1, replica_groups={{0,1,2,3,4,5,6,7},{8,9,10,11,12,13,14,15},{16,17,18,19,20,21,22,23},{24..., dimensions={0} | all-to-all | bytes 1638400 | tf_op jit(solution)/shard_map/all_to_all | solution.py:371
  44.3 4.2 %first_kernel.1 = (f32[2,392,128]{2,1,0:T(8,128)S(1)}, f32[2,256,128]{2,1,0:T(8,128)S(1)}) custom-call(f32[2,8,256]{2,1,0:T(8,128)S(1)} %get-tuple-element.24.refs_0_.refs_2_, f32[8,200,128]{2,1,0:T(8,128)S(1)} %all_to_all.11.refs_1_.refs_0_.refs_3_), custom_call_target="tpu_custom_call" | custom-call | tf_op jit(solution)/shard_map/first_kernel/pallas_call | solution.py:415
  48.5 0.1 collective-permute-start.3
  48.6 0.9 %stay_kernel.1.refs_1_ = f32[2,392,128]{2,1,0:T(8,128)S(1)} custom-call(f32[8,200,128]{2,1,0:T(8,128)S(1)} %all_to_all.11.refs_1_.refs_0_.refs_3_, f32[2,256,128]{2,1,0:T(8,128)S(1)} %get-tuple-element.25.refs_1_, f32[2,8,256]{2,1,0:T(8,128)S(1)} %get-tuple-element.24.refs_0_.refs_2_), custom_call_target="tpu_custom_call" | custom-call | tf_op jit(solution)/shard_map/stay_kernel/pallas_call | solution.py:422
  49.5 0.8 %collective-permute-done.3.refs_2_ = f32[2,392,128]{2,1,0:T(8,128)S(1)} collective-permute-done((f32[2,392,128]{2,1,0:T(8,128)S(1)}, f32[2,392,128]{2,1,0:T(8,128)S(1)}, u32[]{:S(2)}, u32[]{:S(2)}) %collective-permute-start.3) | collective-permute-done | bytes 401440 | tf_op jit(solution)/shard_map/ppermute | solution.py:363
  50.3 4.6 %second_kernel.1 = (f32[2,264,128]{2,1,0:T(8,128)S(1)}, f32[2,256,128]{2,1,0:T(8,128)S(1)}, f32[2,8,128]{2,1,0:T(8,128)S(1)}, bf16[2,256,256]{2,1,0:T(8,128)(2,1)S(1)}, bf16[2,256,256]{2,1,0:T(8,128)(2,1)S(1)}) custom-call(s32[2,1,4]{2,1,0:T(1,128)S(1)} %get-tuple-element.19.refs_0_, f32[2,392,128]{2,1,0:T(8,128)S(1)} %stay_kernel.1.refs_1_, ...), custom_call_target="tpu_custom_call" | custom-call | tf_op jit(solution)/shard_map/second_kernel/pallas_call | solution.py:426
  54.9 0.2 collective-permute-start.4
  55.2 0.4 finish_kernel.1.refs_0_
  55.5 1.0 %collective-permute-done.4.refs_2_ = f32[2,264,128]{2,1,0:T(8,128)S(1)} collective-permute-done((f32[2,264,128]{2,1,0:T(8,128)S(1)}, f32[2,264,128]{2,1,0:T(8,128)S(1)}, u32[]{:S(2)}, u32[]{:S(2)}) %collective-permute-start.4) | collective-permute-done | bytes 270368 | tf_op jit(solution)/shard_map/ppermute | solution.py:363
  56.6 0.9 %last_kernel.1 = (f32[256,512]{1,0:T(8,128)}, f32[4,128]{1,0:T(4,128)}) custom-call(f32[2,256,128]{2,1,0:T(8,128)S(1)} %finish_kernel.1.refs_0_, f32[2,8,128]{2,1,0:T(8,128)S(1)} %get-tuple-element.32.refs_1_, f32[2,264,128]{2,1,0:T(8,128)S(1)} %collective-permute-done.4.refs_2_), custom_call_target="tpu_custom_call" | custom-call | tf_op jit(solution)/shard_map/last_kernel/pallas_call | solution.py:442
  (1 shorter events, 0.0 us)
Async XLA Ops:
  0.6 2.3 %collective-permute-start.1 = (f32[256,512]{1,0:T(8,128)}, f32[256,512]{1,0:T(8,128)S(1)}, u32[]{:S(2)}, u32[]{:S(2)}) collective-permute-start(f32[256,512]{1,0:T(8,128)} %refs_3_.1), channel_id=1, source_target_pairs={{16,0},{0,16},{17,1},{1,17},{18,2},{2,18},{19,3},{3,19},{20,4},{4,... | collective-permute-start | bytes 1572872 | tf_op jit(solution)/shard_map/ppermute | solution.py:356
  1.2 1.7 %collective-permute-start = (s32[2,1,4]{2,1,0:T(1,128)}, s32[2,1,4]{2,1,0:T(1,128)S(1)}, u32[]{:S(2)}, u32[]{:S(2)}) collective-permute-start(s32[2,1,4]{2,1,0:T(1,128)} %refs_0_.1), channel_id=1, source_target_pairs={{16,0},{0,16},{17,1},{1,17},{18,2},{2,18},{19,3},{3,19},{20,4},{4,... | collective-permute-start | bytes 104 | tf_op jit(solution)/shard_map/ppermute | solution.py:356
  22.7 6.7 %collective-permute-start.2 = (f32[200,128]{1,0:T(8,128)S(1)}, f32[200,128]{1,0:T(8,128)S(1)}, u32[]{:S(2)}, u32[]{:S(2)}) collective-permute-start(f32[200,128]{1,0:T(8,128)S(1)} %half_sum_kernel.1.refs_0_), channel_id=1, source_target_pairs={{0,8},{1,9},{2,10},{3,11},{4,12},{5,13},{6,14},{7,15},{8,0},{9,1},... | collective-permute-start | bytes 307208 | tf_op jit(solution)/shard_map/ppermute | solution.py:381
  48.5 1.8 %collective-permute-start.3 = (f32[2,392,128]{2,1,0:T(8,128)S(1)}, f32[2,392,128]{2,1,0:T(8,128)S(1)}, u32[]{:S(2)}, u32[]{:S(2)}) collective-permute-start(f32[2,392,128]{2,1,0:T(8,128)S(1)} %get-tuple-element.26), channel_id=1, source_target_pairs={{16,0},{0,16},{17,1},{1,17},{18,2},{2,18},{19,3},{3,19},{20,4},{4,... | collective-permute-start | bytes 1204232 | tf_op jit(solution)/shard_map/ppermute | solution.py:363
  54.9 1.6 %collective-permute-start.4 = (f32[2,264,128]{2,1,0:T(8,128)S(1)}, f32[2,264,128]{2,1,0:T(8,128)S(1)}, u32[]{:S(2)}, u32[]{:S(2)}) collective-permute-start(f32[2,264,128]{2,1,0:T(8,128)S(1)} %get-tuple-element.33), channel_id=1, source_target_pairs={{16,0},{0,16},{17,1},{1,17},{18,2},{2,18},{19,3},{3,19},{20,4},{4,... | collective-permute-start | bytes 811016 | tf_op jit(solution)/shard_map/ppermute | solution.py:363

commit v8 on v7

--- a/solution.py
+++ b/solution.py
@@ -375,10 +375,12 @@
 def halved_total(parts):
     n = lax.axis_size("row")
     reach = n // 2
-    groups = [list(range(reach)), list(range(reach, n))]
+    quarter = reach // 2
+    mirror = [(3 - i // quarter) * quarter + i % quarter for i in range(n)]
+    groups = [list(range(reach)), mirror[:reach]]
     mine = swap(parts, groups)
     here = call(half_sum_kernel, shape(*parts.shape[1:]), [VMEM])(mine)
-    there = near(lax.ppermute(here, "row", [(i, (i + reach) % n) for i in range(n)]))
+    there = near(lax.ppermute(here, "row", list(enumerate(mirror))))
     both = call(join_kernel, shape(*parts.shape), [VMEM, VMEM])(here, there)
     return swap(both, groups)
 

time: 57.6 us -> 56 us (0.972)
  blocking collectives: 33.9 us -> 32.3 us
    all_to_all x2, blocking collectives: 33.9 us -> 32.3 us  [swap(): lax.all_to_all(parts, 'row', 0, 0, tiled=True, axis_index_groups=groups)]
where the time goes in v8:
time: 56 us; the launch traced here: 55.7 us
  blocking collectives  32.3 us (58%)
  Pallas kernels  13.2 us (24%)
  waiting for transfers between devices  5.97 us (11%)
  starting transfers between devices  3.56 us (6%)
  between operations  0.7 us (1%)
    all_to_all x2, blocking collectives, swap(): lax.all_to_all(parts, 'row', 0, 0, tiled=True, axis_index_groups=groups)  32.3 us
    pallas_call x1, Pallas kernels, body(): call(second_kernel, [shape(2, rows + tile, width), shape(2, 2 * width, wi...  4.62 us
    pallas_call x1, Pallas kernels, body(): call(first_kernel, [shape(2, tall, width), shape(2, 2 * width, width)], [...  4.19 us
    ppermute x1, waiting for transfers between devices, halved_total(): there = near(lax.ppermute(here, 'row', list(enumerate(mirror))))  3.97 us
    ppermute x1, starting transfers between devices, halved_total(): there = near(lax.ppermute(here, 'row', list(enumerate(mirror))))  2.65 us
    ppermute x2, waiting for transfers between devices, exchange(): return near(lax.ppermute(send, 'pair', ahead))  1.87 us
    pallas_call x1, Pallas kernels, body(): call(pack_kernel, [shape(reach, chunk, width), wide, wide, pltpu.VMEM(pla...  1.54 us
  transfers between devices with their start and end apart: 5, of which 4 were waited for; matrix products, arithmetic and copies ran while one was open for 0% of the time, Pallas kernels for 5%

profile of v8, /device:TPU:0, one launch (start us, length us, event | category | flops | bytes accessed | tf_op | source)
XLA Modules:
  0.0 55.7 jit_solution(12611365938884405364)
XLA Ops:
  0.6 0.6 %collective-permute-start.1 = (f32[256,512]{1,0:T(8,128)}, f32[256,512]{1,0:T(8,128)S(1)}, u32[]{:S(2)}, u32[]{:S(2)}) collective-permute-start(f32[256,512]{1,0:T(8,128)} %refs_3_.1), channel_id=1, source_target_pairs={{16,0},{0,16},{17,1},{1,17},{18,2},{2,18},{19,3},{3,19},{20,4},{4,... | collective-permute-start | bytes 1572872 | tf_op jit(solution)/shard_map/ppermute | solution.py:356
  1.2 0.1 collective-permute-start
  1.3 1.5 %pack_kernel.1 = (f32[8,200,128]{2,1,0:T(8,128)S(1)}, bf16[4,256,256]{2,1,0:T(8,128)(2,1)S(1)}, bf16[4,256,256]{2,1,0:T(8,128)(2,1)S(1)}, s32[2,1,4]{2,1,0:T(1,128)S(1)}, f32[2,8,256]{2,1,0:T(8,128)S(1)}) custom-call(s32[2,1,4]{2,1,0:T(1,128)} %refs_0_.1, s32[4]{0:T(128)} %refs_1_.1, f32[8,128]{1,0:T(8,128)} %refs_2_.1, f32[256,512]{1,0:T(8,128)} %refs_3_.1), custom_call_target="tpu_custom_call" | custom-call | tf_op jit(solution)/shard_map/pack_kernel/pallas_call | solution.py:396
  2.8 0.1 collective-permute-done.refs_1_.refs_2_
  2.9 0.0 collective-permute-done.1.refs_3_.refs_4_
  2.9 0.6 %raw_kernel.1 = (f32[8,200,128]{2,1,0:T(8,128)S(1)}, bf16[4,256,256]{2,1,0:T(8,128)(2,1)S(1)}, bf16[4,256,256]{2,1,0:T(8,128)(2,1)S(1)}) custom-call(s32[2,1,4]{2,1,0:T(1,128)S(1)} %get-tuple-element.19.refs_0_, s32[2,1,4]{2,1,0:T(1,128)S(1)} %collective-permute-done.refs_1_.refs_2_, ...), custom_call_target="tpu_custom_call", output_to_operand_aliasing={{0}: (5, {}), {1}: (6, {}), {2}: (7, {})} | custom-call | tf_op jit(solution)/shard_map/raw_kernel/pallas_call | solution.py:408
  3.6 19.1 %all_to_all.10.refs_0_ = f32[8,200,128]{2,1,0:T(8,128)S(1)} all-to-all(f32[8,200,128]{2,1,0:T(8,128)S(1)} %get-tuple-element.23), channel_id=1, replica_groups={{0,1,2,3,4,5,6,7},{12,13,14,15,8,9,10,11},{16,17,18,19,20,21,22,23},{28..., dimensions={0} | all-to-all | bytes 1638400 | tf_op jit(solution)/shard_map/all_to_all | solution.py:371
  22.7 2.7 %collective-permute-start.2 = (f32[200,128]{1,0:T(8,128)S(1)}, f32[200,128]{1,0:T(8,128)S(1)}, u32[]{:S(2)}, u32[]{:S(2)}) collective-permute-start(f32[200,128]{1,0:T(8,128)S(1)} %half_sum_kernel.1.refs_0_), channel_id=1, source_target_pairs={{0,12},{1,13},{2,14},{3,15},{4,8},{5,9},{6,10},{7,11},{8,4},{9,5},... | collective-permute-start | bytes 307208 | tf_op jit(solution)/shard_map/ppermute | solution.py:383
  25.4 4.0 %collective-permute-done.2.refs_1_ = f32[200,128]{1,0:T(8,128)S(1)} collective-permute-done((f32[200,128]{1,0:T(8,128)S(1)}, f32[200,128]{1,0:T(8,128)S(1)}, u32[]{:S(2)}, u32[]{:S(2)}) %collective-permute-start.2) | collective-permute-done | bytes 102432 | tf_op jit(solution)/shard_map/ppermute | solution.py:383
  29.3 0.1 join_kernel.1
  29.4 13.2 %all_to_all.11.refs_1_.refs_0_.refs_3_ = f32[8,200,128]{2,1,0:T(8,128)S(1)} all-to-all(f32[8,200,128]{2,1,0:T(8,128)S(1)} %join_kernel.1), channel_id=1, replica_groups={{0,1,2,3,4,5,6,7},{12,13,14,15,8,9,10,11},{16,17,18,19,20,21,22,23},{28..., dimensions={0} | all-to-all | bytes 1638400 | tf_op jit(solution)/shard_map/all_to_all | solution.py:371
  42.6 4.2 %first_kernel.1 = (f32[2,392,128]{2,1,0:T(8,128)S(1)}, f32[2,256,128]{2,1,0:T(8,128)S(1)}) custom-call(f32[2,8,256]{2,1,0:T(8,128)S(1)} %get-tuple-element.24.refs_0_.refs_2_, f32[8,200,128]{2,1,0:T(8,128)S(1)} %all_to_all.11.refs_1_.refs_0_.refs_3_), custom_call_target="tpu_custom_call" | custom-call | tf_op jit(solution)/shard_map/first_kernel/pallas_call | solution.py:417
  46.8 0.1 collective-permute-start.3
  46.9 0.9 %stay_kernel.1.refs_1_ = f32[2,392,128]{2,1,0:T(8,128)S(1)} custom-call(f32[8,200,128]{2,1,0:T(8,128)S(1)} %all_to_all.11.refs_1_.refs_0_.refs_3_, f32[2,256,128]{2,1,0:T(8,128)S(1)} %get-tuple-element.25.refs_1_, f32[2,8,256]{2,1,0:T(8,128)S(1)} %get-tuple-element.24.refs_0_.refs_2_), custom_call_target="tpu_custom_call" | custom-call | tf_op jit(solution)/shard_map/stay_kernel/pallas_call | solution.py:424
  47.8 0.8 %collective-permute-done.3.refs_2_ = f32[2,392,128]{2,1,0:T(8,128)S(1)} collective-permute-done((f32[2,392,128]{2,1,0:T(8,128)S(1)}, f32[2,392,128]{2,1,0:T(8,128)S(1)}, u32[]{:S(2)}, u32[]{:S(2)}) %collective-permute-start.3) | collective-permute-done | bytes 401440 | tf_op jit(solution)/shard_map/ppermute | solution.py:363
  48.6 4.6 %second_kernel.1 = (f32[2,264,128]{2,1,0:T(8,128)S(1)}, f32[2,256,128]{2,1,0:T(8,128)S(1)}, f32[2,8,128]{2,1,0:T(8,128)S(1)}, bf16[2,256,256]{2,1,0:T(8,128)(2,1)S(1)}, bf16[2,256,256]{2,1,0:T(8,128)(2,1)S(1)}) custom-call(s32[2,1,4]{2,1,0:T(1,128)S(1)} %get-tuple-element.19.refs_0_, f32[2,392,128]{2,1,0:T(8,128)S(1)} %stay_kernel.1.refs_1_, ...), custom_call_target="tpu_custom_call" | custom-call | tf_op jit(solution)/shard_map/second_kernel/pallas_call | solution.py:428
  53.2 0.2 collective-permute-start.4
  53.4 0.4 finish_kernel.1.refs_0_
  53.8 1.1 %collective-permute-done.4.refs_2_ = f32[2,264,128]{2,1,0:T(8,128)S(1)} collective-permute-done((f32[2,264,128]{2,1,0:T(8,128)S(1)}, f32[2,264,128]{2,1,0:T(8,128)S(1)}, u32[]{:S(2)}, u32[]{:S(2)}) %collective-permute-start.4) | collective-permute-done | bytes 270368 | tf_op jit(solution)/shard_map/ppermute | solution.py:363
  54.9 0.9 %last_kernel.1 = (f32[256,512]{1,0:T(8,128)}, f32[4,128]{1,0:T(4,128)}) custom-call(f32[2,256,128]{2,1,0:T(8,128)S(1)} %finish_kernel.1.refs_0_, f32[2,8,128]{2,1,0:T(8,128)S(1)} %get-tuple-element.32.refs_1_, f32[2,264,128]{2,1,0:T(8,128)S(1)} %collective-permute-done.4.refs_2_), custom_call_target="tpu_custom_call" | custom-call | tf_op jit(solution)/shard_map/last_kernel/pallas_call | solution.py:444
  (1 shorter events, 0.0 us)
Async XLA Ops:
  0.6 2.3 %collective-permute-start.1 = (f32[256,512]{1,0:T(8,128)}, f32[256,512]{1,0:T(8,128)S(1)}, u32[]{:S(2)}, u32[]{:S(2)}) collective-permute-start(f32[256,512]{1,0:T(8,128)} %refs_3_.1), channel_id=1, source_target_pairs={{16,0},{0,16},{17,1},{1,17},{18,2},{2,18},{19,3},{3,19},{20,4},{4,... | collective-permute-start | bytes 1572872 | tf_op jit(solution)/shard_map/ppermute | solution.py:356
  1.2 1.7 %collective-permute-start = (s32[2,1,4]{2,1,0:T(1,128)}, s32[2,1,4]{2,1,0:T(1,128)S(1)}, u32[]{:S(2)}, u32[]{:S(2)}) collective-permute-start(s32[2,1,4]{2,1,0:T(1,128)} %refs_0_.1), channel_id=1, source_target_pairs={{16,0},{0,16},{17,1},{1,17},{18,2},{2,18},{19,3},{3,19},{20,4},{4,... | collective-permute-start | bytes 104 | tf_op jit(solution)/shard_map/ppermute | solution.py:356
  22.7 6.6 %collective-permute-start.2 = (f32[200,128]{1,0:T(8,128)S(1)}, f32[200,128]{1,0:T(8,128)S(1)}, u32[]{:S(2)}, u32[]{:S(2)}) collective-permute-start(f32[200,128]{1,0:T(8,128)S(1)} %half_sum_kernel.1.refs_0_), channel_id=1, source_target_pairs={{0,12},{1,13},{2,14},{3,15},{4,8},{5,9},{6,10},{7,11},{8,4},{9,5},... | collective-permute-start | bytes 307208 | tf_op jit(solution)/shard_map/ppermute | solution.py:383
  46.8 1.8 %collective-permute-start.3 = (f32[2,392,128]{2,1,0:T(8,128)S(1)}, f32[2,392,128]{2,1,0:T(8,128)S(1)}, u32[]{:S(2)}, u32[]{:S(2)}) collective-permute-start(f32[2,392,128]{2,1,0:T(8,128)S(1)} %get-tuple-element.26), channel_id=1, source_target_pairs={{16,0},{0,16},{17,1},{1,17},{18,2},{2,18},{19,3},{3,19},{20,4},{4,... | collective-permute-start | bytes 1204232 | tf_op jit(solution)/shard_map/ppermute | solution.py:363
  53.2 1.6 %collective-permute-start.4 = (f32[2,264,128]{2,1,0:T(8,128)S(1)}, f32[2,264,128]{2,1,0:T(8,128)S(1)}, u32[]{:S(2)}, u32[]{:S(2)}) collective-permute-start(f32[2,264,128]{2,1,0:T(8,128)S(1)} %get-tuple-element.33), channel_id=1, source_target_pairs={{16,0},{0,16},{17,1},{1,17},{18,2},{2,18},{19,3},{3,19},{20,4},{4,... | collective-permute-start | bytes 811016 | tf_op jit(solution)/shard_map/ppermute | solution.py:363

commit v9 on v8

--- a/solution.py
+++ b/solution.py
@@ -52,8 +52,8 @@
     i, j = iotas(n)
     same = i == j
     held = jnp.where(same, gram, 0.0)
-    inv_row = lax.rsqrt(jnp.sum(held, axis=0, keepdims=True) + epsilon)
-    inv_col = lax.rsqrt(jnp.sum(held, axis=1, keepdims=True) + epsilon)
+    inv_row = lax.rsqrt(jnp.maximum(jnp.sum(held, axis=0, keepdims=True), 0.0) + epsilon)
+    inv_col = lax.rsqrt(jnp.maximum(jnp.sum(held, axis=1, keepdims=True), 0.0) + epsilon)
     corr = gram * inv_col * inv_row
     skew = step_size * corr * (column(row_weight) - row_weight)
     bound = 1.0 + jnp.max(jnp.sum(jnp.abs(skew), axis=0, keepdims=True), axis=1, keepdims=True)
@@ -246,9 +246,10 @@
         turned[p] = half(turns[p], 1 - p)
 
 
-def stay_kernel(gathered, turned, spread, keep, *, width):
+def stay_kernel(gathered, turned, spread, keep, raw_high, raw_low, *, width):
     tall = 2 * width
     for p in range(2):
+        raw_high[p], raw_low[p] = split(unpack_raw(gathered, p, width))
         q = turned[p]
         keep[p, :tall, :] = q
         keep[p, tall : tall + width, :] = own_gram(unpack(gathered, p, width), split(q))
@@ -261,7 +262,20 @@
 
 
 def second_kernel(
-    plan, keep, received, gathered, high, low, send, turned, norms, block_high, block_low, *, width
+    plan,
+    keep,
+    received,
+    raw_high,
+    raw_low,
+    high,
+    low,
+    send,
+    turned,
+    held,
+    block_high,
+    block_low,
+    *,
+    width,
 ):
     tall = 2 * width
     rows = high.shape[1]
@@ -280,7 +294,7 @@
     for r in range(2):
         order = [plan[1, 0, 2 * r + h] for h in range(2)]
         first, second = [split(slot_value(s, received, keep, slice(0, tall))) for s in order]
-        moved = dot3(split(unpack_raw(gathered, r, width)), first, 1, 0)
+        moved = dot3((raw_high[r], raw_low[r]), first, 1, 0)
         flipped = dot3(second, split(moved), 0, 0)
         own = [slot_value(s, received, keep, slice(tall, tall + width)) for s in order]
         grams.append(whole(own[0], jnp.transpose(flipped), flipped, own[1]))
@@ -291,21 +305,22 @@
         fillers += [filler(r, h, s, q) for h, (s, q) in enumerate(zip(order, (first, second)))]
     turns = rotations(grams, spreads, fillers)
     for p in range(2):
-        q = split(turns[p])
-        send[p, :rows, :] = dot3(
-            (block_high[p], block_low[p]), [half(x, p) for x in q], 1, 0
-        )
-        moved = dot3(split(grams[p]), q, 1, 0)
-        squares = jnp.sum(turns[p] * moved, axis=0, keepdims=True)
-        lengths = jnp.sqrt(squares)
-        send[p, rows:, :] = jnp.broadcast_to(half(lengths, p), (tile, width))
-        norms[p] = jnp.broadcast_to(half(lengths, 1 - p), (tile, width))
+        turn = half(turns[p], p)
+        send[p, :rows, :] = dot3((block_high[p], block_low[p]), split(turn), 1, 0)
+        send[p, rows:, :] = lengths(grams[p], turn)
+        held[p] = grams[p]
         turned[p] = half(turns[p], 1 - p)
 
 
-def finish_kernel(high, low, turned, kept):
+def lengths(gram, turn):
+    squares = jnp.sum(turn * dot3(split(gram), split(turn), 1, 0), axis=0, keepdims=True)
+    return jnp.broadcast_to(jnp.sqrt(jnp.maximum(squares, 0.0)), (tile, turn.shape[1]))
+
+
+def finish_kernel(high, low, turned, grams, kept, norms):
     for p in range(2):
         kept[p] = dot3((high[p], low[p]), split(turned[p]), 1, 0)
+        norms[p] = lengths(grams[p], turned[p])
 
 
 def last_kernel(kept, norms_here, received, final, norms):
@@ -421,26 +436,27 @@
         width=width,
     )(spread, gathered)
     received = exchange(send)
-    keep = call(stay_kernel, shape(2, tall, width), [VMEM, VMEM, VMEM], width=width)(
-        gathered, turned, spread
-    )
+    square = pltpu.VMEM((2, 2 * width, 2 * width), bf16)
+    keep, raw_high, raw_low = call(
+        stay_kernel, [shape(2, tall, width), square, square], [VMEM, VMEM, VMEM], width=width
+    )(gathered, turned, spread)
     block = pltpu.VMEM((2, rows, 2 * width), bf16)
-    send, turned, norms, block_high, block_low = call(
+    send, turned, held, block_high, block_low = call(
         second_kernel,
         [
             shape(2, rows + tile, width),
             shape(2, 2 * width, width),
-            shape(2, tile, width),
+            shape(2, 2 * width, 2 * width),
             block,
             block,
         ],
-        [VMEM] * 6,
+        [VMEM] * 7,
         width=width,
-    )(plan, keep, received, gathered, high, low)
+    )(plan, keep, received, raw_high, raw_low, high, low)
     arrived = exchange(send)
-    kept = call(finish_kernel, shape(2, rows, width), [VMEM, VMEM, VMEM])(
-        block_high, block_low, turned
-    )
+    kept, norms = call(
+        finish_kernel, [shape(2, rows, width), shape(2, tile, width)], [VMEM] * 4
+    )(block_high, block_low, turned, held)
     final, norms = call(
         last_kernel,
         [jax.ShapeDtypeStruct((rows, 4 * width), f32), jax.ShapeDtypeStruct((4, width), f32)],

time: 56 us -> 55.9 us (level)
  no operation moved by 1% of the time
where the time goes in v9:
time: 55.9 us; the launch traced here: 55.6 us
  blocking collectives  32.3 us (58%)
  Pallas kernels  13.3 us (24%)
  waiting for transfers between devices  5.71 us (10%)
  starting transfers between devices  3.57 us (6%)
  between operations  0.68 us (1%)
    all_to_all x2, blocking collectives, swap(): lax.all_to_all(parts, 'row', 0, 0, tiled=True, axis_index_groups=groups)  32.3 us
    pallas_call x1, Pallas kernels, body(): call(second_kernel, [shape(2, rows + tile, width), shape(2, 2 * width, wi...  4.51 us
    pallas_call x1, Pallas kernels, body(): call(first_kernel, [shape(2, tall, width), shape(2, 2 * width, width)], [...  4.2 us
    ppermute x1, waiting for transfers between devices, halved_total(): there = near(lax.ppermute(here, 'row', list(enumerate(mirror))))  3.97 us
    ppermute x1, starting transfers between devices, halved_total(): there = near(lax.ppermute(here, 'row', list(enumerate(mirror))))  2.65 us
    ppermute x2, waiting for transfers between devices, exchange(): return near(lax.ppermute(send, 'pair', ahead))  1.61 us
    pallas_call x1, Pallas kernels, body(): call(pack_kernel, [shape(reach, chunk, width), wide, wide, pltpu.VMEM(pla...  1.54 us
  transfers between devices with their start and end apart: 5, of which 4 were waited for; matrix products, arithmetic and copies ran while one was open for 0% of the time, Pallas kernels for 5%

profile of v9, /device:TPU:0, one launch (start us, length us, event | category | flops | bytes accessed | tf_op | source)
XLA Modules:
  0.0 55.6 jit_solution(13836167212020107857)
XLA Ops:
  0.6 0.6 %collective-permute-start.1 = (f32[256,512]{1,0:T(8,128)}, f32[256,512]{1,0:T(8,128)S(1)}, u32[]{:S(2)}, u32[]{:S(2)}) collective-permute-start(f32[256,512]{1,0:T(8,128)} %refs_3_.1), channel_id=1, source_target_pairs={{16,0},{0,16},{17,1},{1,17},{18,2},{2,18},{19,3},{3,19},{20,4},{4,... | collective-permute-start | bytes 1572872 | tf_op jit(solution)/shard_map/ppermute | solution.py:371
  1.2 0.1 collective-permute-start
  1.3 1.5 %pack_kernel.1 = (f32[8,200,128]{2,1,0:T(8,128)S(1)}, bf16[4,256,256]{2,1,0:T(8,128)(2,1)S(1)}, bf16[4,256,256]{2,1,0:T(8,128)(2,1)S(1)}, s32[2,1,4]{2,1,0:T(1,128)S(1)}, f32[2,8,256]{2,1,0:T(8,128)S(1)}) custom-call(s32[2,1,4]{2,1,0:T(1,128)} %refs_0_.1, s32[4]{0:T(128)} %refs_1_.1, f32[8,128]{1,0:T(8,128)} %refs_2_.1, f32[256,512]{1,0:T(8,128)} %refs_3_.1), custom_call_target="tpu_custom_call" | custom-call | tf_op jit(solution)/shard_map/pack_kernel/pallas_call | solution.py:411
  2.8 0.1 collective-permute-done.refs_1_.refs_2_
  2.9 0.0 collective-permute-done.1.refs_3_.refs_4_
  2.9 0.6 %raw_kernel.1 = (f32[8,200,128]{2,1,0:T(8,128)S(1)}, bf16[4,256,256]{2,1,0:T(8,128)(2,1)S(1)}, bf16[4,256,256]{2,1,0:T(8,128)(2,1)S(1)}) custom-call(s32[2,1,4]{2,1,0:T(1,128)S(1)} %get-tuple-element.24.refs_0_, s32[2,1,4]{2,1,0:T(1,128)S(1)} %collective-permute-done.refs_1_.refs_2_, ...), custom_call_target="tpu_custom_call", output_to_operand_aliasing={{0}: (5, {}), {1}: (6, {}), {2}: (7, {})} | custom-call | tf_op jit(solution)/shard_map/raw_kernel/pallas_call | solution.py:423
  3.6 19.1 %all_to_all.10.refs_0_ = f32[8,200,128]{2,1,0:T(8,128)S(1)} all-to-all(f32[8,200,128]{2,1,0:T(8,128)S(1)} %get-tuple-element.28), channel_id=1, replica_groups={{0,1,2,3,4,5,6,7},{12,13,14,15,8,9,10,11},{16,17,18,19,20,21,22,23},{28..., dimensions={0} | all-to-all | bytes 1638400 | tf_op jit(solution)/shard_map/all_to_all | solution.py:386
  22.7 2.7 %collective-permute-start.2 = (f32[200,128]{1,0:T(8,128)S(1)}, f32[200,128]{1,0:T(8,128)S(1)}, u32[]{:S(2)}, u32[]{:S(2)}) collective-permute-start(f32[200,128]{1,0:T(8,128)S(1)} %half_sum_kernel.1.refs_0_), channel_id=1, source_target_pairs={{0,12},{1,13},{2,14},{3,15},{4,8},{5,9},{6,10},{7,11},{8,4},{9,5},... | collective-permute-start | bytes 307208 | tf_op jit(solution)/shard_map/ppermute | solution.py:398
  25.4 4.0 %collective-permute-done.2.refs_1_ = f32[200,128]{1,0:T(8,128)S(1)} collective-permute-done((f32[200,128]{1,0:T(8,128)S(1)}, f32[200,128]{1,0:T(8,128)S(1)}, u32[]{:S(2)}, u32[]{:S(2)}) %collective-permute-start.2) | collective-permute-done | bytes 102432 | tf_op jit(solution)/shard_map/ppermute | solution.py:398
  29.3 0.1 join_kernel.1
  29.4 13.2 %all_to_all.11.refs_1_.refs_0_ = f32[8,200,128]{2,1,0:T(8,128)S(1)} all-to-all(f32[8,200,128]{2,1,0:T(8,128)S(1)} %join_kernel.1), channel_id=1, replica_groups={{0,1,2,3,4,5,6,7},{12,13,14,15,8,9,10,11},{16,17,18,19,20,21,22,23},{28..., dimensions={0} | all-to-all | bytes 1638400 | tf_op jit(solution)/shard_map/all_to_all | solution.py:386
  42.6 4.2 %first_kernel.1 = (f32[2,392,128]{2,1,0:T(8,128)S(1)}, f32[2,256,128]{2,1,0:T(8,128)S(1)}) custom-call(f32[2,8,256]{2,1,0:T(8,128)S(1)} %get-tuple-element.29.refs_0_.refs_2_, f32[8,200,128]{2,1,0:T(8,128)S(1)} %all_to_all.11.refs_1_.refs_0_), custom_call_target="tpu_custom_call" | custom-call | tf_op jit(solution)/shard_map/first_kernel/pallas_call | solution.py:432
  46.8 0.1 collective-permute-start.3
  46.9 0.9 %stay_kernel.1 = (f32[2,392,128]{2,1,0:T(8,128)S(1)}, bf16[2,256,256]{2,1,0:T(8,128)(2,1)S(1)}, bf16[2,256,256]{2,1,0:T(8,128)(2,1)S(1)}) custom-call(f32[8,200,128]{2,1,0:T(8,128)S(1)} %all_to_all.11.refs_1_.refs_0_, f32[2,256,128]{2,1,0:T(8,128)S(1)} %get-tuple-element.30.refs_1_, f32[2,8,256]{2,1,0:T(8,128)S(1)} %get-tuple-element.29.refs_0_.refs_2_), custom_call_target="tpu_custom_call" | custom-call | tf_op jit(solution)/shard_map/stay_kernel/pallas_call | solution.py:440
  47.8 0.8 %collective-permute-done.3.refs_2_ = f32[2,392,128]{2,1,0:T(8,128)S(1)} collective-permute-done((f32[2,392,128]{2,1,0:T(8,128)S(1)}, f32[2,392,128]{2,1,0:T(8,128)S(1)}, u32[]{:S(2)}, u32[]{:S(2)}) %collective-permute-start.3) | collective-permute-done | bytes 401440 | tf_op jit(solution)/shard_map/ppermute | solution.py:378
  48.6 4.5 %second_kernel.1 = (f32[2,264,128]{2,1,0:T(8,128)S(1)}, f32[2,256,128]{2,1,0:T(8,128)S(1)}, f32[2,256,256]{2,1,0:T(8,128)S(1)}, bf16[2,256,256]{2,1,0:T(8,128)(2,1)S(1)}, bf16[2,256,256]{2,1,0:T(8,128)(2,1)S(1)}) custom-call(s32[2,1,4]{2,1,0:T(1,128)S(1)} %get-tuple-element.24.refs_0_, f32[2,392,128]{2,1,0:T(8,128)S(1)} %get-tuple-element.31.refs_1_, ...), custom_call_target="tpu_custom_call" | custom-call | tf_op jit(solution)/shard_map/second_kernel/pallas_call | solution.py:444
  53.1 0.2 collective-permute-start.4
  53.3 0.6 %finish_kernel.1 = (f32[2,256,128]{2,1,0:T(8,128)S(1)}, f32[2,8,128]{2,1,0:T(8,128)S(1)}) custom-call(bf16[2,256,256]{2,1,0:T(8,128)(2,1)S(1)} %get-tuple-element.37.refs_0_, bf16[2,256,256]{2,1,0:T(8,128)(2,1)S(1)} %get-tuple-element.38.refs_1_, f32[2,256,128]{2,1,0:T(8,128)S(1)} %get-tuple-element.39.refs_2_, f32[2,256,256]{2,1,0:T(8,128)S(1)} %get-tuple-element.40.refs_3_), custom_call_target="tpu_custom_call" | custom-call | tf_op jit(solution)/shard_map/finish_kernel/pallas_call | solution.py:457
  53.9 0.8 %collective-permute-done.4.refs_2_ = f32[2,264,128]{2,1,0:T(8,128)S(1)} collective-permute-done((f32[2,264,128]{2,1,0:T(8,128)S(1)}, f32[2,264,128]{2,1,0:T(8,128)S(1)}, u32[]{:S(2)}, u32[]{:S(2)}) %collective-permute-start.4) | collective-permute-done | bytes 270368 | tf_op jit(solution)/shard_map/ppermute | solution.py:378
  54.7 0.9 %last_kernel.1 = (f32[256,512]{1,0:T(8,128)}, f32[4,128]{1,0:T(4,128)}) custom-call(f32[2,256,128]{2,1,0:T(8,128)S(1)} %get-tuple-element.41.refs_0_, f32[2,8,128]{2,1,0:T(8,128)S(1)} %get-tuple-element.42.refs_1_, f32[2,264,128]{2,1,0:T(8,128)S(1)} %collective-permute-done.4.refs_2_), custom_call_target="tpu_custom_call" | custom-call | tf_op jit(solution)/shard_map/last_kernel/pallas_call | solution.py:460
  (1 shorter events, 0.0 us)
Async XLA Ops:
  0.6 2.3 %collective-permute-start.1 = (f32[256,512]{1,0:T(8,128)}, f32[256,512]{1,0:T(8,128)S(1)}, u32[]{:S(2)}, u32[]{:S(2)}) collective-permute-start(f32[256,512]{1,0:T(8,128)} %refs_3_.1), channel_id=1, source_target_pairs={{16,0},{0,16},{17,1},{1,17},{18,2},{2,18},{19,3},{3,19},{20,4},{4,... | collective-permute-start | bytes 1572872 | tf_op jit(solution)/shard_map/ppermute | solution.py:371
  1.2 1.7 %collective-permute-start = (s32[2,1,4]{2,1,0:T(1,128)}, s32[2,1,4]{2,1,0:T(1,128)S(1)}, u32[]{:S(2)}, u32[]{:S(2)}) collective-permute-start(s32[2,1,4]{2,1,0:T(1,128)} %refs_0_.1), channel_id=1, source_target_pairs={{16,0},{0,16},{17,1},{1,17},{18,2},{2,18},{19,3},{3,19},{20,4},{4,... | collective-permute-start | bytes 104 | tf_op jit(solution)/shard_map/ppermute | solution.py:371
  22.7 6.6 %collective-permute-start.2 = (f32[200,128]{1,0:T(8,128)S(1)}, f32[200,128]{1,0:T(8,128)S(1)}, u32[]{:S(2)}, u32[]{:S(2)}) collective-permute-start(f32[200,128]{1,0:T(8,128)S(1)} %half_sum_kernel.1.refs_0_), channel_id=1, source_target_pairs={{0,12},{1,13},{2,14},{3,15},{4,8},{5,9},{6,10},{7,11},{8,4},{9,5},... | collective-permute-start | bytes 307208 | tf_op jit(solution)/shard_map/ppermute | solution.py:398
  46.8 1.8 %collective-permute-start.3 = (f32[2,392,128]{2,1,0:T(8,128)S(1)}, f32[2,392,128]{2,1,0:T(8,128)S(1)}, u32[]{:S(2)}, u32[]{:S(2)}) collective-permute-start(f32[2,392,128]{2,1,0:T(8,128)S(1)} %get-tuple-element.32), channel_id=1, source_target_pairs={{16,0},{0,16},{17,1},{1,17},{18,2},{2,18},{19,3},{3,19},{20,4},{4,... | collective-permute-start | bytes 1204232 | tf_op jit(solution)/shard_map/ppermute | solution.py:378
  53.1 1.6 %collective-permute-start.4 = (f32[2,264,128]{2,1,0:T(8,128)S(1)}, f32[2,264,128]{2,1,0:T(8,128)S(1)}, u32[]{:S(2)}, u32[]{:S(2)}) collective-permute-start(f32[2,264,128]{2,1,0:T(8,128)S(1)} %get-tuple-element.43), channel_id=1, source_target_pairs={{16,0},{0,16},{17,1},{1,17},{18,2},{2,18},{19,3},{3,19},{20,4},{4,... | collective-permute-start | bytes 811016 | tf_op jit(solution)/shard_map/ppermute | solution.py:378

commit v10 on v9

--- a/solution.py
+++ b/solution.py
@@ -47,7 +47,11 @@
     return jnp.transpose(jnp.broadcast_to(row, (n, n)))
 
 
-def start_rotation(gram, row_weight):
+def difference(row_weight):
+    return step_size * (column(row_weight) - row_weight)
+
+
+def start_rotation(gram, apart):
     n = gram.shape[0]
     i, j = iotas(n)
     same = i == j
@@ -55,18 +59,18 @@
     inv_row = lax.rsqrt(jnp.maximum(jnp.sum(held, axis=0, keepdims=True), 0.0) + epsilon)
     inv_col = lax.rsqrt(jnp.maximum(jnp.sum(held, axis=1, keepdims=True), 0.0) + epsilon)
     corr = gram * inv_col * inv_row
-    skew = step_size * corr * (column(row_weight) - row_weight)
+    skew = corr * apart
     bound = 1.0 + jnp.max(jnp.sum(jnp.abs(skew), axis=0, keepdims=True), axis=1, keepdims=True)
     return jnp.where(same, 1.0, 0.0) + skew * (1.0 / bound)
 
 
-def rotations(grams, row_weights, fillers=()):
+def rotations(grams, aparts, fillers=()):
     n = grams[0].shape[0]
     i, j = iotas(n)
     same = i == j
     diag15 = jnp.where(same, 1.5, 0.0)
     diag05 = jnp.where(same, 0.5, 0.0)
-    current = [start_rotation(g, w) for g, w in zip(grams, row_weights)]
+    current = [start_rotation(g, a) for g, a in zip(grams, aparts)]
     for turn in range(newton_turns - 1):
         parts = [split(x) for x in current]
         inner = [outer(p) for p in parts]
@@ -176,7 +180,8 @@
     out[...] = added([parts[c] for c in range(parts.shape[0])])
 
 
-def join_kernel(here, there, out):
+def join_kernel(here, there, aparts, out):
+    del aparts
     value = here[...] + there[...]
     for c in range(out.shape[0]):
         out[c] = value
@@ -231,13 +236,19 @@
     return dot3(q, split(dot3(split(gram), q, 1, 0)), 0, 0)
 
 
-def first_kernel(spread, gathered, send, turned, *, width):
+def apart_kernel(spread, sums, out):
+    del sums
+    for p in range(2):
+        out[p] = difference(spread[p, :1, :])
+
+
+def first_kernel(spread, aparts, gathered, send, turned, *, width):
     tall = 2 * width
     grams, spreads = [], []
     for p in range(2):
         grams.append(unpack(gathered, p, width))
         spreads.append(spread[p, :1, :])
-    turns = rotations(grams, spreads)
+    turns = rotations(grams, [aparts[p] for p in range(2)])
     for p in range(2):
         q = half(turns[p], p)
         send[p, :tall, :] = q
@@ -303,7 +314,7 @@
         ]
         spreads.append(jnp.concatenate(wide, axis=1))
         fillers += [filler(r, h, s, q) for h, (s, q) in enumerate(zip(order, (first, second)))]
-    turns = rotations(grams, spreads, fillers)
+    turns = rotations(grams, [difference(w) for w in spreads], fillers)
     for p in range(2):
         turn = half(turns[p], p)
         send[p, :rows, :] = dot3((block_high[p], block_low[p]), split(turn), 1, 0)
@@ -387,17 +398,19 @@
     )
 
 
-def halved_total(parts):
+def halved_total(parts, spread):
     n = lax.axis_size("row")
-    reach = n // 2
+    reach, width = n // 2, parts.shape[2]
     quarter = reach // 2
     mirror = [(3 - i // quarter) * quarter + i % quarter for i in range(n)]
     groups = [list(range(reach)), mirror[:reach]]
     mine = swap(parts, groups)
     here = call(half_sum_kernel, shape(*parts.shape[1:]), [VMEM])(mine)
     there = near(lax.ppermute(here, "row", list(enumerate(mirror))))
-    both = call(join_kernel, shape(*parts.shape), [VMEM, VMEM])(here, there)
-    return swap(both, groups)
+    side = 2 * width
+    aparts = call(apart_kernel, shape(2, side, side), [VMEM, VMEM])(spread, here)
+    both = call(join_kernel, shape(*parts.shape), [VMEM] * 3)(here, there, aparts)
+    return swap(both, groups), aparts
 
 
 def body(snapshot, weights, block_home, plan):
@@ -427,14 +440,14 @@
         {5: 0, 6: 1, 7: 2},
         width=width,
     )(plan, near(plan_ahead), near(plan_behind), near(snap_ahead), near(snap_behind), packed, high, low)
-    gathered = halved_total(packed)
+    gathered, aparts = halved_total(packed, spread)
     tall = 3 * width + tile
     send, turned = call(
         first_kernel,
         [shape(2, tall, width), shape(2, 2 * width, width)],
-        [VMEM, VMEM],
+        [VMEM, VMEM, VMEM],
         width=width,
-    )(spread, gathered)
+    )(spread, aparts, gathered)
     received = exchange(send)
     square = pltpu.VMEM((2, 2 * width, 2 * width), bf16)
     keep, raw_high, raw_low = call(

time: 55.9 us -> 55.8 us (level)
  transfers between devices with their start and end apart: 5 -> 5, of which waited for: 4 -> 4; matrix products, arithmetic and copies ran while one was open for 0% -> 0% of each run, Pallas kernels for 5% -> 6%
where the time goes in v10:
time: 55.8 us; the launch traced here: 55.6 us
  blocking collectives  32.3 us (58%)
  Pallas kernels  13.4 us (24%)
  waiting for transfers between devices  5.58 us (10%)
  starting transfers between devices  3.56 us (6%)
  between operations  0.69 us (1%)
    all_to_all x2, blocking collectives, swap(): lax.all_to_all(parts, 'row', 0, 0, tiled=True, axis_index_groups=groups)  32.3 us
    pallas_call x1, Pallas kernels, body(): call(second_kernel, [shape(2, rows + tile, width), shape(2, 2 * width, wi...  4.51 us
    pallas_call x1, Pallas kernels, body(): call(first_kernel, [shape(2, tall, width), shape(2, 2 * width, width)], [...  4.16 us
    ppermute x1, waiting for transfers between devices, halved_total(): there = near(lax.ppermute(here, 'row', list(enumerate(mirror))))  3.83 us
    ppermute x1, starting transfers between devices, halved_total(): there = near(lax.ppermute(here, 'row', list(enumerate(mirror))))  2.65 us
    ppermute x2, waiting for transfers between devices, exchange(): return near(lax.ppermute(send, 'pair', ahead))  1.62 us
    pallas_call x1, Pallas kernels, body(): call(pack_kernel, [shape(reach, chunk, width), wide, wide, pltpu.VMEM(pla...  1.54 us
  transfers between devices with their start and end apart: 5, of which 4 were waited for; matrix products, arithmetic and copies ran while one was open for 0% of the time, Pallas kernels for 6%

profile of v10, /device:TPU:0, one launch (start us, length us, event | category | flops | bytes accessed | tf_op | source)
XLA Modules:
  0.0 55.6 jit_solution(6375775579392870004)
XLA Ops:
  0.6 0.6 %collective-permute-start.1 = (f32[256,512]{1,0:T(8,128)}, f32[256,512]{1,0:T(8,128)S(1)}, u32[]{:S(2)}, u32[]{:S(2)}) collective-permute-start(f32[256,512]{1,0:T(8,128)} %refs_3_.1), channel_id=1, source_target_pairs={{16,0},{0,16},{17,1},{1,17},{18,2},{2,18},{19,3},{3,19},{20,4},{4,... | collective-permute-start | bytes 1572872 | tf_op jit(solution)/shard_map/ppermute | solution.py:382
  1.2 0.1 collective-permute-start
  1.3 1.5 %pack_kernel.1 = (f32[8,200,128]{2,1,0:T(8,128)S(1)}, bf16[4,256,256]{2,1,0:T(8,128)(2,1)S(1)}, bf16[4,256,256]{2,1,0:T(8,128)(2,1)S(1)}, s32[2,1,4]{2,1,0:T(1,128)S(1)}, f32[2,8,256]{2,1,0:T(8,128)S(1)}) custom-call(s32[2,1,4]{2,1,0:T(1,128)} %refs_0_.1, s32[4]{0:T(128)} %refs_1_.1, f32[8,128]{1,0:T(8,128)} %refs_2_.1, f32[256,512]{1,0:T(8,128)} %refs_3_.1), custom_call_target="tpu_custom_call" | custom-call | tf_op jit(solution)/shard_map/pack_kernel/pallas_call | solution.py:424
  2.8 0.1 collective-permute-done.refs_1_.refs_2_
  2.9 0.0 collective-permute-done.1.refs_3_.refs_4_
  2.9 0.6 %raw_kernel.1 = (f32[8,200,128]{2,1,0:T(8,128)S(1)}, bf16[4,256,256]{2,1,0:T(8,128)(2,1)S(1)}, bf16[4,256,256]{2,1,0:T(8,128)(2,1)S(1)}) custom-call(s32[2,1,4]{2,1,0:T(1,128)S(1)} %get-tuple-element.24.refs_0_, s32[2,1,4]{2,1,0:T(1,128)S(1)} %collective-permute-done.refs_1_.refs_2_, ...), custom_call_target="tpu_custom_call", output_to_operand_aliasing={{0}: (5, {}), {1}: (6, {}), {2}: (7, {})} | custom-call | tf_op jit(solution)/shard_map/raw_kernel/pallas_call | solution.py:436
  3.6 19.1 %all_to_all.10.refs_0_ = f32[8,200,128]{2,1,0:T(8,128)S(1)} all-to-all(f32[8,200,128]{2,1,0:T(8,128)S(1)} %get-tuple-element.28), channel_id=1, replica_groups={{0,1,2,3,4,5,6,7},{12,13,14,15,8,9,10,11},{16,17,18,19,20,21,22,23},{28..., dimensions={0} | all-to-all | bytes 1638400 | tf_op jit(solution)/shard_map/all_to_all | solution.py:397
  22.7 2.7 %collective-permute-start.2 = (f32[200,128]{1,0:T(8,128)S(1)}, f32[200,128]{1,0:T(8,128)S(1)}, u32[]{:S(2)}, u32[]{:S(2)}) collective-permute-start(f32[200,128]{1,0:T(8,128)S(1)} %half_sum_kernel.1.refs_1_.refs_0_), channel_id=1, source_target_pairs={{0,12},{1,13},{2,14},{3,15},{4,8},{5,9},{6,10},{7,11},{8,4},{9,5},... | collective-permute-start | bytes 307208 | tf_op jit(solution)/shard_map/ppermute | solution.py:409
  25.3 0.1 apart_kernel.1.refs_2_.refs_1_
  25.5 3.8 %collective-permute-done.2.refs_1_ = f32[200,128]{1,0:T(8,128)S(1)} collective-permute-done((f32[200,128]{1,0:T(8,128)S(1)}, f32[200,128]{1,0:T(8,128)S(1)}, u32[]{:S(2)}, u32[]{:S(2)}) %collective-permute-start.2) | collective-permute-done | bytes 102432 | tf_op jit(solution)/shard_map/ppermute | solution.py:409
  29.3 0.1 join_kernel.1
  29.4 13.2 %all_to_all.11.refs_2_.refs_0_ = f32[8,200,128]{2,1,0:T(8,128)S(1)} all-to-all(f32[8,200,128]{2,1,0:T(8,128)S(1)} %join_kernel.1), channel_id=1, replica_groups={{0,1,2,3,4,5,6,7},{12,13,14,15,8,9,10,11},{16,17,18,19,20,21,22,23},{28..., dimensions={0} | all-to-all | bytes 1638400 | tf_op jit(solution)/shard_map/all_to_all | solution.py:397
  42.6 4.2 %first_kernel.1 = (f32[2,392,128]{2,1,0:T(8,128)S(1)}, f32[2,256,128]{2,1,0:T(8,128)S(1)}) custom-call(f32[2,8,256]{2,1,0:T(8,128)S(1)} %get-tuple-element.29.refs_0_.refs_2_, f32[2,256,256]{2,1,0:T(8,128)S(1)} %apart_kernel.1.refs_2_.refs_1_, f32[8,200,128]{2,1,0:T(8,128)S(1)} %all_to_all.11.refs_2_.refs_0_), custom_call_target="tpu_custom_call" | custom-call | tf_op jit(solution)/shard_map/first_kernel/pallas_call | solution.py:445
  46.8 0.1 collective-permute-start.3
  46.9 0.9 %stay_kernel.1 = (f32[2,392,128]{2,1,0:T(8,128)S(1)}, bf16[2,256,256]{2,1,0:T(8,128)(2,1)S(1)}, bf16[2,256,256]{2,1,0:T(8,128)(2,1)S(1)}) custom-call(f32[8,200,128]{2,1,0:T(8,128)S(1)} %all_to_all.11.refs_2_.refs_0_, f32[2,256,128]{2,1,0:T(8,128)S(1)} %get-tuple-element.30.refs_1_, f32[2,8,256]{2,1,0:T(8,128)S(1)} %get-tuple-element.29.refs_0_.refs_2_), custom_call_target="tpu_custom_call" | custom-call | tf_op jit(solution)/shard_map/stay_kernel/pallas_call | solution.py:453
  47.8 0.8 %collective-permute-done.3.refs_2_ = f32[2,392,128]{2,1,0:T(8,128)S(1)} collective-permute-done((f32[2,392,128]{2,1,0:T(8,128)S(1)}, f32[2,392,128]{2,1,0:T(8,128)S(1)}, u32[]{:S(2)}, u32[]{:S(2)}) %collective-permute-start.3) | collective-permute-done | bytes 401440 | tf_op jit(solution)/shard_map/ppermute | solution.py:389
  48.6 4.5 %second_kernel.1 = (f32[2,264,128]{2,1,0:T(8,128)S(1)}, f32[2,256,128]{2,1,0:T(8,128)S(1)}, f32[2,256,256]{2,1,0:T(8,128)S(1)}, bf16[2,256,256]{2,1,0:T(8,128)(2,1)S(1)}, bf16[2,256,256]{2,1,0:T(8,128)(2,1)S(1)}) custom-call(s32[2,1,4]{2,1,0:T(1,128)S(1)} %get-tuple-element.24.refs_0_, f32[2,392,128]{2,1,0:T(8,128)S(1)} %get-tuple-element.31.refs_1_, ...), custom_call_target="tpu_custom_call" | custom-call | tf_op jit(solution)/shard_map/second_kernel/pallas_call | solution.py:457
  53.1 0.2 collective-permute-start.4
  53.3 0.6 %finish_kernel.1 = (f32[2,256,128]{2,1,0:T(8,128)S(1)}, f32[2,8,128]{2,1,0:T(8,128)S(1)}) custom-call(bf16[2,256,256]{2,1,0:T(8,128)(2,1)S(1)} %get-tuple-element.37.refs_0_, bf16[2,256,256]{2,1,0:T(8,128)(2,1)S(1)} %get-tuple-element.38.refs_1_, f32[2,256,128]{2,1,0:T(8,128)S(1)} %get-tuple-element.39.refs_2_, f32[2,256,256]{2,1,0:T(8,128)S(1)} %get-tuple-element.40.refs_3_), custom_call_target="tpu_custom_call" | custom-call | tf_op jit(solution)/shard_map/finish_kernel/pallas_call | solution.py:470
  53.9 0.8 %collective-permute-done.4.refs_2_ = f32[2,264,128]{2,1,0:T(8,128)S(1)} collective-permute-done((f32[2,264,128]{2,1,0:T(8,128)S(1)}, f32[2,264,128]{2,1,0:T(8,128)S(1)}, u32[]{:S(2)}, u32[]{:S(2)}) %collective-permute-start.4) | collective-permute-done | bytes 270368 | tf_op jit(solution)/shard_map/ppermute | solution.py:389
  54.7 0.9 %last_kernel.1 = (f32[256,512]{1,0:T(8,128)}, f32[4,128]{1,0:T(4,128)}) custom-call(f32[2,256,128]{2,1,0:T(8,128)S(1)} %get-tuple-element.41.refs_0_, f32[2,8,128]{2,1,0:T(8,128)S(1)} %get-tuple-element.42.refs_1_, f32[2,264,128]{2,1,0:T(8,128)S(1)} %collective-permute-done.4.refs_2_), custom_call_target="tpu_custom_call" | custom-call | tf_op jit(solution)/shard_map/last_kernel/pallas_call | solution.py:473
  (1 shorter events, 0.0 us)
Async XLA Ops:
  0.6 2.3 %collective-permute-start.1 = (f32[256,512]{1,0:T(8,128)}, f32[256,512]{1,0:T(8,128)S(1)}, u32[]{:S(2)}, u32[]{:S(2)}) collective-permute-start(f32[256,512]{1,0:T(8,128)} %refs_3_.1), channel_id=1, source_target_pairs={{16,0},{0,16},{17,1},{1,17},{18,2},{2,18},{19,3},{3,19},{20,4},{4,... | collective-permute-start | bytes 1572872 | tf_op jit(solution)/shard_map/ppermute | solution.py:382
  1.2 1.7 %collective-permute-start = (s32[2,1,4]{2,1,0:T(1,128)}, s32[2,1,4]{2,1,0:T(1,128)S(1)}, u32[]{:S(2)}, u32[]{:S(2)}) collective-permute-start(s32[2,1,4]{2,1,0:T(1,128)} %refs_0_.1), channel_id=1, source_target_pairs={{16,0},{0,16},{17,1},{1,17},{18,2},{2,18},{19,3},{3,19},{20,4},{4,... | collective-permute-start | bytes 104 | tf_op jit(solution)/shard_map/ppermute | solution.py:382
  22.7 6.6 %collective-permute-start.2 = (f32[200,128]{1,0:T(8,128)S(1)}, f32[200,128]{1,0:T(8,128)S(1)}, u32[]{:S(2)}, u32[]{:S(2)}) collective-permute-start(f32[200,128]{1,0:T(8,128)S(1)} %half_sum_kernel.1.refs_1_.refs_0_), channel_id=1, source_target_pairs={{0,12},{1,13},{2,14},{3,15},{4,8},{5,9},{6,10},{7,11},{8,4},{9,5},... | collective-permute-start | bytes 307208 | tf_op jit(solution)/shard_map/ppermute | solution.py:409
  46.8 1.8 %collective-permute-start.3 = (f32[2,392,128]{2,1,0:T(8,128)S(1)}, f32[2,392,128]{2,1,0:T(8,128)S(1)}, u32[]{:S(2)}, u32[]{:S(2)}) collective-permute-start(f32[2,392,128]{2,1,0:T(8,128)S(1)} %get-tuple-element.32), channel_id=1, source_target_pairs={{16,0},{0,16},{17,1},{1,17},{18,2},{2,18},{19,3},{3,19},{20,4},{4,... | collective-permute-start | bytes 1204232 | tf_op jit(solution)/shard_map/ppermute | solution.py:389
  53.1 1.6 %collective-permute-start.4 = (f32[2,264,128]{2,1,0:T(8,128)S(1)}, f32[2,264,128]{2,1,0:T(8,128)S(1)}, u32[]{:S(2)}, u32[]{:S(2)}) collective-permute-start(f32[2,264,128]{2,1,0:T(8,128)S(1)} %get-tuple-element.43), channel_id=1, source_target_pairs={{16,0},{0,16},{17,1},{1,17},{18,2},{2,18},{19,3},{3,19},{20,4},{4,... | collective-permute-start | bytes 811016 | tf_op jit(solution)/shard_map/ppermute | solution.py:389
